TPU v7x, 512 devices: a whole 4x8x8 slice. The times are simulated.
512 devices in a mesh: blk: 64 (over y, z), tok: 8 (over x, core).
Axes of the slice: x: 4, y: 8, z: 8, core: 2. Of those that a mesh axis runs over, the one named last changes fastest.
Arguments:
- tokens: bfloat16 [8192, 9216], P(('tok', 'blk')), parts along dimension 0, may hold values from -6 to 6
- block_ids: int32 [8192, 8], P(('tok', 'blk')), parts along dimension 0, may hold values from 0 to 63, all different within a row; in each aligned block of 16 rows (0 to 15, 16 to 31, ...) at most 5 rows name the same one
- w_in: bfloat16 [9216, 8192], P(None, 'blk'), may hold values from -0.0625 to 0.0625
- bias_in: float32 [8192], P('blk'), may hold values from -3 to 3
- w_out: bfloat16 [8192, 9216], P('blk'), may hold values from -0.1875 to 0.1875
Outputs:
- ffn_out: bfloat16 [8192, 9216], P(('tok', 'blk')), parts along dimension 0
There are 8 independent parts, one for each index of `tok`. A program takes and returns all parts, laid end to end along the dimension named above; an argument that names none is the same for every part. Nothing has to cross between parts.
Inputs may be any that keep to these rules, and one draw needn't show every extreme that they name: `block_ids`: each row names 8 different blocks. Among the 16 rows of one device no block is named by more than 5 rows, and some block is named by exactly 5 of them.
All inputs are finite; a program needn't handle non-finite values.
Results may differ from a plain program's by a relative error of at most 0.0057.
Values may be sent and summed in bfloat16 or wider, within the bound.
No kernel may reach another device: no remote copies, remote signals or barrier semaphores. Data moves between devices by JAX's collectives and lax.ppermute only.
A program may use at most 128 MiB of HBM per device.

v0:
```python
import jax
import jax.numpy as jnp
from jax import lax
from jax.sharding import PartitionSpec as P

CAP = 5


def cut_along(array, dim, devices):
    lengths = array.shape
    pieces = array.reshape(*lengths[:dim], devices, lengths[dim] // devices, *lengths[dim + 1 :])
    return jnp.moveaxis(pieces, dim, 0)


def edges_of(length, count):
    hop = length // count
    if hop >= 8:
        hop -= hop % 8
    return [hop * k for k in range(1, count)]


def in_order(pieces, dim):
    lengths = list(pieces.shape[1:])
    lengths[dim] *= pieces.shape[0]
    return jnp.moveaxis(pieces, 0, dim).reshape(lengths)


def exchange_in_pieces(array, axis, pieces, split_dim, concat_dim):
    blocks = cut_along(array, split_dim, lax.axis_size(axis))
    split_at = max(range(1, max(2, blocks.ndim - 1)), key=lambda d: blocks.shape[d])
    finished = []
    for share in jnp.split(blocks, edges_of(blocks.shape[split_at], pieces), axis=split_at):
        if share.size:
            finished.append(lax.all_to_all(share, axis, split_axis=0, concat_axis=0, tiled=True))
    return in_order(jnp.concatenate(finished, axis=split_at), concat_dim)


def body(tokens, block_ids, w_in, bias_in, w_out):
    tok_dev = tokens.shape[0]
    model_width = tokens.shape[1]
    peer_count = lax.axis_size("blk")
    top_count = block_ids.shape[1]
    slot_total = peer_count * CAP
    flat_ids = block_ids.reshape(-1)
    onehot = (flat_ids[:, None] == jnp.arange(peer_count, dtype=jnp.int32)[None, :]).astype(
        jnp.int32
    )
    before = jnp.cumsum(onehot, axis=0) - onehot
    position = jnp.sum(before * onehot, axis=1)
    slot_index = (flat_ids * CAP + position).reshape(tok_dev, top_count)
    slot_range = jnp.arange(slot_total, dtype=jnp.int32)
    routing = jnp.any(slot_index[:, :, None] == slot_range[None, None, :], axis=1).astype(
        jnp.bfloat16
    )
    outgoing = jnp.dot(routing.T, tokens, preferred_element_type=jnp.float32).astype(jnp.bfloat16)
    outgoing = outgoing.reshape(peer_count, CAP, model_width)
    incoming = exchange_in_pieces(outgoing, "blk", 2, 0, 0)
    shape_in = incoming.shape
    flat_rows = incoming.reshape(-1, model_width)
    pre_act = jnp.dot(flat_rows, w_in, preferred_element_type=jnp.float32) + bias_in[None, :]
    hidden = jnp.maximum(pre_act, 0.0).astype(jnp.bfloat16)
    result = jnp.dot(hidden, w_out, preferred_element_type=jnp.float32).astype(jnp.bfloat16)
    partial_value = result.reshape(shape_in)
    returned = exchange_in_pieces(partial_value, "blk", 2, 0, 0)
    returned = returned.reshape(slot_total, model_width)
    combined = jnp.dot(routing, returned, preferred_element_type=jnp.float32)
    return combined.astype(jnp.bfloat16)


def solution(mesh):
    return jax.shard_map(
        body,
        mesh=mesh,
        in_specs=(
            P(("tok", "blk"), None),
            P(("tok", "blk"), None),
            P(None, "blk"),
            P("blk"),
            P("blk", None),
        ),
        out_specs=P(("tok", "blk"), None),
        check_vma=False,
    )
```

profile of v0, /device:TPU:26, one launch (start us, length us, event | category | flops | bytes accessed | tf_op | source)
XLA Modules:
  0.0 494.8 jit_solution(1518378613642959315)
XLA Ops:
  0.0 0.0 copy-start
  0.0 0.9 copy.16
  0.9 0.1 eq.28
  1.0 0.1 fusion.5
  1.1 0.2 reduce_window_sum.11
  1.3 0.2 select_reduce_fusion
  1.4 0.1 reduce_sum.12
  1.5 0.1 fusion.2
  1.7 5.3 %convolution_convert_fusion = bf16[320,9216]{1,0:T(8,128)(2,1)} fusion(pred[16,320]{1,0:T(8,128)(4,1)S(1)} %fusion.2, bf16[16,9216]{1,0:T(8,128)(2,1)} %param.5), kind=kOutput, calls=%fused_computation | convolution fusion | flops 97320960 | bytes 6198272 | tf_op jit(solution)/shard_map/dot_general | solution.py:55
  7.0 9.1 %reshape_reshape.12 = bf16[64,1,5,9216]{3,2,0,1:T(8,128)(2,1)} reshape(bf16[320,9216]{1,0:T(8,128)(2,1)} %convolution_convert_fusion) | data formatting | bytes 11796480 | tf_op jit(solution)/shard_map/reshape;reshape | solution.py:11
  16.1 6.9 %slice_bitcast_fusion.3 = bf16[64,1,2,9216]{3,2,1,0:T(2,128)(2,1)} fusion(bf16[64,1,5,9216]{3,2,0,1:T(8,128)(2,1)} %reshape_reshape.12), kind=kLoop, calls=%fused_computation.8 | loop fusion | bytes 4718592 | tf_op jit(solution)/shard_map/split | solution.py:32
  23.0 16.6 %all-to-all-start = ((bf16[64,1,2,9216]{3,2,1,0:T(2,128)(2,1)}), bf16[64,1,2,9216]{3,2,1,0:T(2,128)(2,1)}, u32[]{:S(2)}, u32[]{:S(2)}) async-start(bf16[64,1,2,9216]{3,2,1,0:T(2,128)(2,1)} %slice_bitcast_fusion.3), calls=%async_computation | async-start | bytes 4718592 | tf_op jit(solution)/shard_map/all_to_all | solution.py:34
  39.6 8.5 %slice_bitcast_fusion.1 = bf16[64,1,3,9216]{3,2,1,0:T(4,128)(2,1)} fusion(bf16[64,1,5,9216]{3,2,0,1:T(8,128)(2,1)} %reshape_reshape.12), kind=kLoop, calls=%fused_computation.6 | loop fusion | bytes 7077888 | tf_op jit(solution)/shard_map/split | solution.py:32
  48.1 52.8 %all-to-all-done = bf16[64,1,2,9216]{3,2,1,0:T(2,128)(2,1)} async-done(((bf16[64,1,2,9216]{3,2,1,0:T(2,128)(2,1)}), bf16[64,1,2,9216]{3,2,1,0:T(2,128)(2,1)}, u32[]{:S(2)}, u32[]{:S(2)}) %all-to-all-start) | async-done | bytes 2359328 | tf_op jit(solution)/shard_map/all_to_all | solution.py:34
  100.9 124.5 %all_to_all.20 = bf16[64,1,3,9216]{3,2,1,0:T(4,128)(2,1)} all-to-all(bf16[64,1,3,9216]{3,2,1,0:T(4,128)(2,1)} %slice_bitcast_fusion.1), channel_id=1, replica_groups=mesh['blk'=64,'tok'=8] {'blk'}, dimensions={0} | all-to-all | bytes 7077888 | tf_op jit(solution)/shard_map/all_to_all | solution.py:34
  225.4 11.3 %pad_maximum_fusion = bf16[64,1,5,9216]{3,2,1,0:T(8,128)(2,1)} fusion(bf16[64,1,3,9216]{3,2,1,0:T(4,128)(2,1)} %all_to_all.20, bf16[64,1,2,9216]{3,2,1,0:T(2,128)(2,1)} %all-to-all-done), kind=kLoop, calls=%fused_computation.3 | loop fusion | flops 11796480 | bytes 11796480 | tf_op jit(solution)/shard_map/concatenate | solution.py:35
  236.7 0.0 copy-start.2
  236.7 9.4 %reshape_reshape.13 = bf16[320,9216]{1,0:T(8,128)(2,1)} reshape(bf16[64,1,5,9216]{3,2,1,0:T(8,128)(2,1)} %pad_maximum_fusion) | data formatting | bytes 11796480 | tf_op jit(solution)/shard_map/reshape;reshape | solution.py:59
  246.1 0.0 copy-done
  246.1 0.0 copy-done.2
  246.1 9.2 %convolution_convert_fusion.1 = bf16[320,9216]{1,0:T(8,128)(2,1)} fusion(bf16[128,9216]{1,0:T(8,128)(2,1)S(1)} %copy-done, bf16[320,9216]{1,0:T(8,128)(2,1)} %reshape_reshape.13, bf16[9216,128]{1,0:T(8,128)(2,1)} %param.7, f32[128]{0:T(128)S(1)} %copy-done.2), kind=kOutput, calls=%fused_computation.1 | convolution fusion | flops 1513021440 | bytes 16515584 | tf_op jit(solution)/shard_map/dot_general | solution.py:62
  255.2 9.1 %reshape_reshape.14 = bf16[64,1,5,9216]{3,2,0,1:T(8,128)(2,1)} reshape(bf16[320,9216]{1,0:T(8,128)(2,1)} %convolution_convert_fusion.1) | data formatting | bytes 11796480 | tf_op jit(solution)/shard_map/reshape;reshape | solution.py:11
  264.4 6.9 %slice_bitcast_fusion.2 = bf16[64,1,2,9216]{3,2,1,0:T(2,128)(2,1)} fusion(bf16[64,1,5,9216]{3,2,0,1:T(8,128)(2,1)} %reshape_reshape.14), kind=kLoop, calls=%fused_computation.7 | loop fusion | bytes 4718592 | tf_op jit(solution)/shard_map/split | solution.py:32
  271.2 10.1 %all-to-all-start.2 = ((bf16[64,1,2,9216]{3,2,1,0:T(2,128)(2,1)}), bf16[64,1,2,9216]{3,2,1,0:T(2,128)(2,1)S(1)}, u32[]{:S(2)}, u32[]{:S(2)}) async-start(bf16[64,1,2,9216]{3,2,1,0:T(2,128)(2,1)} %slice_bitcast_fusion.2), calls=%async_computation.2 | async-start | bytes 4718592 | tf_op jit(solution)/shard_map/all_to_all | solution.py:34
  281.4 8.5 %slice_bitcast_fusion = bf16[64,1,3,9216]{3,2,1,0:T(4,128)(2,1)} fusion(bf16[64,1,5,9216]{3,2,0,1:T(8,128)(2,1)} %reshape_reshape.14), kind=kLoop, calls=%fused_computation.5 | loop fusion | bytes 7077888 | tf_op jit(solution)/shard_map/split | solution.py:32
  289.9 52.5 %all-to-all-done.2 = bf16[64,1,2,9216]{3,2,1,0:T(2,128)(2,1)S(1)} async-done(((bf16[64,1,2,9216]{3,2,1,0:T(2,128)(2,1)}), bf16[64,1,2,9216]{3,2,1,0:T(2,128)(2,1)S(1)}, u32[]{:S(2)}, u32[]{:S(2)}) %all-to-all-start.2) | async-done | bytes 2359328 | tf_op jit(solution)/shard_map/all_to_all | solution.py:34
  342.5 127.9 %all_to_all.21 = bf16[64,1,3,9216]{3,2,1,0:T(4,128)(2,1)} all-to-all(bf16[64,1,3,9216]{3,2,1,0:T(4,128)(2,1)} %slice_bitcast_fusion), channel_id=1, replica_groups=mesh['blk'=64,'tok'=8] {'blk'}, dimensions={0} | all-to-all | bytes 7077888 | tf_op jit(solution)/shard_map/all_to_all | solution.py:34
  470.4 10.5 %pad_maximum_fusion.1 = bf16[64,1,5,9216]{3,2,1,0:T(8,128)(2,1)} fusion(bf16[64,1,3,9216]{3,2,1,0:T(4,128)(2,1)} %all_to_all.21, bf16[64,1,2,9216]{3,2,1,0:T(2,128)(2,1)S(1)} %all-to-all-done.2), kind=kLoop, calls=%fused_computation.4 | loop fusion | flops 11796480 | bytes 11796480 | tf_op jit(solution)/shard_map/concatenate | solution.py:35
  480.9 0.0 copy-start.1
  480.9 9.6 %reshape_reshape.15 = bf16[320,9216]{1,0:T(8,128)(2,1)} reshape(bf16[64,1,5,9216]{3,2,1,0:T(8,128)(2,1)} %pad_maximum_fusion.1) | data formatting | bytes 11796480 | tf_op jit(solution)/shard_map/reshape;reshape | solution.py:65
  490.5 4.4 convolution_convert_fusion.2
  494.8 0.0 copy-done.1
  (1 shorter events, 0.0 us)
Async XLA Ops:
  0.0 246.1 %copy-start = (bf16[128,9216]{1,0:T(8,128)(2,1)S(1)}, bf16[128,9216]{1,0:T(8,128)(2,1)}, u32[]{:S(2)}) copy-start(bf16[128,9216]{1,0:T(8,128)(2,1)} %param.9) | copy-start | bytes 7077892
  23.0 77.9 %all-to-all-start = ((bf16[64,1,2,9216]{3,2,1,0:T(2,128)(2,1)}), bf16[64,1,2,9216]{3,2,1,0:T(2,128)(2,1)}, u32[]{:S(2)}, u32[]{:S(2)}) async-start(bf16[64,1,2,9216]{3,2,1,0:T(2,128)(2,1)} %slice_bitcast_fusion.3), calls=%async_computation | async-start | bytes 4718592 | tf_op jit(solution)/shard_map/all_to_all | solution.py:34
  236.7 9.4 %copy-start.2 = (f32[128]{0:T(128)S(1)}, f32[128]{0:T(128)}, u32[]{:S(2)}) copy-start(f32[128]{0:T(128)} %param.8) | copy-start | bytes 1540
  271.2 71.2 %all-to-all-start.2 = ((bf16[64,1,2,9216]{3,2,1,0:T(2,128)(2,1)}), bf16[64,1,2,9216]{3,2,1,0:T(2,128)(2,1)S(1)}, u32[]{:S(2)}, u32[]{:S(2)}) async-start(bf16[64,1,2,9216]{3,2,1,0:T(2,128)(2,1)} %slice_bitcast_fusion.2), calls=%async_computation.2 | async-start | bytes 4718592 | tf_op jit(solution)/shard_map/all_to_all | solution.py:34
  480.9 13.9 %copy-start.1 = (bf16[128,9216]{1,0:T(8,128)(2,1)S(1)}, bf16[128,9216]{1,0:T(8,128)(2,1)}, u32[]{:S(2)}) copy-start(bf16[128,9216]{1,0:T(8,128)(2,1)} %param.9) | copy-start | bytes 7077892
where the time goes:
time: 496 us; the launch traced here: 495 us
  blocking collectives  252 us (51%)
  waiting for transfers between devices  105 us (21%)
  local copies, waits for them, and re-layouts  69.1 us (14%)
  starting transfers between devices  26.7 us (5%)
  other arithmetic  22.4 us (5%)
  matrix products  18.8 us (4%)
    all_to_all x2, blocking collectives, exchange_in_pieces(): lax.all_to_all(share, axis, split_axis=0, concat_axis=0, tiled=True)  252 us
    all_to_all x2, waiting for transfers between devices, exchange_in_pieces(): lax.all_to_all(share, axis, split_axis=0, concat_axis=0, tiled=True)  105 us
    split x4, local copies, waits for them, and re-layouts, exchange_in_pieces(): jnp.split(blocks, edges_of(blocks.shape[split_at], pieces), axis=split_at)  30.8 us
    all_to_all x2, starting transfers between devices, exchange_in_pieces(): lax.all_to_all(share, axis, split_axis=0, concat_axis=0, tiled=True)  26.7 us
    concatenate x2, other arithmetic, exchange_in_pieces(): return in_order(jnp.concatenate(finished, axis=split_at), concat_dim)  21.8 us
    another operation x2, local copies, waits for them, and re-layouts, cut_along(): array.reshape(*lengths[:dim], devices, lengths[dim] // devices, *lengths[...  18.3 us
  transfers between devices with their start and end apart: 2, of which 2 were waited for; matrix products, arithmetic and copies ran while one was open for 3% of the time, Pallas kernels for 0%

commit v1 on v0

v1 whole, which is shorter than its diff:
```python
import functools
import math

import jax
import jax.numpy as jnp
from jax import lax
from jax.experimental import pallas as pl
from jax.experimental.pallas import tpu as pltpu
from jax.sharding import Mesh
from jax.sharding import PartitionSpec as P

CAP = 5
LANES = 128
BF16 = jnp.bfloat16
F32 = jnp.float32


def pack_kernel(where_ref, tokens_ref, ids_ref, w_in_ref, w_out_ref, out_ref, in_rows, sems, *, ny, nt):
    share = where_ref[0]
    width = tokens_ref.shape[1] // ny
    part = width // nt
    toks = tokens_ref.shape[0]
    copies = []
    for k in range(ny):
        copies.append(
            pltpu.make_async_copy(
                w_in_ref.at[pl.ds(k * width + share * part, part), :], in_rows.at[k], sems.at[k]
            )
        )
    for c in copies:
        c.start()
    ids = ids_ref[...]
    lane = lax.broadcasted_iota(jnp.int32, (toks, LANES), 1)
    nz = LANES // 2 // ny
    block = jnp.where(lane < ny * nz, (lane % ny) * nz + lane // ny, -1)
    named = jnp.zeros((toks, LANES), F32)
    for k in range(ids.shape[1]):
        named = jnp.where(ids[:, k : k + 1] == block, 1.0, named)
    row = lax.broadcasted_iota(jnp.int32, (toks, toks), 0)
    col = lax.broadcasted_iota(jnp.int32, (toks, toks), 1)
    before = jnp.where(col < row, 1.0, 0.0).astype(BF16)
    position = jnp.dot(before, named.astype(BF16), preferred_element_type=F32)
    slots = jnp.where(named > 0.0, position, -1.0).astype(BF16)
    for k in range(ny):
        out_ref[k, :, 0:width] = tokens_ref[:, k * width : (k + 1) * width]
        out_ref[k, :, width : width + LANES] = slots
        out_ref[k, :, width + LANES : 2 * width + LANES] = w_out_ref[:, k * width : (k + 1) * width]
    base = 2 * width + LANES
    for k in range(ny):
        copies[k].wait()
        for g in range(part // toks):
            out_ref[k, :, base + g * LANES : base + (g + 1) * LANES] = in_rows[
                k, g * toks : (g + 1) * toks, :
            ]


def pack(where, tokens, ids, w_in, w_out, ny, nt):
    toks, model = tokens.shape
    width = model // ny
    part = width // nt
    return pl.pallas_call(
        functools.partial(pack_kernel, ny=ny, nt=nt),
        out_shape=jax.ShapeDtypeStruct((ny, toks, 3 * width + LANES), BF16),
        grid_spec=pltpu.PrefetchScalarGridSpec(
            num_scalar_prefetch=1,
            grid=(1,),
            in_specs=[
                pl.BlockSpec((toks, model), lambda i, s: (0, 0)),
                pl.BlockSpec(ids.shape, lambda i, s: (0, 0)),
                pl.BlockSpec(memory_space=pl.ANY),
                pl.BlockSpec((w_out.shape[0] // nt, model), lambda i, s: (s[0], 0)),
            ],
            out_specs=pl.BlockSpec((ny, toks, 3 * width + LANES), lambda i, s: (0, 0, 0)),
            scratch_shapes=[
                pltpu.VMEM((ny, part, LANES), BF16),
                pltpu.SemaphoreType.DMA((ny,)),
            ],
        ),
        name="pack",
    )(where, tokens, ids, w_in, w_out)


def first_kernel(x_ref, pick_ref, w_ref, out_ref, wide, *, ny, chunk, toks):
    nt, _, rows, lanes = w_ref.shape
    groups = lanes // LANES
    width = nt * rows * groups
    for t in range(nt):
        for g in range(groups):
            top = (t * groups + g) * rows
            for j in range(ny):
                wide[top : top + rows, j * LANES : (j + 1) * LANES] = w_ref[
                    t, j, :, g * LANES : (g + 1) * LANES
                ]
    per = chunk // toks * CAP
    col = lax.broadcasted_iota(jnp.int32, (pick_ref.shape[0], chunk), 1)
    slot = lax.broadcasted_iota(jnp.int32, (per, chunk), 0).astype(F32)
    first = (col // toks * CAP).astype(F32)
    for m in range(x_ref.shape[0] // chunk):
        x = x_ref[m * chunk : (m + 1) * chunk, 0:width]
        pos = x_ref[m * chunk : (m + 1) * chunk, width : width + LANES]
        h = jnp.dot(x, wide[...], preferred_element_type=F32).astype(BF16)
        at = lax.dot_general(
            pick_ref[...], pos, (((1,), (1,)), ((), ())), preferred_element_type=F32
        )
        at = jnp.where(at >= 0.0, at + first, -1.0)
        for j in range(ny):
            s = jnp.where(slot == at[j : j + 1, :], 1.0, 0.0).astype(BF16)
            rows_j = jnp.dot(s, h[:, j * LANES : (j + 1) * LANES], preferred_element_type=F32)
            out_ref[j, m * per : (m + 1) * per, :] = rows_j.astype(BF16)


def first_product(x, pick, w, ny, toks):
    chunk = 256
    slots = x.shape[0] // toks * CAP
    return pl.pallas_call(
        functools.partial(first_kernel, ny=ny, chunk=chunk, toks=toks),
        out_shape=jax.ShapeDtypeStruct((ny, slots, LANES), BF16),
        scratch_shapes=[pltpu.VMEM((x.shape[1] - LANES, ny * LANES), BF16)],
        name="first_product",
    )(x, pick, w)


def second_kernel(h_ref, pos_ref, pick_ref, w_ref, out_ref, tall, spread, *, ny, chunk, toks):
    nt, _, rows, _ = w_ref.shape
    for j in range(ny):
        for t in range(nt):
            top = (j * nt + t) * rows
            tall[top : top + rows, :] = w_ref[t, j]
    per = chunk // toks * CAP
    row = lax.broadcasted_iota(jnp.int32, (chunk, pick_ref.shape[0]), 0)
    slot = lax.broadcasted_iota(jnp.int32, (chunk, per), 1).astype(F32)
    first = (row // toks * CAP).astype(F32)
    for m in range(pos_ref.shape[0] // chunk):
        pos = pos_ref[m * chunk : (m + 1) * chunk, :]
        at = lax.dot_general(
            pos, pick_ref[...], (((1,), (1,)), ((), ())), preferred_element_type=F32
        )
        at = jnp.where(at >= 0.0, at + first, -1.0)
        for j in range(ny):
            s = jnp.where(slot == at[:, j : j + 1], 1.0, 0.0).astype(BF16)
            full = jnp.dot(s, h_ref[j, m * per : (m + 1) * per, :], preferred_element_type=F32)
            spread[:, j * LANES : (j + 1) * LANES] = full.astype(BF16)
        y = jnp.dot(spread[...], tall[...], preferred_element_type=F32).astype(BF16)
        per_dev = chunk // toks
        out_ref[m * per_dev : (m + 1) * per_dev] = y.reshape(per_dev, toks, y.shape[1])


def second_product(h, x, pick, w, ny, toks):
    chunk = 256
    width = x.shape[1] - LANES
    total = x.shape[0]
    return pl.pallas_call(
        functools.partial(second_kernel, ny=ny, chunk=chunk, toks=toks),
        out_shape=jax.ShapeDtypeStruct((total // toks, toks, width), BF16),
        grid=(1,),
        in_specs=[
            pl.BlockSpec(h.shape, lambda i: (0, 0, 0)),
            pl.BlockSpec((total, LANES), lambda i: (0, width // LANES)),
            pl.BlockSpec(pick.shape, lambda i: (0, 0)),
            pl.BlockSpec(w.shape, lambda i: (0, 0, 0, 0)),
        ],
        out_specs=pl.BlockSpec((total // toks, toks, width), lambda i: (0, 0, 0)),
        scratch_shapes=[
            pltpu.VMEM((ny * LANES, width), BF16),
            pltpu.VMEM((chunk, ny * LANES), BF16),
        ],
        name="second_product",
    )(h, x, pick, w)


def combine_kernel(y_ref, out_ref, *, ny):
    width = y_ref.shape[2]
    for k in range(ny):
        total = y_ref[k].astype(F32)
        for other in range(ny + k, y_ref.shape[0], ny):
            total = total + y_ref[other].astype(F32)
        out_ref[:, k * width : (k + 1) * width] = total.astype(BF16)


def combine(y, ny):
    return pl.pallas_call(
        functools.partial(combine_kernel, ny=ny),
        out_shape=jax.ShapeDtypeStruct((y.shape[1], y.shape[2] * ny), BF16),
        name="combine",
    )(y)


def body(tokens, block_ids, w_in, bias_in, w_out):
    toks = tokens.shape[0]
    ny, nz = lax.axis_size("y"), lax.axis_size("z")
    nt = lax.axis_size("x") * lax.axis_size("c")
    width = tokens.shape[1] // ny
    share = lax.axis_index("x") * lax.axis_size("c") + lax.axis_index("c")
    z = lax.axis_index("z")
    payload = pack(share.reshape(1).astype(jnp.int32), tokens, block_ids, w_in, w_out, ny, nt)
    got = lax.all_to_all(payload, "y", split_axis=0, concat_axis=0, tiled=True)
    x_part = got[:, :, : width + LANES].reshape(ny * toks, width + LANES)
    x = lax.all_gather(x_part, "z", axis=0, tiled=True)
    w1 = got[:, :, 2 * width + LANES :]
    w1 = lax.all_to_all(
        jnp.broadcast_to(w1[None], (nt,) + w1.shape), ("x", "c"), split_axis=0, concat_axis=0, tiled=True
    )
    w2_part = got[:, :, width + LANES : 2 * width + LANES]
    pick = (
        jnp.arange(LANES, dtype=jnp.int32)[None, :] == z * ny + jnp.arange(16, dtype=jnp.int32)[:, None]
    ) & (jnp.arange(16)[:, None] < ny)
    pick = pick.astype(BF16)
    x, w2_part = lax.optimization_barrier((x, w2_part))
    w2 = lax.all_gather(w2_part[None], ("x", "c"), axis=0, tiled=True)
    h = first_product(x, pick, w1, ny, toks)
    h = lax.all_to_all(h, "y", split_axis=0, concat_axis=0, tiled=True)
    h = jnp.sum(h.astype(F32), axis=0) + bias_in[None, :]
    h = jnp.maximum(h, 0.0).astype(BF16)
    h = lax.all_to_all(
        jnp.broadcast_to(h[None], (ny,) + h.shape), "y", split_axis=0, concat_axis=0, tiled=True
    )
    y = second_product(h, x, pick, w2, ny, toks)
    y = lax.all_to_all(y, ("z", "y"), split_axis=0, concat_axis=0, tiled=True)
    return combine(y, ny)


def solution(mesh):
    side = math.isqrt(mesh.shape["blk"])
    cores = 2
    fine = Mesh(
        mesh.devices.reshape(side, side, mesh.shape["tok"] // cores, cores), ("y", "z", "x", "c")
    )
    rows = ("x", "c", "y", "z")
    return jax.shard_map(
        body,
        mesh=fine,
        in_specs=(
            P(rows, None),
            P(rows, None),
            P(None, ("y", "z")),
            P(("y", "z")),
            P(("y", "z"), None),
        ),
        out_specs=P(rows, None),
        check_vma=False,
    )
```

time: 496 us -> 222 us (0.45)
  the two profiles are of different devices: /device:TPU:26 before, /device:TPU:14 now
where the time goes in v1:
time: 222 us
  blocking collectives  137 us (62%)
  waiting for transfers between devices  38.7 us (17%)
  Pallas kernels  21.3 us (10%)
  between operations  13.5 us (6%)
  local copies, waits for them, and re-layouts  6 us (3%)
  starting transfers between devices  4.78 us (2%)
    all_to_all x1, blocking collectives, body(): y = lax.all_to_all(y, ('z', 'y'), split_axis=0, concat_axis=0, tiled=True)  62.4 us
    all_gather x1, waiting for transfers between devices, body(): x = lax.all_gather(x_part, 'z', axis=0, tiled=True)  38.7 us
    all_to_all x1, blocking collectives, body(): got = lax.all_to_all(payload, 'y', split_axis=0, concat_axis=0, tiled=True)  32 us
    all_to_all x1, blocking collectives, body(): h = lax.all_to_all(h, 'y', split_axis=0, concat_axis=0, tiled=True)  23 us
    all_to_all x1, blocking collectives, body(): lax.all_to_all(jnp.broadcast_to(h[None], (ny,) + h.shape), 'y', split_axi...  19.3 us
    pallas_call x1, Pallas kernels, second_product(): pl.pallas_call(functools.partial(second_kernel, ny=ny, chunk=chunk, toks=...  8.29 us
    pallas_call x1, Pallas kernels, first_product(): pl.pallas_call(functools.partial(first_kernel, ny=ny, chunk=chunk, toks=t...  7.32 us
    all_to_all x1, starting transfers between devices, body(): lax.all_to_all(jnp.broadcast_to(w1[None], (nt,) + w1.shape), ('x', 'c'),...  4.78 us
  transfers between devices with their start and end apart: 3, of which 1 were waited for; matrix products, arithmetic and copies ran while one was open for 1% of the time, Pallas kernels for 3%

profile of v1, /device:TPU:14, one launch (start us, length us, event | category | flops | bytes accessed | tf_op | source)
XLA Modules:
  0.0 221.7 jit_solution(17830178540648899285)
XLA Ops:
  6.5 0.0 all-gather.4.cloned.1.call-start
  6.5 1.4 copy.7.ids_ref
  7.9 3.0 %pack.1 = bf16[8,16,3584]{2,1,0:T(8,128)(2,1)} custom-call(s32[1]{0:T(128)} %bitcast.where_ref, bf16[16,9216]{1,0:T(8,128)(2,1)} %tokens_ref.1, s32[16,8]{1,0:T(8,128)} %copy.7.ids_ref, bf16[9216,128]{1,0:T(8,128)(2,1)} %w_in_ref.1, bf16[128,9216]{1,0:T(8,128)(2,1)} %w_out_ref.1), custom_call_target="tpu_custom_call" | custom-call | tf_op jit(solution)/shard_map/pack/pallas_call | solution.py:61
  10.9 32.0 %all_to_all.25 = bf16[8,16,3584]{2,1,0:T(8,128)(2,1)S(1)} all-to-all(bf16[8,16,3584]{2,1,0:T(8,128)(2,1)} %pack.1), channel_id=1, replica_groups=mesh['y'=8,'z'=8,'x'=4,'c'=2] {'y'}, dimensions={0} | all-to-all | bytes 1835008 | tf_op jit(solution)/shard_map/all_to_all | solution.py:196
  42.9 0.8 slice.12
  43.7 0.0 all-gather.4.cloned.1.call-update
  43.7 0.8 fusion.2
  44.4 1.6 broadcast_in_dim.6
  46.0 4.8 %all-to-all-start.1 = ((bf16[8,8,16,1152]{3,2,1,0:T(8,128)(2,1)}), bf16[8,8,16,1152]{3,2,1,0:T(8,128)(2,1)S(1)}, u32[]{:S(2)}, u32[]{:S(2)}) async-start(bf16[8,8,16,1152]{3,2,1,0:T(8,128)(2,1)} %broadcast_in_dim.6), calls=%async_computation.1 | async-start | bytes 4718592 | tf_op jit(solution)/shard_map/all_to_all | solution.py:200
  50.8 0.0 all-gather.6.cloned.1.call-start
  50.8 38.7 %all-gather.4.cloned.1.call-done.x_ref.pos_ref = bf16[1024,1280]{1,0:T(8,128)(2,1)} async-done(((bf16[128,1280]{1,0:T(8,128)(2,1)}), bf16[1024,1280]{1,0:T(8,128)(2,1)}) %all-gather.4.cloned.1.call-update) | async-done | bytes 2621456 | tf_op jit(solution)/shard_map/all_gather | solution.py:198
  89.5 0.0 all-gather.6.cloned.1.call-update
  89.6 0.7 fusion.1.pick_ref
  90.2 0.0 copy-start.1
  90.2 0.0 all-to-all-done.1.w_ref
  90.3 0.0 copy-start
  90.3 1.4 copy-done
  91.7 7.3 %first_product.1 = bf16[8,320,128]{2,1,0:T(8,128)(2,1)} custom-call(bf16[1024,1280]{1,0:T(8,128)(2,1)} %all-gather.4.cloned.1.call-done.x_ref.pos_ref, bf16[16,128]{1,0:T(8,128)(2,1)} %fusion.1.pick_ref, bf16[8,8,16,1152]{3,2,1,0:T(8,128)(2,1)} %copy-done), custom_call_target="tpu_custom_call" | custom-call | tf_op jit(solution)/shard_map/first_product/pallas_call | solution.py:115
  99.0 23.0 %all_to_all.26 = bf16[8,320,128]{2,1,0:T(8,128)(2,1)S(1)} all-to-all(bf16[8,320,128]{2,1,0:T(8,128)(2,1)} %first_product.1), channel_id=1, replica_groups=mesh['y'=8,'z'=8,'x'=4,'c'=2] {'y'}, dimensions={0} | all-to-all | bytes 1310720 | tf_op jit(solution)/shard_map/all_to_all | solution.py:211
  122.0 0.1 convert_reduce_fusion
  122.1 0.0 copy-done.1
  122.1 0.1 broadcast_in_dim.7
  122.2 19.3 %all_to_all.27.h_ref = bf16[8,320,128]{2,1,0:T(8,128)(2,1)} all-to-all(bf16[8,320,128]{2,1,0:T(8,128)(2,1)S(1)} %broadcast_in_dim.7), channel_id=1, replica_groups=mesh['y'=8,'z'=8,'x'=4,'c'=2] {'y'}, dimensions={0} | all-to-all | bytes 1310720 | tf_op jit(solution)/shard_map/all_to_all | solution.py:214
  141.5 0.0 all-gather.6.cloned.1.call-done
  141.5 8.3 %second_product.1 = bf16[64,16,1152]{2,1,0:T(8,128)(2,1)} custom-call(bf16[8,320,128]{2,1,0:T(8,128)(2,1)} %all_to_all.27.h_ref, bf16[1024,1280]{1,0:T(8,128)(2,1)} %all-gather.4.cloned.1.call-done.x_ref.pos_ref, bf16[16,128]{1,0:T(8,128)(2,1)} %fusion.1.pick_ref, bf16[8,8,16,1152]{3,2,1,0:T(8,128)(2,1)} %bitcast.3), custom_call_target="tpu_custom_call" | custom-call | tf_op jit(solution)/shard_map/second_product/pallas_call | solution.py:152
  149.8 62.4 %all_to_all.28.y_ref = bf16[64,16,1152]{2,1,0:T(8,128)(2,1)} all-to-all(bf16[64,16,1152]{2,1,0:T(8,128)(2,1)} %second_product.1), channel_id=1, replica_groups=mesh['y'=8,'z'=8,'x'=4,'c'=2] {'z','y'}, dimensions={0} | all-to-all | bytes 4718592 | tf_op jit(solution)/shard_map/all_to_all | solution.py:218
  212.2 2.7 %combine.1 = bf16[16,9216]{1,0:T(8,128)(2,1)} custom-call(bf16[64,16,1152]{2,1,0:T(8,128)(2,1)} %all_to_all.28.y_ref), custom_call_target="tpu_custom_call" | custom-call | tf_op jit(solution)/shard_map/combine/pallas_call | solution.py:181
  (3 shorter events, 0.0 us)
Async XLA Ops:
  6.5 83.0 %all-gather.4.cloned.1.call-start = ((), (), s32[]{:S(2)}) async-start(), calls=%async_computation.5 | async-start | bytes 2949120 | tf_op jit(solution)/shard_map/all_gather | solution.py:198
  46.0 44.2 %all-to-all-start.1 = ((bf16[8,8,16,1152]{3,2,1,0:T(8,128)(2,1)}), bf16[8,8,16,1152]{3,2,1,0:T(8,128)(2,1)S(1)}, u32[]{:S(2)}, u32[]{:S(2)}) async-start(bf16[8,8,16,1152]{3,2,1,0:T(8,128)(2,1)} %broadcast_in_dim.6), calls=%async_computation.1 | async-start | bytes 4718592 | tf_op jit(solution)/shard_map/all_to_all | solution.py:200
  50.8 90.7 %all-gather.6.cloned.1.call-start = ((), (), s32[]{:S(2)}) async-start(), calls=%async_computation.6 | async-start | bytes 2654208 | tf_op jit(solution)/shard_map/all_gather | solution.py:209
  90.2 31.8 %copy-start.1 = (f32[128]{0:T(128)S(1)}, f32[128]{0:T(128)}, u32[]{:S(2)}) copy-start(f32[128]{0:T(128)} %param.8) | copy-start | bytes 1540
  90.3 1.4 copy-start
Sparse Core Ops, SparseCore 0:
  43.8 45.6 all-gather.3
  91.6 28.2 all-gather.5

commit v2 on v1

v2 whole, which is shorter than its diff:
```python
import functools
import math

import jax
import jax.numpy as jnp
from jax import lax
from jax.experimental import pallas as pl
from jax.experimental.pallas import tpu as pltpu
from jax.sharding import Mesh
from jax.sharding import PartitionSpec as P

CAP = 5
LANES = 128
BF16 = jnp.bfloat16
F32 = jnp.float32


def tokens_kernel(tokens_ref, ids_ref, out_ref, *, ny, nz):
    width = tokens_ref.shape[1] // ny
    toks = tokens_ref.shape[0]
    same = lax.broadcasted_iota(jnp.int32, (ids_ref.shape[0],) * 2, 0)
    same = same == lax.broadcasted_iota(jnp.int32, same.shape, 1)
    ids = lax.dot_general(
        ids_ref[...].astype(F32).astype(BF16),
        jnp.where(same, 1.0, 0.0).astype(BF16),
        (((0,), (0,)), ((), ())),
        preferred_element_type=F32,
    )
    lane = lax.broadcasted_iota(jnp.int32, (toks, LANES), 1)
    block = jnp.where(lane < ny * nz, (lane % ny) * nz + lane // ny, -1).astype(F32)
    named = jnp.zeros((toks, LANES), F32)
    for k in range(ids.shape[1]):
        named = jnp.where(ids[:, k : k + 1] == block, 1.0, named)
    row = lax.broadcasted_iota(jnp.int32, (toks, toks), 0)
    col = lax.broadcasted_iota(jnp.int32, (toks, toks), 1)
    before = jnp.where(col < row, 1.0, 0.0).astype(BF16)
    position = jnp.dot(before, named.astype(BF16), preferred_element_type=F32)
    slots = jnp.where(named > 0.0, position, -1.0).astype(BF16)
    for k in range(ny):
        piece = tokens_ref[:, k * width : (k + 1) * width]
        for z in range(nz):
            out_ref[k * nz + z, :, 0:width] = piece
            out_ref[k * nz + z, :, width : width + LANES] = slots


def spread_tokens(tokens, ids, ny, nz):
    toks, model = tokens.shape
    width = model // ny
    return pl.pallas_call(
        functools.partial(tokens_kernel, ny=ny, nz=nz),
        out_shape=jax.ShapeDtypeStruct((ny * nz, toks, width + LANES), BF16),
        name="spread_tokens",
    )(tokens, ids)


def weights_kernel(where_ref, w_in_ref, w_out_ref, out_ref, in_rows, out_rows, sems, *, ny, nt):
    share, y = where_ref[0], where_ref[1]
    width = w_out_ref.shape[1] // ny
    part = width // nt
    rows = out_rows.shape[1]
    copies = []
    for k in range(ny):
        dest = (y + k) % ny
        copies.append(
            pltpu.make_async_copy(
                w_in_ref.at[pl.ds(pl.multiple_of(dest * width + share * part, 16), part), :],
                in_rows.at[k],
                sems.at[k, 0],
            )
        )
        copies.append(
            pltpu.make_async_copy(
                w_out_ref.at[
                    pl.ds(pl.multiple_of(share * rows, 16), rows),
                    pl.ds(pl.multiple_of(dest * width, LANES), width),
                ],
                out_rows.at[k],
                sems.at[k, 1],
            )
        )
    for c in copies:
        c.start()
    for k in range(ny):
        copies[2 * k].wait()
        copies[2 * k + 1].wait()
        out_ref[k, :, 0:width] = out_rows[k]
        for g in range(part // rows):
            out_ref[k, :, width + g * LANES : width + (g + 1) * LANES] = in_rows[
                k, g * rows : (g + 1) * rows, :
            ]


def pack_weights(where, w_in, w_out, ny, nt):
    rows = w_out.shape[0] // nt
    width = w_out.shape[1] // ny
    return pl.pallas_call(
        functools.partial(weights_kernel, ny=ny, nt=nt),
        out_shape=jax.ShapeDtypeStruct((ny, rows, 2 * width), BF16),
        grid_spec=pltpu.PrefetchScalarGridSpec(
            num_scalar_prefetch=1,
            grid=(1,),
            in_specs=[
                pl.BlockSpec(memory_space=pl.ANY),
                pl.BlockSpec(memory_space=pl.ANY),
            ],
            out_specs=pl.BlockSpec((ny, rows, 2 * width), lambda i, s: (0, 0, 0)),
            scratch_shapes=[
                pltpu.VMEM((ny, width // nt, LANES), BF16),
                pltpu.VMEM((ny, rows, width), BF16),
                pltpu.SemaphoreType.DMA((ny, 2)),
            ],
        ),
        name="pack_weights",
    )(where, w_in, w_out)


def tile_kernel(where_ref, mine_ref, other_ref, wide_ref, tall_ref, *, nc):
    x, c = where_ref[2], where_ref[3]
    nx, ny, rows, lanes = mine_ref.shape
    width = lanes // 2
    groups = width // LANES
    for source, core in ((mine_ref, c), (other_ref, nc - 1 - c)):
        for s in range(nx):
            share = (x + nx - s) % nx * nc + core
            for k in range(ny):
                top = pl.multiple_of(k * LANES + share * rows, 16)
                tall_ref[pl.ds(top, rows), :] = source[s, k, :, 0:width]
                for g in range(groups):
                    top = pl.multiple_of((share * groups + g) * rows, 16)
                    wide_ref[pl.ds(top, rows), k * LANES : (k + 1) * LANES] = source[
                        s, k, :, width + g * LANES : width + (g + 1) * LANES
                    ]


def tile_weights(where, mine, other, nc):
    _, ny, _, lanes = mine.shape
    width = lanes // 2
    return pl.pallas_call(
        functools.partial(tile_kernel, nc=nc),
        out_shape=(
            jax.ShapeDtypeStruct((width, ny * LANES), BF16),
            jax.ShapeDtypeStruct((ny * LANES, width), BF16),
        ),
        in_specs=[
            pl.BlockSpec(memory_space=pltpu.SMEM),
            pl.BlockSpec(memory_space=pltpu.VMEM),
            pl.BlockSpec(memory_space=pltpu.VMEM),
        ],
        out_specs=(
            pl.BlockSpec(memory_space=pltpu.VMEM),
            pl.BlockSpec(memory_space=pltpu.VMEM),
        ),
        name="tile_weights",
    )(where, mine, other)


def first_kernel(where_ref, x_ref, pick_ref, wide_ref, out_ref, *, ny, chunk, toks):
    width = wide_ref.shape[0]
    y = where_ref[1]
    per = chunk // toks * CAP
    col = lax.broadcasted_iota(jnp.int32, (pick_ref.shape[0], chunk), 1)
    slot = lax.broadcasted_iota(jnp.int32, (per, chunk), 0).astype(F32)
    first = (col // toks * CAP).astype(F32)
    for m in range(x_ref.shape[0] // chunk):
        x = x_ref[m * chunk : (m + 1) * chunk, 0:width]
        pos = x_ref[m * chunk : (m + 1) * chunk, width : width + LANES]
        h = jnp.dot(x, wide_ref[...], preferred_element_type=F32).astype(BF16)
        at = lax.dot_general(
            pick_ref[...], pos, (((1,), (1,)), ((), ())), preferred_element_type=F32
        )
        at = jnp.where(at >= 0.0, at + first, -1.0)
        for k in range(ny):
            s = jnp.where(slot == at[k : k + 1, :], 1.0, 0.0).astype(BF16)
            rows_k = jnp.dot(s, h[:, k * LANES : (k + 1) * LANES], preferred_element_type=F32)
            out_ref[(y + ny - k) % ny, m * per : (m + 1) * per, :] = rows_k.astype(BF16)


def first_product(where, x, pick, wide, ny, toks):
    chunk = 256
    slots = x.shape[0] // toks * CAP
    return pl.pallas_call(
        functools.partial(first_kernel, ny=ny, chunk=chunk, toks=toks),
        out_shape=jax.ShapeDtypeStruct((ny, slots, LANES), BF16),
        in_specs=[pl.BlockSpec(memory_space=pltpu.SMEM)]
        + [pl.BlockSpec(memory_space=pltpu.VMEM)] * 3,
        out_specs=pl.BlockSpec(memory_space=pltpu.VMEM),
        name="first_product",
    )(where, x, pick, wide)


def second_kernel(where_ref, h_ref, x_ref, pick_ref, tall_ref, out_ref, spread, *, ny, chunk, toks):
    y = where_ref[1]
    width = tall_ref.shape[1]
    per = chunk // toks * CAP
    row = lax.broadcasted_iota(jnp.int32, (chunk, pick_ref.shape[0]), 0)
    slot = lax.broadcasted_iota(jnp.int32, (chunk, per), 1).astype(F32)
    first = (row // toks * CAP).astype(F32)
    for m in range(x_ref.shape[0] // chunk):
        pos = x_ref[m * chunk : (m + 1) * chunk, width : width + LANES]
        at = lax.dot_general(
            pos, pick_ref[...], (((1,), (1,)), ((), ())), preferred_element_type=F32
        )
        at = jnp.where(at >= 0.0, at + first, -1.0)
        for k in range(ny):
            s = jnp.where(slot == at[:, k : k + 1], 1.0, 0.0).astype(BF16)
            full = jnp.dot(
                s, h_ref[(y + ny - k) % ny, m * per : (m + 1) * per, :], preferred_element_type=F32
            )
            spread[:, k * LANES : (k + 1) * LANES] = full.astype(BF16)
        out = jnp.dot(spread[...], tall_ref[...], preferred_element_type=F32).astype(BF16)
        per_dev = chunk // toks
        out_ref[m * per_dev : (m + 1) * per_dev] = out.reshape(per_dev, toks, width)


def second_product(where, h, x, pick, tall, ny, toks):
    chunk = 256
    width = x.shape[1] - LANES
    total = x.shape[0]
    return pl.pallas_call(
        functools.partial(second_kernel, ny=ny, chunk=chunk, toks=toks),
        out_shape=jax.ShapeDtypeStruct((total // toks, toks, width), BF16),
        in_specs=[pl.BlockSpec(memory_space=pltpu.SMEM)]
        + [pl.BlockSpec(memory_space=pltpu.VMEM)] * 4,
        out_specs=pl.BlockSpec(memory_space=pltpu.VMEM),
        scratch_shapes=[pltpu.VMEM((chunk, ny * LANES), BF16)],
        name="second_product",
    )(where, h, x, pick, tall)


def combine_kernel(y_ref, out_ref, *, ny):
    width = y_ref.shape[2]
    for k in range(ny):
        nz = y_ref.shape[0] // ny
        total = y_ref[k * nz].astype(F32)
        for other in range(k * nz + 1, (k + 1) * nz):
            total = total + y_ref[other].astype(F32)
        out_ref[:, k * width : (k + 1) * width] = total.astype(BF16)


def combine(y, ny):
    return pl.pallas_call(
        functools.partial(combine_kernel, ny=ny),
        out_shape=jax.ShapeDtypeStruct((y.shape[1], y.shape[2] * ny), BF16),
        in_specs=[pl.BlockSpec(memory_space=pltpu.VMEM)],
        name="combine",
    )(y)


def steps(n, k):
    return [(i, (i + k) % n) for i in range(n)]


def body(tokens, block_ids, w_in, bias_in, w_out):
    toks = tokens.shape[0]
    ny, nz = lax.axis_size("y"), lax.axis_size("z")
    nx, nc = lax.axis_size("x"), lax.axis_size("c")
    nt = nx * nc
    width = tokens.shape[1] // ny
    y, z = lax.axis_index("y"), lax.axis_index("z")
    place = lax.axis_index("x"), lax.axis_index("c")
    where = jnp.stack([place[0] * nc + place[1], y, place[0], place[1]]).astype(jnp.int32)

    x = spread_tokens(tokens, block_ids.T, ny, nz)
    x, where = lax.optimization_barrier((x, where))
    x = lax.all_to_all(x, ("y", "z"), split_axis=0, concat_axis=0, tiled=True)
    x = x.reshape(-1, width + LANES)

    pieces = pack_weights(where, w_in, w_out, ny, nt)
    got = [pieces[0]]
    for k in range(1, ny):
        got.append(lax.ppermute(pieces[k], "y", steps(ny, k)))
    got = jnp.stack(got)
    mine = [got]
    for s in range(1, nx):
        mine.append(lax.ppermute(got, "x", steps(nx, s)))
    mine = jnp.stack(mine)
    other = lax.ppermute(mine, "c", steps(nc, 1))
    wide, tall = tile_weights(where, mine, other, nc)

    step = jnp.arange(16, dtype=jnp.int32)[:, None]
    lane = jnp.arange(LANES, dtype=jnp.int32)[None, :]
    pick = ((lane == z * ny + (y + ny - step) % ny) & (step < ny)).astype(BF16)
    h = first_product(where, x, pick, wide, ny, toks)
    h = lax.all_to_all(h, "y", split_axis=0, concat_axis=0, tiled=True)
    h = jnp.sum(h.astype(F32), axis=0) + bias_in[None, :]
    h = jnp.maximum(h, 0.0).astype(BF16)
    h = lax.all_to_all(
        jnp.broadcast_to(h[None], (ny,) + h.shape), "y", split_axis=0, concat_axis=0, tiled=True
    )
    out = second_product(where, h, x, pick, tall, ny, toks)
    out = lax.all_to_all(out, ("y", "z"), split_axis=0, concat_axis=0, tiled=True)
    return combine(out, ny)


def solution(mesh):
    side = math.isqrt(mesh.shape["blk"])
    cores = 2
    fine = Mesh(
        mesh.devices.reshape(side, side, mesh.shape["tok"] // cores, cores), ("y", "z", "x", "c")
    )
    rows = ("x", "c", "y", "z")
    return jax.shard_map(
        body,
        mesh=fine,
        in_specs=(
            P(rows, None),
            P(rows, None),
            P(None, ("y", "z")),
            P(("y", "z")),
            P(("y", "z"), None),
        ),
        out_specs=P(rows, None),
        check_vma=False,
    )
```

time: 222 us -> 296 us (1.33)
  the two profiles are of different devices: /device:TPU:14 before, /device:TPU:50 now
where the time goes in v2:
time: 296 us; the launch traced here: 295 us
  blocking collectives  123 us (42%)
  waiting for transfers between devices  76.1 us (26%)
  starting transfers between devices  55.4 us (19%)
  Pallas kernels  29.8 us (10%)
  local copies, waits for them, and re-layouts  7.9 us (3%)
  other arithmetic  3.19 us (1%)
    all_to_all x1, blocking collectives, body(): lax.all_to_all(out, ('y', 'z'), split_axis=0, concat_axis=0, tiled=True)  76.1 us
    ppermute x7, waiting for transfers between devices, body(): got.append(lax.ppermute(pieces[k], 'y', steps(ny, k)))  49.1 us
    ppermute x7, starting transfers between devices, body(): got.append(lax.ppermute(pieces[k], 'y', steps(ny, k)))  27.5 us
    all_to_all x1, blocking collectives, body(): h = lax.all_to_all(h, 'y', split_axis=0, concat_axis=0, tiled=True)  24 us
    ppermute x3, waiting for transfers between devices, body(): mine.append(lax.ppermute(got, 'x', steps(nx, s)))  22.9 us
    all_to_all x1, blocking collectives, body(): lax.all_to_all(jnp.broadcast_to(h[None], (ny,) + h.shape), 'y', split_axi...  22.6 us
    all_to_all x1, starting transfers between devices, body(): x = lax.all_to_all(x, ('y', 'z'), split_axis=0, concat_axis=0, tiled=True)  15.4 us
    ppermute x3, starting transfers between devices, body(): mine.append(lax.ppermute(got, 'x', steps(nx, s)))  10.5 us
  transfers between devices with their start and end apart: 12, of which 6 were waited for; matrix products, arithmetic and copies ran while one was open for 2% of the time, Pallas kernels for 2%

profile of v2, /device:TPU:50, one launch (start us, length us, event | category | flops | bytes accessed | tf_op | source)
XLA Modules:
  0.0 295.1 jit_solution(3655751170699151372)
XLA Ops:
  0.0 2.9 spread_tokens.1
  3.5 2.7 pack_weights.1
  6.2 1.8 slice_bitcast_fusion
  8.0 2.6 collective-permute-start
  10.6 2.7 collective-permute-start.1
  13.3 6.7 %collective-permute-start.2 = (bf16[16,2304]{1,0:T(8,128)(2,1)}, bf16[16,2304]{1,0:T(8,128)(2,1)}, u32[]{:S(2)}, u32[]{:S(2)}) collective-permute-start(bf16[16,2304]{1,0:T(8,128)(2,1)} %get-tuple-element.17), channel_id=1, source_target_pairs={{0,192},{64,256},{128,320},{192,384},{256,448},{320,0},{384,64},{4... | collective-permute-start | bytes 221192 | tf_op jit(solution)/shard_map/ppermute | solution.py:271
  20.1 2.3 collective-permute-start.3
  22.3 6.7 %collective-permute-start.4 = (bf16[16,2304]{1,0:T(8,128)(2,1)S(1)}, bf16[16,2304]{1,0:T(8,128)(2,1)}, u32[]{:S(2)}, u32[]{:S(2)}) collective-permute-start(bf16[16,2304]{1,0:T(8,128)(2,1)S(1)} %get-tuple-element.15), channel_id=1, source_target_pairs={{0,320},{64,384},{128,448},{192,0},{256,64},{320,128},{384,192},{4... | collective-permute-start | bytes 221192 | tf_op jit(solution)/shard_map/ppermute | solution.py:271
  29.0 15.4 %all-to-all-start = ((bf16[64,16,1280]{2,1,0:T(8,128)(2,1)}), bf16[64,16,1280]{2,1,0:T(8,128)(2,1)S(1)}, u32[]{:S(2)}, u32[]{:S(2)}) async-start(bf16[64,16,1280]{2,1,0:T(8,128)(2,1)} %spread_tokens.1), calls=%async_computation | async-start | bytes 5242880 | tf_op jit(solution)/shard_map/all_to_all | solution.py:265
  44.5 4.2 %collective-permute-start.5 = (bf16[16,2304]{1,0:T(8,128)(2,1)S(1)}, bf16[16,2304]{1,0:T(8,128)(2,1)S(1)}, u32[]{:S(2)}, u32[]{:S(2)}) collective-permute-start(bf16[16,2304]{1,0:T(8,128)(2,1)S(1)} %get-tuple-element.14), channel_id=1, source_target_pairs={{0,384},{64,448},{128,0},{192,64},{256,128},{320,192},{384,256},{4... | collective-permute-start | bytes 221192 | tf_op jit(solution)/shard_map/ppermute | solution.py:271
  48.7 0.9 bitcast_dynamic-update-slice_fusion.6
  49.6 2.4 collective-permute-start.6
  52.0 0.9 bitcast_dynamic-update-slice_fusion.5
  55.6 47.6 %collective-permute-done.5 = bf16[16,2304]{1,0:T(8,128)(2,1)S(1)} collective-permute-done((bf16[16,2304]{1,0:T(8,128)(2,1)S(1)}, bf16[16,2304]{1,0:T(8,128)(2,1)S(1)}, u32[]{:S(2)}, u32[]{:S(2)}) %collective-permute-start.5) | collective-permute-done | bytes 73760 | tf_op jit(solution)/shard_map/ppermute | solution.py:271
  103.1 1.5 collective-permute-done.6
  104.6 3.4 %collective-permute-start.7 = (bf16[8,16,2304]{2,1,0:T(8,128)(2,1)S(1)}, bf16[8,16,2304]{2,1,0:T(8,128)(2,1)S(1)}, u32[]{:S(2)}, u32[]{:S(2)}) collective-permute-start(bf16[8,16,2304]{2,1,0:T(8,128)(2,1)S(1)} %bitcast_dynamic-update-slice_fusion), channel_id=1, source_target_pairs={{0,2},{2,4},{4,6},{6,0},{1,3},{3,5},{5,7},{7,1},{8,10},{10,12},{12... | collective-permute-start | bytes 1769480 | tf_op jit(solution)/shard_map/ppermute | solution.py:275
  108.0 3.0 %collective-permute-start.8 = (bf16[8,16,2304]{2,1,0:T(8,128)(2,1)S(1)}, bf16[8,16,2304]{2,1,0:T(8,128)(2,1)S(1)}, u32[]{:S(2)}, u32[]{:S(2)}) collective-permute-start(bf16[8,16,2304]{2,1,0:T(8,128)(2,1)S(1)} %bitcast_dynamic-update-slice_fusion), channel_id=1, source_target_pairs={{0,4},{2,6},{4,0},{6,2},{1,5},{3,7},{5,1},{7,3},{8,12},{10,14},{12... | collective-permute-start | bytes 1769480 | tf_op jit(solution)/shard_map/ppermute | solution.py:275
  111.0 4.1 %collective-permute-start.9 = (bf16[8,16,2304]{2,1,0:T(8,128)(2,1)S(1)}, bf16[8,16,2304]{2,1,0:T(8,128)(2,1)S(1)}, u32[]{:S(2)}, u32[]{:S(2)}) collective-permute-start(bf16[8,16,2304]{2,1,0:T(8,128)(2,1)S(1)} %bitcast_dynamic-update-slice_fusion), channel_id=1, source_target_pairs={{0,6},{2,0},{4,2},{6,4},{1,7},{3,1},{5,3},{7,5},{8,14},{10,8},{12,... | collective-permute-start | bytes 1769480 | tf_op jit(solution)/shard_map/ppermute | solution.py:275
  115.1 7.6 %collective-permute-done.7 = bf16[8,16,2304]{2,1,0:T(8,128)(2,1)S(1)} collective-permute-done((bf16[8,16,2304]{2,1,0:T(8,128)(2,1)S(1)}, bf16[8,16,2304]{2,1,0:T(8,128)(2,1)S(1)}, u32[]{:S(2)}, u32[]{:S(2)}) %collective-permute-start.7) | collective-permute-done | bytes 589856 | tf_op jit(solution)/shard_map/ppermute | solution.py:275
  122.7 5.0 %collective-permute-done.8 = bf16[8,16,2304]{2,1,0:T(8,128)(2,1)S(1)} collective-permute-done((bf16[8,16,2304]{2,1,0:T(8,128)(2,1)S(1)}, bf16[8,16,2304]{2,1,0:T(8,128)(2,1)S(1)}, u32[]{:S(2)}, u32[]{:S(2)}) %collective-permute-start.8) | collective-permute-done | bytes 589856 | tf_op jit(solution)/shard_map/ppermute | solution.py:275
  127.7 10.3 %collective-permute-done.9 = bf16[8,16,2304]{2,1,0:T(8,128)(2,1)S(1)} collective-permute-done((bf16[8,16,2304]{2,1,0:T(8,128)(2,1)S(1)}, bf16[8,16,2304]{2,1,0:T(8,128)(2,1)S(1)}, u32[]{:S(2)}, u32[]{:S(2)}) %collective-permute-start.9) | collective-permute-done | bytes 589856 | tf_op jit(solution)/shard_map/ppermute | solution.py:275
  138.0 1.8 pad_maximum_fusion.mine_ref
  139.8 1.9 collective-permute-start.10
  142.4 4.1 %collective-permute-done.10.other_ref = bf16[4,8,16,2304]{3,2,1,0:T(8,128)(2,1)} collective-permute-done((bf16[4,8,16,2304]{3,2,1,0:T(8,128)(2,1)}, bf16[4,8,16,2304]{3,2,1,0:T(8,128)(2,1)}, u32[]{:S(2)}, u32[]{:S(2)}) %collective-permute-start.10) | collective-permute-done | bytes 2359328 | tf_op jit(solution)/shard_map/ppermute | solution.py:277
  146.5 5.3 %tile_weights.1 = (bf16[1152,1024]{1,0:T(8,128)(2,1)}, bf16[1024,1152]{1,0:T(8,128)(2,1)}) custom-call(s32[4]{0:T(128)} %pad_add_fusion.where_ref, bf16[4,8,16,2304]{3,2,1,0:T(8,128)(2,1)} %pad_maximum_fusion.mine_ref, bf16[4,8,16,2304]{3,2,1,0:T(8,128)(2,1)} %collective-permute-done.10.other_ref), custom_call_target="tpu_custom_call" | custom-call | tf_op jit(solution)/shard_map/tile_weights/pallas_call | solution.py:138
  151.8 1.5 copy-done
  153.3 7.2 %first_product.1 = bf16[8,320,128]{2,1,0:T(8,128)(2,1)} custom-call(s32[4]{0:T(128)} %pad_add_fusion.where_ref, bf16[1024,1280]{1,0:T(8,128)(2,1)} %bitcast.38, bf16[16,128]{1,0:T(8,128)(2,1)} %fusion.1.pick_ref, bf16[1152,1024]{1,0:T(8,128)(2,1)} %get-tuple-element.11.wide_ref), custom_call_target="tpu_custom_call" | custom-call | tf_op jit(solution)/shard_map/first_product/pallas_call | solution.py:181
  160.6 24.0 %all_to_all.20 = bf16[8,320,128]{2,1,0:T(8,128)(2,1)S(1)} all-to-all(bf16[8,320,128]{2,1,0:T(8,128)(2,1)} %first_product.1), channel_id=1, replica_groups=mesh['y'=8,'z'=8,'x'=4,'c'=2] {'y'}, dimensions={0} | all-to-all | bytes 1310720 | tf_op jit(solution)/shard_map/all_to_all | solution.py:284
  184.7 22.6 %all_to_all.21.h_ref = bf16[8,320,128]{2,1,0:T(8,128)(2,1)} all-to-all(bf16[8,320,128]{2,1,0:T(8,128)(2,1)S(1)} %broadcast_in_dim.2), channel_id=1, replica_groups=mesh['y'=8,'z'=8,'x'=4,'c'=2] {'y'}, dimensions={0} | all-to-all | bytes 1310720 | tf_op jit(solution)/shard_map/all_to_all | solution.py:287
  207.3 9.0 %second_product.1 = bf16[64,16,1152]{2,1,0:T(8,128)(2,1)} custom-call(s32[4]{0:T(128)} %pad_add_fusion.where_ref, bf16[8,320,128]{2,1,0:T(8,128)(2,1)} %all_to_all.21.h_ref, bf16[1024,1280]{1,0:T(8,128)(2,1)} %bitcast.39, bf16[16,128]{1,0:T(8,128)(2,1)} %fusion.1.pick_ref, bf16[1024,1152]{1,0:T(8,128)(2,1)} %get-tuple-element.12.tall_ref), custom_call_target="tpu_custom_call" | custom-call | tf_op jit(solution)/shard_map/second_product/pallas_call | solution.py:219
  216.4 76.1 %all_to_all.22.y_ref = bf16[64,16,1152]{2,1,0:T(8,128)(2,1)} all-to-all(bf16[64,16,1152]{2,1,0:T(8,128)(2,1)} %second_product.1), channel_id=1, replica_groups=mesh['y'=8,'z'=8,'x'=4,'c'=2] {'y','z'}, dimensions={0} | all-to-all | bytes 4718592 | tf_op jit(solution)/shard_map/all_to_all | solution.py:291
  292.4 2.7 combine.1
  (21 shorter events, 4.2 us)
Async XLA Ops:
  8.0 36.5 %collective-permute-start = (bf16[16,2304]{1,0:T(8,128)(2,1)}, bf16[16,2304]{1,0:T(8,128)(2,1)}, u32[]{:S(2)}, u32[]{:S(2)}) collective-permute-start(bf16[16,2304]{1,0:T(8,128)(2,1)} %get-tuple-element.19), channel_id=1, source_target_pairs={{0,64},{64,128},{128,192},{192,256},{256,320},{320,384},{384,448},... | collective-permute-start | bytes 221192 | tf_op jit(solution)/shard_map/ppermute | solution.py:271
  10.6 38.9 %collective-permute-start.1 = (bf16[16,2304]{1,0:T(8,128)(2,1)}, bf16[16,2304]{1,0:T(8,128)(2,1)}, u32[]{:S(2)}, u32[]{:S(2)}) collective-permute-start(bf16[16,2304]{1,0:T(8,128)(2,1)} %get-tuple-element.18), channel_id=1, source_target_pairs={{0,128},{64,192},{128,256},{192,320},{256,384},{320,448},{384,0},{... | collective-permute-start | bytes 221192 | tf_op jit(solution)/shard_map/ppermute | solution.py:271
  13.3 39.6 %collective-permute-start.2 = (bf16[16,2304]{1,0:T(8,128)(2,1)}, bf16[16,2304]{1,0:T(8,128)(2,1)}, u32[]{:S(2)}, u32[]{:S(2)}) collective-permute-start(bf16[16,2304]{1,0:T(8,128)(2,1)} %get-tuple-element.17), channel_id=1, source_target_pairs={{0,192},{64,256},{128,320},{192,384},{256,448},{320,0},{384,64},{4... | collective-permute-start | bytes 221192 | tf_op jit(solution)/shard_map/ppermute | solution.py:271
  20.1 33.7 %collective-permute-start.3 = (bf16[16,2304]{1,0:T(8,128)(2,1)S(1)}, bf16[16,2304]{1,0:T(8,128)(2,1)}, u32[]{:S(2)}, u32[]{:S(2)}) collective-permute-start(bf16[16,2304]{1,0:T(8,128)(2,1)S(1)} %get-tuple-element.16), channel_id=1, source_target_pairs={{0,256},{64,320},{128,384},{192,448},{256,0},{320,64},{384,128},{4... | collective-permute-start | bytes 221192 | tf_op jit(solution)/shard_map/ppermute | solution.py:271
  22.3 32.3 %collective-permute-start.4 = (bf16[16,2304]{1,0:T(8,128)(2,1)S(1)}, bf16[16,2304]{1,0:T(8,128)(2,1)}, u32[]{:S(2)}, u32[]{:S(2)}) collective-permute-start(bf16[16,2304]{1,0:T(8,128)(2,1)S(1)} %get-tuple-element.15), channel_id=1, source_target_pairs={{0,320},{64,384},{128,448},{192,0},{256,64},{320,128},{384,192},{4... | collective-permute-start | bytes 221192 | tf_op jit(solution)/shard_map/ppermute | solution.py:271
  29.0 122.8 %all-to-all-start = ((bf16[64,16,1280]{2,1,0:T(8,128)(2,1)}), bf16[64,16,1280]{2,1,0:T(8,128)(2,1)S(1)}, u32[]{:S(2)}, u32[]{:S(2)}) async-start(bf16[64,16,1280]{2,1,0:T(8,128)(2,1)} %spread_tokens.1), calls=%async_computation | async-start | bytes 5242880 | tf_op jit(solution)/shard_map/all_to_all | solution.py:265
  44.5 58.6 %collective-permute-start.5 = (bf16[16,2304]{1,0:T(8,128)(2,1)S(1)}, bf16[16,2304]{1,0:T(8,128)(2,1)S(1)}, u32[]{:S(2)}, u32[]{:S(2)}) collective-permute-start(bf16[16,2304]{1,0:T(8,128)(2,1)S(1)} %get-tuple-element.14), channel_id=1, source_target_pairs={{0,384},{64,448},{128,0},{192,64},{256,128},{320,192},{384,256},{4... | collective-permute-start | bytes 221192 | tf_op jit(solution)/shard_map/ppermute | solution.py:271
  49.6 55.0 %collective-permute-start.6 = (bf16[16,2304]{1,0:T(8,128)(2,1)S(1)}, bf16[16,2304]{1,0:T(8,128)(2,1)S(1)}, u32[]{:S(2)}, u32[]{:S(2)}) collective-permute-start(bf16[16,2304]{1,0:T(8,128)(2,1)S(1)} %get-tuple-element.13), channel_id=1, source_target_pairs={{0,448},{64,0},{128,64},{192,128},{256,192},{320,256},{384,320},{4... | collective-permute-start | bytes 221192 | tf_op jit(solution)/shard_map/ppermute | solution.py:271
  104.6 18.1 %collective-permute-start.7 = (bf16[8,16,2304]{2,1,0:T(8,128)(2,1)S(1)}, bf16[8,16,2304]{2,1,0:T(8,128)(2,1)S(1)}, u32[]{:S(2)}, u32[]{:S(2)}) collective-permute-start(bf16[8,16,2304]{2,1,0:T(8,128)(2,1)S(1)} %bitcast_dynamic-update-slice_fusion), channel_id=1, source_target_pairs={{0,2},{2,4},{4,6},{6,0},{1,3},{3,5},{5,7},{7,1},{8,10},{10,12},{12... | collective-permute-start | bytes 1769480 | tf_op jit(solution)/shard_map/ppermute | solution.py:275
  108.0 19.6 %collective-permute-start.8 = (bf16[8,16,2304]{2,1,0:T(8,128)(2,1)S(1)}, bf16[8,16,2304]{2,1,0:T(8,128)(2,1)S(1)}, u32[]{:S(2)}, u32[]{:S(2)}) collective-permute-start(bf16[8,16,2304]{2,1,0:T(8,128)(2,1)S(1)} %bitcast_dynamic-update-slice_fusion), channel_id=1, source_target_pairs={{0,4},{2,6},{4,0},{6,2},{1,5},{3,7},{5,1},{7,3},{8,12},{10,14},{12... | collective-permute-start | bytes 1769480 | tf_op jit(solution)/shard_map/ppermute | solution.py:275
  111.0 26.9 %collective-permute-start.9 = (bf16[8,16,2304]{2,1,0:T(8,128)(2,1)S(1)}, bf16[8,16,2304]{2,1,0:T(8,128)(2,1)S(1)}, u32[]{:S(2)}, u32[]{:S(2)}) collective-permute-start(bf16[8,16,2304]{2,1,0:T(8,128)(2,1)S(1)} %bitcast_dynamic-update-slice_fusion), channel_id=1, source_target_pairs={{0,6},{2,0},{4,2},{6,4},{1,7},{3,1},{5,3},{7,5},{8,14},{10,8},{12,... | collective-permute-start | bytes 1769480 | tf_op jit(solution)/shard_map/ppermute | solution.py:275
  139.8 6.8 %collective-permute-start.10 = (bf16[4,8,16,2304]{3,2,1,0:T(8,128)(2,1)}, bf16[4,8,16,2304]{3,2,1,0:T(8,128)(2,1)}, u32[]{:S(2)}, u32[]{:S(2)}) collective-permute-start(bf16[4,8,16,2304]{3,2,1,0:T(8,128)(2,1)} %pad_maximum_fusion.mine_ref), channel_id=1, source_target_pairs={{0,1},{1,0},{2,3},{3,2},{4,5},{5,4},{6,7},{7,6},{8,9},{9,8},{10,11... | collective-permute-start | bytes 7077896 | tf_op jit(solution)/shard_map/ppermute | solution.py:277
  151.8 1.5 copy-start
  153.3 31.3 %copy-start.1 = (f32[128]{0:T(128)S(1)}, f32[128]{0:T(128)}, u32[]{:S(2)}) copy-start(f32[128]{0:T(128)} %param.8) | copy-start | bytes 1540

commit v3 on v1

v3 whole, which is shorter than its diff:
```python
import functools
import math

import jax
import jax.numpy as jnp
from jax import lax
from jax.experimental import pallas as pl
from jax.experimental.pallas import tpu as pltpu
from jax.sharding import Mesh
from jax.sharding import PartitionSpec as P

CAP = 5
LANES = 128
BF16 = jnp.bfloat16
F32 = jnp.float32


def pack_kernel(where_ref, tokens_ref, ids_ref, w_in_ref, w_out_ref, out_ref, in_rows, sems, *, ny, nz, nt):
    share = where_ref[0]
    width = tokens_ref.shape[1] // ny
    part = width // nt
    toks = tokens_ref.shape[0]
    copies = []
    for k in range(ny):
        copies.append(
            pltpu.make_async_copy(
                w_in_ref.at[pl.ds(k * width + share * part, part), :], in_rows.at[k], sems.at[k]
            )
        )
    for c in copies:
        c.start()
    same = lax.broadcasted_iota(jnp.int32, (ids_ref.shape[0],) * 2, 0)
    same = same == lax.broadcasted_iota(jnp.int32, same.shape, 1)
    ids = lax.dot_general(
        ids_ref[...].astype(F32).astype(BF16),
        jnp.where(same, 1.0, 0.0).astype(BF16),
        (((0,), (0,)), ((), ())),
        preferred_element_type=F32,
    )
    lane = lax.broadcasted_iota(jnp.int32, (toks, LANES), 1)
    block = jnp.where(lane < ny * nz, (lane % ny) * nz + lane // ny, -1).astype(F32)
    named = jnp.zeros((toks, LANES), F32)
    for k in range(ids.shape[1]):
        named = jnp.where(ids[:, k : k + 1] == block, 1.0, named)
    row = lax.broadcasted_iota(jnp.int32, (toks, toks), 0)
    col = lax.broadcasted_iota(jnp.int32, (toks, toks), 1)
    before = jnp.where(col < row, 1.0, 0.0).astype(BF16)
    position = jnp.dot(before, named.astype(BF16), preferred_element_type=F32)
    slots = jnp.where(named > 0.0, position, -1.0).astype(BF16)
    for k in range(ny):
        out_ref[k, :, 0:width] = tokens_ref[:, k * width : (k + 1) * width]
        out_ref[k, :, width : width + LANES] = slots
        out_ref[k, :, width + LANES : 2 * width + LANES] = w_out_ref[:, k * width : (k + 1) * width]
    base = 2 * width + LANES
    for k in range(ny):
        copies[k].wait()
        for g in range(part // toks):
            out_ref[k, :, base + g * LANES : base + (g + 1) * LANES] = in_rows[
                k, g * toks : (g + 1) * toks, :
            ]


def pack(where, tokens, ids, w_in, w_out, ny, nz, nt):
    toks, model = tokens.shape
    width = model // ny
    part = width // nt
    return pl.pallas_call(
        functools.partial(pack_kernel, ny=ny, nz=nz, nt=nt),
        out_shape=jax.ShapeDtypeStruct((ny, toks, 3 * width + LANES), BF16),
        grid_spec=pltpu.PrefetchScalarGridSpec(
            num_scalar_prefetch=1,
            grid=(1,),
            in_specs=[
                pl.BlockSpec((toks, model), lambda i, s: (0, 0)),
                pl.BlockSpec(ids.shape, lambda i, s: (0, 0)),
                pl.BlockSpec(memory_space=pl.ANY),
                pl.BlockSpec((w_out.shape[0] // nt, model), lambda i, s: (s[0], 0)),
            ],
            out_specs=pl.BlockSpec((ny, toks, 3 * width + LANES), lambda i, s: (0, 0, 0)),
            scratch_shapes=[
                pltpu.VMEM((ny, part, LANES), BF16),
                pltpu.SemaphoreType.DMA((ny,)),
            ],
        ),
        name="pack",
    )(where, tokens, ids, w_in, w_out)


def first_kernel(x_ref, pick_ref, w_ref, out_ref, wide, *, ny, nm, chunk, toks):
    nt, _, rows, lanes = w_ref.shape
    groups = lanes // LANES
    width = nt * rows * groups
    for t in range(nt):
        for g in range(groups):
            top = (t * groups + g) * rows
            for j in range(ny):
                wide[top : top + rows, j * LANES : (j + 1) * LANES] = w_ref[
                    t, j, :, g * LANES : (g + 1) * LANES
                ]
    per = chunk // toks * CAP
    band = ny * toks
    col = lax.broadcasted_iota(jnp.int32, (pick_ref.shape[0], chunk), 1)
    slot = lax.broadcasted_iota(jnp.int32, (per, chunk), 0).astype(F32)
    first = (col // toks * CAP).astype(F32)
    halves = x_ref.shape[0] // chunk // nm
    for m in range(x_ref.shape[0] // chunk):
        bands = [
            (m // halves) + nm * (m % halves * (chunk // band) + i) for i in range(chunk // band)
        ]
        x = jnp.concatenate([x_ref[r * band : (r + 1) * band, :] for r in bands], axis=0)
        h = jnp.dot(x[:, 0:width], wide[...], preferred_element_type=F32).astype(BF16)
        at = lax.dot_general(
            pick_ref[...],
            x[:, width : width + LANES],
            (((1,), (1,)), ((), ())),
            preferred_element_type=F32,
        )
        at = jnp.where(at >= 0.0, at + first, -1.0)
        for j in range(ny):
            s = jnp.where(slot == at[j : j + 1, :], 1.0, 0.0).astype(BF16)
            rows_j = jnp.dot(s, h[:, j * LANES : (j + 1) * LANES], preferred_element_type=F32)
            out_ref[j, m * per : (m + 1) * per, :] = rows_j.astype(BF16)


def first_product(x, pick, w, ny, nm, toks):
    chunk = 256
    slots = x.shape[0] // toks * CAP
    return pl.pallas_call(
        functools.partial(first_kernel, ny=ny, nm=nm, chunk=chunk, toks=toks),
        out_shape=jax.ShapeDtypeStruct((ny, slots, LANES), BF16),
        scratch_shapes=[pltpu.VMEM((x.shape[1] - LANES, ny * LANES), BF16)],
        name="first_product",
    )(x, pick, w)


def second_kernel(
    where_ref, h_ref, x_ref, pick_ref, w_ref, out_ref, tall, spread, *, ny, nm, chunk, toks
):
    zm = where_ref[1]
    nt, _, _, rows, width = w_ref.shape
    band = ny * toks
    blocks = nm * ny
    for q in range(nm):
        for j in range(ny):
            for t in range(nt):
                top = ((q * ny + j) * nt + t) * rows
                tall[top : top + rows, :] = w_ref[t, q, j]
    per = chunk // toks * CAP
    row = lax.broadcasted_iota(jnp.int32, (chunk, pick_ref.shape[0]), 0)
    slot = lax.broadcasted_iota(jnp.int32, (chunk, per), 1).astype(F32)
    first = (row // toks * CAP).astype(F32)
    for m in range(x_ref.shape[0] // chunk // nm):
        pos = []
        for i in range(chunk // band):
            top = (nm * (m * (chunk // band) + i) + zm) * band
            pos.append(x_ref[pl.ds(pl.multiple_of(top, band), band), :])
        at = lax.dot_general(
            jnp.concatenate(pos, axis=0),
            pick_ref[...],
            (((1,), (1,)), ((), ())),
            preferred_element_type=F32,
        )
        at = jnp.where(at >= 0.0, at + first, -1.0)
        for b in range(blocks):
            source = b % ny * nm + (zm + b // ny) % nm
            s = jnp.where(slot == at[:, b : b + 1], 1.0, 0.0).astype(BF16)
            full = jnp.dot(
                s, h_ref[source, m * per : (m + 1) * per, :], preferred_element_type=F32
            )
            spread[:, b * LANES : (b + 1) * LANES] = full.astype(BF16)
        out = jnp.dot(spread[...], tall[...], preferred_element_type=F32).astype(BF16)
        devices = chunk // toks
        out_ref[m * devices : (m + 1) * devices] = out.reshape(devices, toks, width)


def second_product(where, h, x, pick, w, ny, nm, toks):
    chunk = 256
    width = w.shape[-1]
    total = x.shape[0]
    devices = total // toks // nm
    return pl.pallas_call(
        functools.partial(second_kernel, ny=ny, nm=nm, chunk=chunk, toks=toks),
        out_shape=jax.ShapeDtypeStruct((devices, toks, width), BF16),
        grid_spec=pltpu.PrefetchScalarGridSpec(
            num_scalar_prefetch=1,
            grid=(1,),
            in_specs=[
                pl.BlockSpec(h.shape, lambda i, s: (0, 0, 0)),
                pl.BlockSpec((total, LANES), lambda i, s: (0, width // LANES)),
                pl.BlockSpec(pick.shape, lambda i, s: (0, 0)),
                pl.BlockSpec(w.shape, lambda i, s: (0,) * 5),
            ],
            out_specs=pl.BlockSpec((devices, toks, width), lambda i, s: (0, 0, 0)),
            scratch_shapes=[
                pltpu.VMEM((nm * ny * LANES, width), BF16),
                pltpu.VMEM((chunk, nm * ny * LANES), BF16),
            ],
        ),
        name="second_product",
    )(where, h, x, pick, w)


def combine_kernel(y_ref, out_ref, *, ny):
    width = y_ref.shape[2]
    for k in range(ny):
        total = y_ref[k].astype(F32)
        for other in range(ny + k, y_ref.shape[0], ny):
            total = total + y_ref[other].astype(F32)
        out_ref[:, k * width : (k + 1) * width] = total.astype(BF16)


def combine(y, ny):
    return pl.pallas_call(
        functools.partial(combine_kernel, ny=ny),
        out_shape=jax.ShapeDtypeStruct((y.shape[1], y.shape[2] * ny), BF16),
        name="combine",
    )(y)


def near(value):
    return pltpu.with_memory_space_constraint(value, pltpu.VMEM)


def body(tokens, block_ids, w_in, bias_in, w_out):
    toks = tokens.shape[0]
    plane = ("zn", "zm")
    ny, nm = lax.axis_size("y"), lax.axis_size("zm")
    nz = lax.axis_size("zn") * nm
    nt = lax.axis_size("x") * lax.axis_size("c")
    width = tokens.shape[1] // ny
    share = lax.axis_index("x") * lax.axis_size("c") + lax.axis_index("c")
    zn, zm = lax.axis_index("zn"), lax.axis_index("zm")
    where = jnp.stack([share, zm]).astype(jnp.int32)

    payload = pack(where, tokens, block_ids.T, w_in, w_out, ny, nz, nt)
    got = lax.all_to_all(payload, "y", split_axis=0, concat_axis=0, tiled=True)
    x_part = got[:, :, : width + LANES].reshape(ny * toks, width + LANES)
    x = lax.all_gather(x_part, plane, axis=0, tiled=True)
    w1 = got[:, :, 2 * width + LANES :]
    w1 = lax.all_to_all(
        jnp.broadcast_to(w1[None], (nt,) + w1.shape), ("x", "c"), split_axis=0, concat_axis=0, tiled=True
    )
    w2 = got[:, :, width + LANES : 2 * width + LANES]
    w2 = jnp.stack([w2] + [lax.ppermute(w2, "zm", [(i, (i - k) % nm) for i in range(nm)]) for k in range(1, nm)])
    x, w1, w2 = lax.optimization_barrier((x, w1, w2))
    w2 = lax.all_gather(w2[None], ("x", "c"), axis=0, tiled=True)

    lane = jnp.arange(LANES, dtype=jnp.int32)[None, :]
    block = jnp.arange(nm * ny, dtype=jnp.int32)[:, None]
    group = zn * nm + (zm + block // ny) % nm
    pick2 = (lane == group * ny + block % ny).astype(BF16)
    pick1 = ((lane == (zn * nm + zm) * ny + block) & (block < ny)).astype(BF16)

    h = first_product(x, pick1, near(w1), ny, nm, toks)
    h = lax.all_to_all(h, "y", split_axis=0, concat_axis=0, tiled=True)
    h = jnp.sum(h.astype(F32), axis=0) + bias_in[None, :]
    h = jnp.maximum(h, 0.0).astype(BF16)
    h = h.reshape(1, nm, h.shape[0] // nm, LANES)
    h = jnp.broadcast_to(h, (ny,) + h.shape[1:]).reshape((ny * nm,) + h.shape[2:])
    h = lax.all_to_all(h, ("y", "zm"), split_axis=0, concat_axis=0, tiled=True)
    y = second_product(where, near(h), x, pick2, w2, ny, nm, toks)
    y = lax.all_to_all(y, ("zn", "y"), split_axis=0, concat_axis=0, tiled=True)
    return combine(near(y), ny)


def solution(mesh):
    side = math.isqrt(mesh.shape["blk"])
    cores, pair = 2, 2
    fine = Mesh(
        mesh.devices.reshape(side, side // pair, pair, mesh.shape["tok"] // cores, cores),
        ("y", "zn", "zm", "x", "c"),
    )
    rows = ("x", "c", "y", "zn", "zm")
    blocks = ("y", "zn", "zm")
    return jax.shard_map(
        body,
        mesh=fine,
        in_specs=(P(rows, None), P(rows, None), P(None, blocks), P(blocks), P(blocks, None)),
        out_specs=P(rows, None),
        check_vma=False,
    )
```

time: 222 us -> 204 us (0.919)
  the two profiles are of different devices: /device:TPU:14 before, /device:TPU:2 now
where the time goes in v3:
time: 204 us; the launch traced here: 203 us
  blocking collectives  96.3 us (47%)
  waiting for transfers between devices  54.7 us (27%)
  Pallas kernels  19.9 us (10%)
  between operations  13.5 us (7%)
  starting transfers between devices  12.7 us (6%)
  local copies, waits for them, and re-layouts  3.33 us (2%)
  other arithmetic  2.98 us (1%)
    all_to_all x1, blocking collectives, body(): y = lax.all_to_all(y, ('zn', 'y'), split_axis=0, concat_axis=0, tiled=True)  41.6 us
    all_to_all x1, blocking collectives, body(): got = lax.all_to_all(payload, 'y', split_axis=0, concat_axis=0, tiled=True)  33 us
    all_to_all x1, blocking collectives, body(): h = lax.all_to_all(h, 'y', split_axis=0, concat_axis=0, tiled=True)  21.7 us
    all_to_all x1, waiting for transfers between devices, body(): h = lax.all_to_all(h, ('y', 'zm'), split_axis=0, concat_axis=0, tiled=True)  15.7 us
    all_gather x1, waiting for transfers between devices, body(): x = lax.all_gather(x_part, plane, axis=0, tiled=True)  15.6 us
    all_to_all x1, waiting for transfers between devices, body(): lax.all_to_all(jnp.broadcast_to(w1[None], (nt,) + w1.shape), ('x', 'c'),...  12.1 us
    ppermute x1, waiting for transfers between devices, body(): lax.ppermute(w2, 'zm', [(i, (i - k) % nm) for i in range(nm)])  11.2 us
    pallas_call x1, Pallas kernels, second_product(): pl.pallas_call(functools.partial(second_kernel, ny=ny, nm=nm, chunk=chunk...  8.81 us
  transfers between devices with their start and end apart: 5, of which 4 were waited for; matrix products, arithmetic and copies ran while one was open for 2% of the time, Pallas kernels for 3%

profile of v3, /device:TPU:2, one launch (start us, length us, event | category | flops | bytes accessed | tf_op | source)
XLA Modules:
  0.0 203.4 jit_solution(15397031432468470754)
XLA Ops:
  6.5 0.0 all-gather.4.cloned.1.call-start
  6.5 0.6 pad_add_fusion.where_ref
  7.1 3.6 %pack.1 = bf16[8,16,3584]{2,1,0:T(8,128)(2,1)} custom-call(s32[2]{0:T(128)} %pad_add_fusion.where_ref, bf16[16,9216]{1,0:T(8,128)(2,1)} %tokens_ref.1, s32[8,16]{1,0:T(8,128)} %bitcast.14, bf16[9216,128]{1,0:T(8,128)(2,1)} %w_in_ref.1, bf16[128,9216]{1,0:T(8,128)(2,1)} %w_out_ref.1), custom_call_target="tpu_custom_call" | custom-call | tf_op jit(solution)/shard_map/pack/pallas_call | solution.py:67
  10.8 33.0 %all_to_all.25 = bf16[8,16,3584]{2,1,0:T(8,128)(2,1)S(1)} all-to-all(bf16[8,16,3584]{2,1,0:T(8,128)(2,1)} %pack.1), channel_id=1, replica_groups=mesh['y'=8,'zn'=4,'zm'=2,'x'=4,'c'=2] {'y'}, dimensions={0} | all-to-all | bytes 1835008 | tf_op jit(solution)/shard_map/all_to_all | solution.py:236
  43.8 0.7 slice.12
  44.5 0.0 all-gather.4.cloned.1.call-update
  44.6 0.1 slice_bitcast_fusion
  44.6 1.6 broadcast_in_dim.6
  46.2 4.8 %all-to-all-start.1 = ((bf16[8,8,16,1152]{3,2,1,0:T(8,128)(2,1)}), bf16[8,8,16,1152]{3,2,1,0:T(8,128)(2,1)S(1)}, u32[]{:S(2)}, u32[]{:S(2)}) async-start(bf16[8,8,16,1152]{3,2,1,0:T(8,128)(2,1)} %broadcast_in_dim.6), calls=%async_computation.1 | async-start | bytes 4718592 | tf_op jit(solution)/shard_map/all_to_all | solution.py:240
  51.0 0.0 all-gather.6.cloned.1.call-start
  51.0 4.3 %collective-permute-start = (bf16[8,16,1152]{2,1,0:T(8,128)(2,1)S(1)}, bf16[8,16,1152]{2,1,0:T(8,128)(2,1)S(1)}, u32[]{:S(2)}, u32[]{:S(2)}) collective-permute-start(bf16[8,16,1152]{2,1,0:T(8,128)(2,1)S(1)} %get-tuple-element.12), channel_id=1, source_target_pairs={{0,8},{8,0},{1,9},{9,1},{2,10},{10,2},{3,11},{11,3},{4,12},{12,4},... | collective-permute-start | bytes 884744 | tf_op jit(solution)/shard_map/ppermute | solution.py:244
  55.3 11.2 %collective-permute-done = bf16[8,16,1152]{2,1,0:T(8,128)(2,1)S(1)} collective-permute-done((bf16[8,16,1152]{2,1,0:T(8,128)(2,1)S(1)}, bf16[8,16,1152]{2,1,0:T(8,128)(2,1)S(1)}, u32[]{:S(2)}, u32[]{:S(2)}) %collective-permute-start) | collective-permute-done | bytes 294944 | tf_op jit(solution)/shard_map/ppermute | solution.py:244
  66.5 0.9 pad_maximum_fusion
  67.4 12.1 %all-to-all-done.1.w_ref = bf16[8,8,16,1152]{3,2,1,0:T(8,128)(2,1)S(1)} async-done(((bf16[8,8,16,1152]{3,2,1,0:T(8,128)(2,1)}), bf16[8,8,16,1152]{3,2,1,0:T(8,128)(2,1)S(1)}, u32[]{:S(2)}, u32[]{:S(2)}) %all-to-all-start.1) | async-done | bytes 2359328 | tf_op jit(solution)/shard_map/all_to_all | solution.py:240
  79.6 15.6 %all-gather.4.cloned.1.call-done.x_ref = bf16[1024,1280]{1,0:T(8,128)(2,1)} async-done(((bf16[128,1280]{1,0:T(8,128)(2,1)}), bf16[1024,1280]{1,0:T(8,128)(2,1)}) %all-gather.4.cloned.1.call-update) | async-done | bytes 2621456 | tf_op jit(solution)/shard_map/all_gather | solution.py:238
  95.2 0.0 all-gather.6.cloned.1.call-update
  95.2 0.7 fusion.1.pick_ref
  95.9 0.0 copy-start
  95.9 6.6 %first_product.1 = bf16[8,320,128]{2,1,0:T(8,128)(2,1)} custom-call(bf16[1024,1280]{1,0:T(8,128)(2,1)} %all-gather.4.cloned.1.call-done.x_ref, bf16[16,128]{1,0:T(8,128)(2,1)} %fusion.1.pick_ref, bf16[8,8,16,1152]{3,2,1,0:T(8,128)(2,1)S(1)} %all-to-all-done.1.w_ref), custom_call_target="tpu_custom_call" | custom-call | tf_op jit(solution)/shard_map/first_product/pallas_call | solution.py:128
  102.5 21.7 %all_to_all.26 = bf16[8,320,128]{2,1,0:T(8,128)(2,1)S(1)} all-to-all(bf16[8,320,128]{2,1,0:T(8,128)(2,1)} %first_product.1), channel_id=1, replica_groups=mesh['y'=8,'zn'=4,'zm'=2,'x'=4,'c'=2] {'y'}, dimensions={0} | all-to-all | bytes 1310720 | tf_op jit(solution)/shard_map/all_to_all | solution.py:255
  124.2 0.1 convert_reduce_fusion
  124.3 0.0 copy-done
  124.4 0.9 broadcast_in_dim.7
  125.3 3.6 %all-to-all-start.3 = ((bf16[16,160,128]{2,1,0:T(8,128)(2,1)}), bf16[16,160,128]{2,1,0:T(8,128)(2,1)S(1)}, u32[]{:S(2)}, u32[]{:S(2)}) async-start(bf16[16,160,128]{2,1,0:T(8,128)(2,1)} %bitcast.7), calls=%async_computation.3 | async-start | bytes 1310720 | tf_op jit(solution)/shard_map/all_to_all | solution.py:260
  128.9 0.7 fusion.2.pick_ref
  129.6 15.7 %all-to-all-done.3.h_ref = bf16[16,160,128]{2,1,0:T(8,128)(2,1)S(1)} async-done(((bf16[16,160,128]{2,1,0:T(8,128)(2,1)}), bf16[16,160,128]{2,1,0:T(8,128)(2,1)S(1)}, u32[]{:S(2)}, u32[]{:S(2)}) %all-to-all-start.3) | async-done | bytes 655392 | tf_op jit(solution)/shard_map/all_to_all | solution.py:260
  145.3 0.0 all-gather.6.cloned.1.call-done
  145.3 8.8 %second_product.1 = bf16[32,16,1152]{2,1,0:T(8,128)(2,1)} custom-call(s32[2]{0:T(128)} %pad_add_fusion.where_ref, bf16[16,160,128]{2,1,0:T(8,128)(2,1)S(1)} %all-to-all-done.3.h_ref, bf16[1024,1280]{1,0:T(8,128)(2,1)} %all-gather.4.cloned.1.call-done.x_ref, bf16[16,128]{1,0:T(8,128)(2,1)} %fusion.2.pick_ref, bf16[8,2,8,16,1152]{4,3,2,1,0:T(8,128)(2,1)} %bitcast.10), custom_call_target="tpu_custom_call" | custom-call | tf_op jit(solution)/shard_map/second_product/pallas_call | solution.py:181
  154.2 41.6 %all_to_all.27.y_ref = bf16[32,16,1152]{2,1,0:T(8,128)(2,1)S(1)} all-to-all(bf16[32,16,1152]{2,1,0:T(8,128)(2,1)} %second_product.1), channel_id=1, replica_groups=mesh['y'=8,'zn'=4,'zm'=2,'x'=4,'c'=2] {'zn','y'}, dimensions={0} | all-to-all | bytes 2359296 | tf_op jit(solution)/shard_map/all_to_all | solution.py:262
  195.7 0.9 combine.1
  (4 shorter events, 0.1 us)
Async XLA Ops:
  6.5 88.6 %all-gather.4.cloned.1.call-start = ((), (), s32[]{:S(2)}) async-start(), calls=%async_computation.5 | async-start | bytes 2949120 | tf_op jit(solution)/shard_map/all_gather | solution.py:238
  46.2 33.4 %all-to-all-start.1 = ((bf16[8,8,16,1152]{3,2,1,0:T(8,128)(2,1)}), bf16[8,8,16,1152]{3,2,1,0:T(8,128)(2,1)S(1)}, u32[]{:S(2)}, u32[]{:S(2)}) async-start(bf16[8,8,16,1152]{3,2,1,0:T(8,128)(2,1)} %broadcast_in_dim.6), calls=%async_computation.1 | async-start | bytes 4718592 | tf_op jit(solution)/shard_map/all_to_all | solution.py:240
  51.0 94.3 %all-gather.6.cloned.1.call-start = ((), (), s32[]{:S(2)}) async-start(), calls=%async_computation.6 | async-start | bytes 5308416 | tf_op jit(solution)/shard_map/all_gather | solution.py:246
  51.0 15.4 %collective-permute-start = (bf16[8,16,1152]{2,1,0:T(8,128)(2,1)S(1)}, bf16[8,16,1152]{2,1,0:T(8,128)(2,1)S(1)}, u32[]{:S(2)}, u32[]{:S(2)}) collective-permute-start(bf16[8,16,1152]{2,1,0:T(8,128)(2,1)S(1)} %get-tuple-element.12), channel_id=1, source_target_pairs={{0,8},{8,0},{1,9},{9,1},{2,10},{10,2},{3,11},{11,3},{4,12},{12,4},... | collective-permute-start | bytes 884744 | tf_op jit(solution)/shard_map/ppermute | solution.py:244
  95.9 28.4 %copy-start = (f32[128]{0:T(128)S(1)}, f32[128]{0:T(128)}, u32[]{:S(2)}) copy-start(f32[128]{0:T(128)} %param.8) | copy-start | bytes 1540
  125.3 20.0 %all-to-all-start.3 = ((bf16[16,160,128]{2,1,0:T(8,128)(2,1)}), bf16[16,160,128]{2,1,0:T(8,128)(2,1)S(1)}, u32[]{:S(2)}, u32[]{:S(2)}) async-start(bf16[16,160,128]{2,1,0:T(8,128)(2,1)} %bitcast.7), calls=%async_computation.3 | async-start | bytes 1310720 | tf_op jit(solution)/shard_map/all_to_all | solution.py:260
Sparse Core Ops, SparseCore 0:
  44.7 50.4 all-gather.3
  97.3 32.4 all-gather.5

commit v4 on v3

v4 whole, which is shorter than its diff:
```python
import functools
import math

import jax
import jax.numpy as jnp
from jax import lax
from jax.experimental import pallas as pl
from jax.experimental.pallas import tpu as pltpu
from jax.sharding import Mesh
from jax.sharding import PartitionSpec as P

CAP = 5
LANES = 128
CHUNK = 256
BF16 = jnp.bfloat16
F32 = jnp.float32
ANY = pl.BlockSpec(memory_space=pl.ANY)
VMEM = pl.BlockSpec(memory_space=pltpu.VMEM)


def sizes():
    ny, nn, nm = lax.axis_size("y"), lax.axis_size("zn"), lax.axis_size("zm")
    return ny, nn, nm, lax.axis_size("x"), lax.axis_size("c")


def near(value):
    return pltpu.with_memory_space_constraint(value, pltpu.VMEM)


def pack_kernel(tokens_ref, ids_ref, w_in_ref, w_out_ref, out_ref, w2_ref, in_rows, sems, *, dims):
    ny, nn, nm, nx, nc = dims
    nz, nt = nn * nm, nx * nc
    share = lax.axis_index("x") * nc + lax.axis_index("c")
    width = tokens_ref.shape[1] // ny
    part = width // nt
    toks = tokens_ref.shape[0]
    rows = w_out_ref.shape[0] // nt
    copies = []
    for k in range(ny):
        top = pl.multiple_of(k * width + share * part, 16)
        copies.append(
            pltpu.make_async_copy(w_in_ref.at[pl.ds(top, part), :], in_rows.at[k], sems.at[0, k])
        )
    for k in range(ny):
        cut = pl.ds(k * width, width)
        copies.append(
            pltpu.make_async_copy(
                tokens_ref.at[:, cut], out_ref.at[k, :, pl.ds(0, width)], sems.at[1, k]
            )
        )
        for m in range(nm):
            top = pl.multiple_of(share * rows, 16)
            copies.append(
                pltpu.make_async_copy(
                    w_out_ref.at[pl.ds(top, rows), cut], w2_ref.at[k * nm + m], sems.at[2 + m, k]
                )
            )
    for c in copies:
        c.start()
    same = lax.broadcasted_iota(jnp.int32, (ids_ref.shape[0],) * 2, 0)
    same = same == lax.broadcasted_iota(jnp.int32, same.shape, 1)
    ids = lax.dot_general(
        ids_ref[...].astype(F32).astype(BF16),
        jnp.where(same, 1.0, 0.0).astype(BF16),
        (((0,), (0,)), ((), ())),
        preferred_element_type=F32,
    )
    lane = lax.broadcasted_iota(jnp.int32, (toks, LANES), 1)
    block = jnp.where(lane < ny * nz, (lane % ny) * nz + lane // ny, -1).astype(F32)
    named = jnp.zeros((toks, LANES), F32)
    for k in range(ids.shape[1]):
        named = jnp.where(ids[:, k : k + 1] == block, 1.0, named)
    row = lax.broadcasted_iota(jnp.int32, (toks, toks), 0)
    col = lax.broadcasted_iota(jnp.int32, (toks, toks), 1)
    before = jnp.where(col < row, 1.0, 0.0).astype(BF16)
    position = jnp.dot(before, named.astype(BF16), preferred_element_type=F32)
    slots = jnp.where(named > 0.0, position, -1.0).astype(BF16)
    base = width + LANES
    for k in range(ny):
        out_ref[k, :, width:base] = slots
    for k in range(ny):
        copies[k].wait()
        for g in range(part // toks):
            out_ref[k, :, base + g * LANES : base + (g + 1) * LANES] = in_rows[
                k, g * toks : (g + 1) * toks, :
            ]
    for c in copies[ny:]:
        c.wait()


def pack(tokens, ids, w_in, w_out, dims):
    ny, _, nm, nx, nc = dims
    toks, model = tokens.shape
    width = model // ny
    rows = w_out.shape[0] // (nx * nc)
    return pl.pallas_call(
        functools.partial(pack_kernel, dims=dims),
        out_shape=(
            jax.ShapeDtypeStruct((ny, toks, 2 * width + LANES), BF16),
            jax.ShapeDtypeStruct((ny * nm, rows, width), BF16),
        ),
        in_specs=[ANY, VMEM, ANY, ANY],
        out_specs=(VMEM, VMEM),
        scratch_shapes=[
            pltpu.VMEM((ny, width // (nx * nc), LANES), BF16),
            pltpu.SemaphoreType.DMA((2 + nm, ny)),
        ],
        name="pack",
    )(tokens, ids, w_in, w_out)


def tile_kernel(mine_ref, other_ref, wide_ref, *, dims):
    ny, _, _, nx, nc = dims
    x, c = lax.axis_index("x"), lax.axis_index("c")
    rows, width = mine_ref.shape[2:]
    groups = width // LANES
    for source, core in ((mine_ref, c), (other_ref, nc - 1 - c)):
        for s in range(nx):
            share = (x + nx - s) % nx * nc + core
            for g in range(groups):
                top = pl.multiple_of((share * groups + g) * rows, 16)
                for k in range(ny):
                    wide_ref[pl.ds(top, rows), k * LANES : (k + 1) * LANES] = source[
                        s, k, :, g * LANES : (g + 1) * LANES
                    ]


def tile(mine, other, dims):
    ny, width = dims[0], mine.shape[3]
    return pl.pallas_call(
        functools.partial(tile_kernel, dims=dims),
        out_shape=jax.ShapeDtypeStruct((width, ny * LANES), BF16),
        in_specs=[VMEM, VMEM],
        out_specs=VMEM,
        name="tile",
    )(mine, other)


def first_kernel(x_ref, wide_ref, out_ref, wide, bands, wide_sem, sems, *, dims, toks):
    ny, nn, nm, _, _ = dims
    width = wide_ref.shape[0]
    weight = pltpu.make_async_copy(wide_ref, wide, wide_sem)
    weight.start()
    band = ny * toks
    order = [a * nm + m for m in range(nm) for a in range(nn)]
    copies = {
        r: pltpu.make_async_copy(x_ref.at[pl.ds(r * band, band), :], bands.at[r], sems.at[r])
        for r in order
    }
    for r in order:
        copies[r].start()
    per = CHUNK // toks * CAP
    base = (lax.axis_index("zn") * nm + lax.axis_index("zm")) * ny
    row = lax.broadcasted_iota(jnp.int32, (16, LANES), 0)
    lane = lax.broadcasted_iota(jnp.int32, (16, LANES), 1)
    pick = jnp.where((lane == base + row) & (row < ny), 1.0, 0.0).astype(BF16)
    col = lax.broadcasted_iota(jnp.int32, (16, CHUNK), 1)
    slot = lax.broadcasted_iota(jnp.int32, (per, CHUNK), 0).astype(F32)
    first = (col // toks * CAP).astype(F32)
    step = CHUNK // band
    weight.wait()
    for m in range(len(order) // step):
        used = order[m * step : (m + 1) * step]
        for r in used:
            copies[r].wait()
        x = jnp.concatenate([bands[r] for r in used], axis=0)
        h = jnp.dot(x[:, 0:width], wide[...], preferred_element_type=F32).astype(BF16)
        at = lax.dot_general(
            pick, x[:, width : width + LANES], (((1,), (1,)), ((), ())), preferred_element_type=F32
        )
        at = jnp.where(at >= 0.0, at + first, -1.0)
        for j in range(ny):
            s = jnp.where(slot == at[j : j + 1, :], 1.0, 0.0).astype(BF16)
            rows_j = jnp.dot(s, h[:, j * LANES : (j + 1) * LANES], preferred_element_type=F32)
            out_ref[j, m * per : (m + 1) * per, :] = rows_j.astype(BF16)


def first_product(x, wide, dims, toks):
    ny, nn, nm, _, _ = dims
    slots = x.shape[0] // toks * CAP
    return pl.pallas_call(
        functools.partial(first_kernel, dims=dims, toks=toks),
        out_shape=jax.ShapeDtypeStruct((ny, slots, LANES), BF16),
        in_specs=[ANY, ANY],
        out_specs=VMEM,
        scratch_shapes=[
            pltpu.VMEM(wide.shape, BF16),
            pltpu.VMEM((nn * nm, ny * toks, x.shape[1]), BF16),
            pltpu.SemaphoreType.DMA,
            pltpu.SemaphoreType.DMA((nn * nm,)),
        ],
        name="first_product",
    )(x, wide)


def activate_kernel(part_ref, bias_ref, out_ref, *, dims):
    ny, _, nm, _, _ = dims
    rows = out_ref.shape[1]
    for m in range(nm):
        total = part_ref[0, m * rows : (m + 1) * rows, :].astype(F32)
        for k in range(1, ny):
            total = total + part_ref[k, m * rows : (m + 1) * rows, :].astype(F32)
        h = jnp.maximum(total + bias_ref[...], 0.0).astype(BF16)
        for k in range(ny):
            out_ref[k * nm + m] = h


def activate(part, bias, dims):
    ny, _, nm, _, _ = dims
    return pl.pallas_call(
        functools.partial(activate_kernel, dims=dims),
        out_shape=jax.ShapeDtypeStruct((ny * nm, part.shape[1] // nm, LANES), BF16),
        in_specs=[VMEM, VMEM],
        out_specs=VMEM,
        name="activate",
    )(part, bias)


def second_kernel(h_ref, x_ref, w_ref, out_ref, tall, spread, places, sems, place_sems, *, dims, toks):
    ny, nn, nm, _, _ = dims
    zn, zm = lax.axis_index("zn"), lax.axis_index("zm")
    blocks, nt, rows, width = tall.shape
    band = ny * toks
    marks = []
    for a in range(nn):
        top = pl.multiple_of((a * nm + zm) * band, band)
        marks.append(
            pltpu.make_async_copy(
                x_ref.at[pl.ds(top, band), pl.ds(width, LANES)], places.at[a], place_sems.at[a]
            )
        )
    copies = [
        pltpu.make_async_copy(w_ref.at[:, b], tall.at[b], sems.at[b]) for b in range(blocks)
    ]
    for c in marks + copies:
        c.start()
    per = CHUNK // toks * CAP
    row = lax.broadcasted_iota(jnp.int32, (16, LANES), 0)
    lane = lax.broadcasted_iota(jnp.int32, (16, LANES), 1)
    pick = lane == (zn * nm + row % nm) * ny + row // nm
    pick = jnp.where(pick & (row < blocks), 1.0, 0.0).astype(BF16)
    row = lax.broadcasted_iota(jnp.int32, (CHUNK, 16), 0)
    slot = lax.broadcasted_iota(jnp.int32, (CHUNK, per), 1).astype(F32)
    first = (row // toks * CAP).astype(F32)
    step = CHUNK // band
    for c in marks:
        c.wait()
    for m in range(nn // step):
        at = lax.dot_general(
            jnp.concatenate([places[m * step + i] for i in range(step)], axis=0),
            pick,
            (((1,), (1,)), ((), ())),
            preferred_element_type=F32,
        )
        at = jnp.where(at >= 0.0, at + first, -1.0)
        for b in range(blocks):
            s = jnp.where(slot == at[:, b : b + 1], 1.0, 0.0).astype(BF16)
            full = jnp.dot(s, h_ref[b, m * per : (m + 1) * per, :], preferred_element_type=F32)
            spread[m * CHUNK : (m + 1) * CHUNK, b * LANES : (b + 1) * LANES] = full.astype(BF16)
    for c in copies:
        c.wait()
    devices = CHUNK // toks
    for m in range(nn // step):
        out = jnp.dot(
            spread[m * CHUNK : (m + 1) * CHUNK, :],
            tall[...].reshape(blocks * nt * rows, width),
            preferred_element_type=F32,
        )
        out_ref[m * devices : (m + 1) * devices] = out.astype(BF16).reshape(devices, toks, width)


def second_product(h, x, w, dims, toks):
    ny, nn, nm, nx, nc = dims
    rows, width = w.shape[2:]
    return pl.pallas_call(
        functools.partial(second_kernel, dims=dims, toks=toks),
        out_shape=jax.ShapeDtypeStruct((ny * nn, toks, width), BF16),
        in_specs=[VMEM, ANY, ANY],
        out_specs=VMEM,
        scratch_shapes=[
            pltpu.VMEM((ny * nm, nx * nc, rows, width), BF16),
            pltpu.VMEM((ny * nn * toks, ny * nm * LANES), BF16),
            pltpu.VMEM((nn, ny * toks, LANES), BF16),
            pltpu.SemaphoreType.DMA((ny * nm,)),
            pltpu.SemaphoreType.DMA((nn,)),
        ],
        name="second_product",
    )(h, x, w)


def combine_kernel(y_ref, out_ref, *, ny):
    width = y_ref.shape[2]
    for k in range(ny):
        total = y_ref[k].astype(F32)
        for other in range(ny + k, y_ref.shape[0], ny):
            total = total + y_ref[other].astype(F32)
        out_ref[:, k * width : (k + 1) * width] = total.astype(BF16)


def combine(y, ny):
    return pl.pallas_call(
        functools.partial(combine_kernel, ny=ny),
        out_shape=jax.ShapeDtypeStruct((y.shape[1], y.shape[2] * ny), BF16),
        in_specs=[VMEM],
        out_specs=VMEM,
        name="combine",
    )(y)


def exchange(value, axes):
    return lax.all_to_all(value, axes, split_axis=0, concat_axis=0, tiled=True)


def body(tokens, block_ids, w_in, bias_in, w_out):
    dims = sizes()
    ny, _, _, nx, nc = dims
    toks = tokens.shape[0]
    width = tokens.shape[1] // ny

    payload, w2 = pack(tokens, block_ids.T, w_in, w_out, dims)
    got = exchange(payload, "y")
    x = lax.all_gather(
        got[:, :, : width + LANES].reshape(ny * toks, width + LANES), ("zn", "zm"), axis=0, tiled=True
    )
    w1 = got[:, :, width + LANES :]
    w2, w1 = lax.optimization_barrier((w2, w1))
    w2 = exchange(w2, ("y", "zm"))
    mine = [w1]
    for s in range(1, nx):
        mine.append(lax.ppermute(w1, "x", [(i, (i + s) % nx) for i in range(nx)]))
    mine = jnp.stack(mine)
    other = lax.ppermute(mine, "c", [(i, nc - 1 - i) for i in range(nc)])
    wide = tile(near(mine), near(other), dims)
    x, wide, w2 = lax.optimization_barrier((x, wide, w2))
    w2 = lax.all_gather(w2[None], ("x", "c"), axis=0, tiled=True)

    h = exchange(first_product(x, wide, dims, toks), "y")
    h = exchange(activate(near(h), bias_in[None, :], dims), ("y", "zm"))
    y = exchange(second_product(near(h), x, w2, dims, toks), ("zn", "y"))
    return combine(near(y), ny)


def solution(mesh):
    side = math.isqrt(mesh.shape["blk"])
    cores, pair = 2, 2
    fine = Mesh(
        mesh.devices.reshape(side, side // pair, pair, mesh.shape["tok"] // cores, cores),
        ("y", "zn", "zm", "x", "c"),
    )
    rows = ("x", "c", "y", "zn", "zm")
    blocks = ("y", "zn", "zm")
    return jax.shard_map(
        body,
        mesh=fine,
        in_specs=(P(rows, None), P(rows, None), P(None, blocks), P(blocks), P(blocks, None)),
        out_specs=P(rows, None),
        check_vma=False,
    )
```

time: 204 us -> 200 us (0.980)
  the two profiles are of different devices: /device:TPU:2 before, /device:TPU:8 now
where the time goes in v4:
time: 200 us; the launch traced here: 199 us
  blocking collectives  113 us (56%)
  waiting for transfers between devices  29.4 us (15%)
  Pallas kernels  23.3 us (12%)
  starting transfers between devices  19.4 us (10%)
  between operations  13.5 us (7%)
    all_to_all x4, blocking collectives, exchange(): return lax.all_to_all(value, axes, split_axis=0, concat_axis=0, tiled=True)  113 us
    all_to_all x1, waiting for transfers between devices, exchange(): return lax.all_to_all(value, axes, split_axis=0, concat_axis=0, tiled=True)  14.3 us
    ppermute x3, waiting for transfers between devices, body(): mine.append(lax.ppermute(w1, 'x', [(i, (i + s) % nx) for i in range(nx)]))  10.3 us
    ppermute x3, starting transfers between devices, body(): mine.append(lax.ppermute(w1, 'x', [(i, (i + s) % nx) for i in range(nx)]))  10.2 us
    pallas_call x1, Pallas kernels, second_product(): pl.pallas_call(functools.partial(second_kernel, dims=dims, toks=toks), ou...  8 us
    pallas_call x1, Pallas kernels, first_product(): pl.pallas_call(functools.partial(first_kernel, dims=dims, toks=toks), out...  7.59 us
    all_to_all x1, starting transfers between devices, exchange(): return lax.all_to_all(value, axes, split_axis=0, concat_axis=0, tiled=True)  7.25 us
    all_gather x1, waiting for transfers between devices, body(): lax.all_gather(got[:, :, :width + LANES].reshape(ny * toks, width + LANES...  4.71 us
  transfers between devices with their start and end apart: 7, of which 5 were waited for; matrix products, arithmetic and copies ran while one was open for 0% of the time, Pallas kernels for 6%

profile of v4, /device:TPU:8, one launch (start us, length us, event | category | flops | bytes accessed | tf_op | source)
XLA Modules:
  0.0 199.1 jit_solution(617647514018642615)
XLA Ops:
  6.5 0.0 all-gather.4.cloned.1.call-start
  6.5 3.2 %pack.1 = (bf16[8,16,2432]{2,1,0:T(8,128)(2,1)}, bf16[16,16,1152]{2,1,0:T(8,128)(2,1)}) custom-call(bf16[16,9216]{1,0:T(8,128)(2,1)} %tokens_ref.1, s32[8,16]{1,0:T(8,128)} %bitcast.14, bf16[9216,128]{1,0:T(8,128)(2,1)} %w_in_ref.1, bf16[128,9216]{1,0:T(8,128)(2,1)} %w_out_ref.1), custom_call_target="tpu_custom_call" | custom-call | tf_op jit(solution)/shard_map/pack/pallas_call | solution.py:96
  9.8 25.7 %all_to_all.25 = bf16[8,16,2432]{2,1,0:T(8,128)(2,1)S(1)} all-to-all(bf16[8,16,2432]{2,1,0:T(8,128)(2,1)} %get-tuple-element.12), channel_id=1, replica_groups=mesh['y'=8,'zn'=4,'zm'=2,'x'=4,'c'=2] {'y'}, dimensions={0} | all-to-all | bytes 1245184 | tf_op jit(solution)/shard_map/all_to_all | solution.py:311
  35.5 0.7 slice.8
  36.2 0.0 all-gather.4.cloned.1.call-update
  36.3 4.7 %collective-permute-start.2 = (bf16[8,16,1152]{2,1,0:T(8,128)(2,1)S(1)}, bf16[8,16,1152]{2,1,0:T(8,128)(2,1)S(1)}, u32[]{:S(2)}, u32[]{:S(2)}) collective-permute-start(bf16[8,16,1152]{2,1,0:T(8,128)(2,1)S(1)} %slice.9), channel_id=1, source_target_pairs={{0,6},{2,0},{4,2},{6,4},{1,7},{3,1},{5,3},{7,5},{8,14},{10,8},{12,... | collective-permute-start | bytes 884744 | tf_op jit(solution)/shard_map/ppermute | solution.py:330
  41.0 2.7 %collective-permute-start.1 = (bf16[8,16,1152]{2,1,0:T(8,128)(2,1)S(1)}, bf16[8,16,1152]{2,1,0:T(8,128)(2,1)S(1)}, u32[]{:S(2)}, u32[]{:S(2)}) collective-permute-start(bf16[8,16,1152]{2,1,0:T(8,128)(2,1)S(1)} %slice.9), channel_id=1, source_target_pairs={{0,4},{2,6},{4,0},{6,2},{1,5},{3,7},{5,1},{7,3},{8,12},{10,14},{12... | collective-permute-start | bytes 884744 | tf_op jit(solution)/shard_map/ppermute | solution.py:330
  43.7 2.8 %collective-permute-start = (bf16[8,16,1152]{2,1,0:T(8,128)(2,1)S(1)}, bf16[8,16,1152]{2,1,0:T(8,128)(2,1)S(1)}, u32[]{:S(2)}, u32[]{:S(2)}) collective-permute-start(bf16[8,16,1152]{2,1,0:T(8,128)(2,1)S(1)} %slice.9), channel_id=1, source_target_pairs={{0,2},{2,4},{4,6},{6,0},{1,3},{3,5},{5,7},{7,1},{8,10},{10,12},{12... | collective-permute-start | bytes 884744 | tf_op jit(solution)/shard_map/ppermute | solution.py:330
  46.5 4.7 %collective-permute-done.2 = bf16[8,16,1152]{2,1,0:T(8,128)(2,1)S(1)} collective-permute-done((bf16[8,16,1152]{2,1,0:T(8,128)(2,1)S(1)}, bf16[8,16,1152]{2,1,0:T(8,128)(2,1)S(1)}, u32[]{:S(2)}, u32[]{:S(2)}) %collective-permute-start.2) | collective-permute-done | bytes 294944 | tf_op jit(solution)/shard_map/ppermute | solution.py:330
  51.2 2.4 %collective-permute-done.1 = bf16[8,16,1152]{2,1,0:T(8,128)(2,1)S(1)} collective-permute-done((bf16[8,16,1152]{2,1,0:T(8,128)(2,1)S(1)}, bf16[8,16,1152]{2,1,0:T(8,128)(2,1)S(1)}, u32[]{:S(2)}, u32[]{:S(2)}) %collective-permute-start.1) | collective-permute-done | bytes 294944 | tf_op jit(solution)/shard_map/ppermute | solution.py:330
  53.6 3.2 %collective-permute-done = bf16[8,16,1152]{2,1,0:T(8,128)(2,1)S(1)} collective-permute-done((bf16[8,16,1152]{2,1,0:T(8,128)(2,1)S(1)}, bf16[8,16,1152]{2,1,0:T(8,128)(2,1)S(1)}, u32[]{:S(2)}, u32[]{:S(2)}) %collective-permute-start) | collective-permute-done | bytes 294944 | tf_op jit(solution)/shard_map/ppermute | solution.py:330
  56.8 0.2 pad_maximum_fusion.mine_ref
  57.0 1.9 collective-permute-start.3
  58.9 7.2 %all-to-all-start.1 = ((bf16[16,16,1152]{2,1,0:T(8,128)(2,1)}), bf16[16,16,1152]{2,1,0:T(8,128)(2,1)S(1)}, u32[]{:S(2)}, u32[]{:S(2)}) async-start(bf16[16,16,1152]{2,1,0:T(8,128)(2,1)} %get-tuple-element.15), calls=%async_computation.1 | async-start | bytes 1179648 | tf_op jit(solution)/shard_map/all_to_all | solution.py:311
  66.1 0.0 all-gather.6.cloned.1.call-start
  66.2 0.0 collective-permute-done.3.other_ref
  66.2 2.0 tile.1.wide_ref
  68.2 14.3 %all-to-all-done.1 = bf16[16,16,1152]{2,1,0:T(8,128)(2,1)S(1)} async-done(((bf16[16,16,1152]{2,1,0:T(8,128)(2,1)}), bf16[16,16,1152]{2,1,0:T(8,128)(2,1)S(1)}, u32[]{:S(2)}, u32[]{:S(2)}) %all-to-all-start.1) | async-done | bytes 589856 | tf_op jit(solution)/shard_map/all_to_all | solution.py:311
  82.5 0.0 copy-start
  82.5 4.7 %all-gather.4.cloned.1.call-done.x_ref = bf16[1024,1280]{1,0:T(8,128)(2,1)} async-done(((bf16[128,1280]{1,0:T(8,128)(2,1)}), bf16[1024,1280]{1,0:T(8,128)(2,1)}) %all-gather.4.cloned.1.call-update) | async-done | bytes 2621456 | tf_op jit(solution)/shard_map/all_gather | solution.py:322
  87.2 0.0 copy-done
  87.2 0.0 all-gather.6.cloned.1.call-update
  87.2 7.6 %first_product.1 = bf16[8,320,128]{2,1,0:T(8,128)(2,1)} custom-call(bf16[1024,1280]{1,0:T(8,128)(2,1)} %all-gather.4.cloned.1.call-done.x_ref, bf16[1152,1024]{1,0:T(8,128)(2,1)} %tile.1.wide_ref), custom_call_target="tpu_custom_call" | custom-call | tf_op jit(solution)/shard_map/first_product/pallas_call | solution.py:181
  94.8 24.5 %all_to_all.26.part_ref = bf16[8,320,128]{2,1,0:T(8,128)(2,1)S(1)} all-to-all(bf16[8,320,128]{2,1,0:T(8,128)(2,1)} %first_product.1), channel_id=1, replica_groups=mesh['y'=8,'zn'=4,'zm'=2,'x'=4,'c'=2] {'y'}, dimensions={0} | all-to-all | bytes 1310720 | tf_op jit(solution)/shard_map/all_to_all | solution.py:311
  119.3 1.6 activate.1
  120.9 21.5 %all_to_all.27.h_ref = bf16[16,160,128]{2,1,0:T(8,128)(2,1)S(1)} all-to-all(bf16[16,160,128]{2,1,0:T(8,128)(2,1)} %activate.1), channel_id=1, replica_groups=mesh['y'=8,'zn'=4,'zm'=2,'x'=4,'c'=2] {'y','zm'}, dimensions={0} | all-to-all | bytes 1310720 | tf_op jit(solution)/shard_map/all_to_all | solution.py:311
  142.5 0.0 all-gather.6.cloned.1.call-done
  142.5 8.0 %second_product.1 = bf16[32,16,1152]{2,1,0:T(8,128)(2,1)} custom-call(bf16[16,160,128]{2,1,0:T(8,128)(2,1)S(1)} %all_to_all.27.h_ref, bf16[1024,1280]{1,0:T(8,128)(2,1)} %all-gather.4.cloned.1.call-done.x_ref, bf16[8,16,16,1152]{3,2,1,0:T(8,128)(2,1)} %bitcast.8), custom_call_target="tpu_custom_call" | custom-call | tf_op jit(solution)/shard_map/second_product/pallas_call | solution.py:275
  150.5 41.0 %all_to_all.28.y_ref = bf16[32,16,1152]{2,1,0:T(8,128)(2,1)S(1)} all-to-all(bf16[32,16,1152]{2,1,0:T(8,128)(2,1)} %second_product.1), channel_id=1, replica_groups=mesh['y'=8,'zn'=4,'zm'=2,'x'=4,'c'=2] {'zn','y'}, dimensions={0} | all-to-all | bytes 2359296 | tf_op jit(solution)/shard_map/all_to_all | solution.py:311
  191.4 0.9 combine.1
  (1 shorter events, 0.0 us)
Async XLA Ops:
  6.5 80.7 %all-gather.4.cloned.1.call-start = ((), (), s32[]{:S(2)}) async-start(), calls=%async_computation.5 | async-start | bytes 2949120 | tf_op jit(solution)/shard_map/all_gather | solution.py:322
  36.3 14.9 %collective-permute-start.2 = (bf16[8,16,1152]{2,1,0:T(8,128)(2,1)S(1)}, bf16[8,16,1152]{2,1,0:T(8,128)(2,1)S(1)}, u32[]{:S(2)}, u32[]{:S(2)}) collective-permute-start(bf16[8,16,1152]{2,1,0:T(8,128)(2,1)S(1)} %slice.9), channel_id=1, source_target_pairs={{0,6},{2,0},{4,2},{6,4},{1,7},{3,1},{5,3},{7,5},{8,14},{10,8},{12,... | collective-permute-start | bytes 884744 | tf_op jit(solution)/shard_map/ppermute | solution.py:330
  41.0 12.7 %collective-permute-start.1 = (bf16[8,16,1152]{2,1,0:T(8,128)(2,1)S(1)}, bf16[8,16,1152]{2,1,0:T(8,128)(2,1)S(1)}, u32[]{:S(2)}, u32[]{:S(2)}) collective-permute-start(bf16[8,16,1152]{2,1,0:T(8,128)(2,1)S(1)} %slice.9), channel_id=1, source_target_pairs={{0,4},{2,6},{4,0},{6,2},{1,5},{3,7},{5,1},{7,3},{8,12},{10,14},{12... | collective-permute-start | bytes 884744 | tf_op jit(solution)/shard_map/ppermute | solution.py:330
  43.7 13.1 %collective-permute-start = (bf16[8,16,1152]{2,1,0:T(8,128)(2,1)S(1)}, bf16[8,16,1152]{2,1,0:T(8,128)(2,1)S(1)}, u32[]{:S(2)}, u32[]{:S(2)}) collective-permute-start(bf16[8,16,1152]{2,1,0:T(8,128)(2,1)S(1)} %slice.9), channel_id=1, source_target_pairs={{0,2},{2,4},{4,6},{6,0},{1,3},{3,5},{5,7},{7,1},{8,10},{10,12},{12... | collective-permute-start | bytes 884744 | tf_op jit(solution)/shard_map/ppermute | solution.py:330
  57.0 9.2 %collective-permute-start.3 = (bf16[4,8,16,1152]{3,2,1,0:T(8,128)(2,1)S(1)}, bf16[4,8,16,1152]{3,2,1,0:T(8,128)(2,1)S(1)}, u32[]{:S(2)}, u32[]{:S(2)}) collective-permute-start(bf16[4,8,16,1152]{3,2,1,0:T(8,128)(2,1)S(1)} %pad_maximum_fusion.mine_ref), channel_id=1, source_target_pairs={{0,1},{1,0},{2,3},{3,2},{4,5},{5,4},{6,7},{7,6},{8,9},{9,8},{10,11... | collective-permute-start | bytes 3538952 | tf_op jit(solution)/shard_map/ppermute | solution.py:332
  58.9 23.6 %all-to-all-start.1 = ((bf16[16,16,1152]{2,1,0:T(8,128)(2,1)}), bf16[16,16,1152]{2,1,0:T(8,128)(2,1)S(1)}, u32[]{:S(2)}, u32[]{:S(2)}) async-start(bf16[16,16,1152]{2,1,0:T(8,128)(2,1)} %get-tuple-element.15), calls=%async_computation.1 | async-start | bytes 1179648 | tf_op jit(solution)/shard_map/all_to_all | solution.py:311
  66.1 76.3 %all-gather.6.cloned.1.call-start = ((), (), s32[]{:S(2)}) async-start(), calls=%async_computation.6 | async-start | bytes 5308416 | tf_op jit(solution)/shard_map/all_gather | solution.py:335
  82.5 4.7 %copy-start = (bf16[16,16,1152]{2,1,0:T(8,128)(2,1)}, bf16[16,16,1152]{2,1,0:T(8,128)(2,1)S(1)}, u32[]{:S(2)}) copy-start(bf16[16,16,1152]{2,1,0:T(8,128)(2,1)S(1)} %all-to-all-done.1) | copy-start | bytes 1769476
Sparse Core Ops, SparseCore 0:
  36.4 50.7 all-gather.3
  89.3 38.2 all-gather.5

commit v5 on v4

--- a/solution.py
+++ b/solution.py
@@ -9,18 +9,23 @@
 from jax.sharding import Mesh
 from jax.sharding import PartitionSpec as P
 
+
 CAP = 5
 LANES = 128
 CHUNK = 256
 BF16 = jnp.bfloat16
 F32 = jnp.float32
-ANY = pl.BlockSpec(memory_space=pl.ANY)
+HBM = pl.BlockSpec(memory_space=pltpu.HBM)
 VMEM = pl.BlockSpec(memory_space=pltpu.VMEM)
 
 
 def sizes():
     ny, nn, nm = lax.axis_size("y"), lax.axis_size("zn"), lax.axis_size("zm")
     return ny, nn, nm, lax.axis_size("x"), lax.axis_size("c")
+
+
+def room(mebibytes):
+    return pltpu.CompilerParams(vmem_limit_bytes=mebibytes << 20)
 
 
 def near(value):
@@ -96,10 +101,10 @@
     return pl.pallas_call(
         functools.partial(pack_kernel, dims=dims),
         out_shape=(
-            jax.ShapeDtypeStruct((ny, toks, 2 * width + LANES), BF16),
+            pltpu.VMEM((ny, toks, 2 * width + LANES), BF16),
             jax.ShapeDtypeStruct((ny * nm, rows, width), BF16),
         ),
-        in_specs=[ANY, VMEM, ANY, ANY],
+        in_specs=[HBM, VMEM, HBM, HBM],
         out_specs=(VMEM, VMEM),
         scratch_shapes=[
             pltpu.VMEM((ny, width // (nx * nc), LANES), BF16),
@@ -129,18 +134,17 @@
     ny, width = dims[0], mine.shape[3]
     return pl.pallas_call(
         functools.partial(tile_kernel, dims=dims),
-        out_shape=jax.ShapeDtypeStruct((width, ny * LANES), BF16),
+        out_shape=pltpu.VMEM((width, ny * LANES), BF16),
         in_specs=[VMEM, VMEM],
         out_specs=VMEM,
+        compiler_params=room(56),
         name="tile",
     )(mine, other)
 
 
-def first_kernel(x_ref, wide_ref, out_ref, wide, bands, wide_sem, sems, *, dims, toks):
+def first_kernel(x_ref, wide_ref, out_ref, bands, sems, *, dims, toks):
     ny, nn, nm, _, _ = dims
     width = wide_ref.shape[0]
-    weight = pltpu.make_async_copy(wide_ref, wide, wide_sem)
-    weight.start()
     band = ny * toks
     order = [a * nm + m for m in range(nm) for a in range(nn)]
     copies = {
@@ -158,13 +162,12 @@
     slot = lax.broadcasted_iota(jnp.int32, (per, CHUNK), 0).astype(F32)
     first = (col // toks * CAP).astype(F32)
     step = CHUNK // band
-    weight.wait()
     for m in range(len(order) // step):
         used = order[m * step : (m + 1) * step]
         for r in used:
             copies[r].wait()
         x = jnp.concatenate([bands[r] for r in used], axis=0)
-        h = jnp.dot(x[:, 0:width], wide[...], preferred_element_type=F32).astype(BF16)
+        h = jnp.dot(x[:, 0:width], wide_ref[...], preferred_element_type=F32).astype(BF16)
         at = lax.dot_general(
             pick, x[:, width : width + LANES], (((1,), (1,)), ((), ())), preferred_element_type=F32
         )
@@ -180,13 +183,11 @@
     slots = x.shape[0] // toks * CAP
     return pl.pallas_call(
         functools.partial(first_kernel, dims=dims, toks=toks),
-        out_shape=jax.ShapeDtypeStruct((ny, slots, LANES), BF16),
-        in_specs=[ANY, ANY],
+        out_shape=pltpu.VMEM((ny, slots, LANES), BF16),
+        in_specs=[HBM, VMEM],
         out_specs=VMEM,
         scratch_shapes=[
-            pltpu.VMEM(wide.shape, BF16),
             pltpu.VMEM((nn * nm, ny * toks, x.shape[1]), BF16),
-            pltpu.SemaphoreType.DMA,
             pltpu.SemaphoreType.DMA((nn * nm,)),
         ],
         name="first_product",
@@ -209,83 +210,107 @@
     ny, _, nm, _, _ = dims
     return pl.pallas_call(
         functools.partial(activate_kernel, dims=dims),
-        out_shape=jax.ShapeDtypeStruct((ny * nm, part.shape[1] // nm, LANES), BF16),
+        out_shape=pltpu.VMEM((ny * nm, part.shape[1] // nm, LANES), BF16),
         in_specs=[VMEM, VMEM],
         out_specs=VMEM,
         name="activate",
     )(part, bias)
 
 
-def second_kernel(h_ref, x_ref, w_ref, out_ref, tall, spread, places, sems, place_sems, *, dims, toks):
+def place_kernel(x_ref, place_ref, marks, sems, *, dims, toks):
     ny, nn, nm, _, _ = dims
     zn, zm = lax.axis_index("zn"), lax.axis_index("zm")
-    blocks, nt, rows, width = tall.shape
+    width = x_ref.shape[1] - LANES
+    blocks = ny * nm
     band = ny * toks
-    marks = []
+    copies = []
     for a in range(nn):
         top = pl.multiple_of((a * nm + zm) * band, band)
-        marks.append(
+        copies.append(
             pltpu.make_async_copy(
-                x_ref.at[pl.ds(top, band), pl.ds(width, LANES)], places.at[a], place_sems.at[a]
+                x_ref.at[pl.ds(top, band), pl.ds(width, LANES)], marks.at[a], sems.at[a]
             )
         )
+    for c in copies:
+        c.start()
+    per = CHUNK // toks * CAP
+    row = lax.broadcasted_iota(jnp.int32, (blocks, LANES), 0)
+    lane = lax.broadcasted_iota(jnp.int32, (blocks, LANES), 1)
+    pick = jnp.where(lane == (zn * nm + row % nm) * ny + row // nm, 1.0, 0.0).astype(BF16)
+    row = lax.broadcasted_iota(jnp.int32, (CHUNK, blocks), 0)
+    slot = lax.broadcasted_iota(jnp.int32, (CHUNK, per), 1).astype(F32)
+    first = (row // toks * CAP).astype(F32)
+    step = CHUNK // band
+    for c in copies:
+        c.wait()
+    for m in range(nn // step):
+        at = lax.dot_general(
+            jnp.concatenate([marks[m * step + i] for i in range(step)], axis=0),
+            pick,
+            (((1,), (1,)), ((), ())),
+            preferred_element_type=F32,
+        )
+        at = jnp.where(at >= 0.0, at + first, -1.0)
+        for b in range(blocks):
+            place_ref[m, b] = jnp.where(slot == at[:, b : b + 1], 1.0, 0.0).astype(BF16)
+
+
+def place(x, dims, toks):
+    ny, nn, nm, _, _ = dims
+    band = ny * toks
+    return pl.pallas_call(
+        functools.partial(place_kernel, dims=dims, toks=toks),
+        out_shape=pltpu.VMEM((nn * band // CHUNK, ny * nm, CHUNK, CHUNK // toks * CAP), BF16),
+        in_specs=[HBM],
+        out_specs=VMEM,
+        scratch_shapes=[
+            pltpu.VMEM((nn, band, LANES), BF16),
+            pltpu.SemaphoreType.DMA((nn,)),
+        ],
+        name="place",
+    )(x)
+
+
+def second_kernel(h_ref, place_ref, w_ref, out_ref, tall, spread, sems, *, toks):
+    chunks, blocks, _, per = place_ref.shape
+    width = w_ref.shape[3]
+    devices = CHUNK // toks
     copies = [
         pltpu.make_async_copy(w_ref.at[:, b], tall.at[b], sems.at[b]) for b in range(blocks)
     ]
-    for c in marks + copies:
+    for c in copies:
         c.start()
-    per = CHUNK // toks * CAP
-    row = lax.broadcasted_iota(jnp.int32, (16, LANES), 0)
-    lane = lax.broadcasted_iota(jnp.int32, (16, LANES), 1)
-    pick = lane == (zn * nm + row % nm) * ny + row // nm
-    pick = jnp.where(pick & (row < blocks), 1.0, 0.0).astype(BF16)
-    row = lax.broadcasted_iota(jnp.int32, (CHUNK, 16), 0)
-    slot = lax.broadcasted_iota(jnp.int32, (CHUNK, per), 1).astype(F32)
-    first = (row // toks * CAP).astype(F32)
-    step = CHUNK // band
-    for c in marks:
+    for m in range(chunks):
+        for b in range(blocks):
+            full = jnp.dot(
+                place_ref[m, b], h_ref[b, m * per : (m + 1) * per, :], preferred_element_type=F32
+            )
+            spread[m, :, b * LANES : (b + 1) * LANES] = full.astype(BF16)
+    for c in copies:
         c.wait()
-    for m in range(nn // step):
-        at = lax.dot_general(
-            jnp.concatenate([places[m * step + i] for i in range(step)], axis=0),
-            pick,
-            (((1,), (1,)), ((), ())),
-            preferred_element_type=F32,
-        )
-        at = jnp.where(at >= 0.0, at + first, -1.0)
-        for b in range(blocks):
-            s = jnp.where(slot == at[:, b : b + 1], 1.0, 0.0).astype(BF16)
-            full = jnp.dot(s, h_ref[b, m * per : (m + 1) * per, :], preferred_element_type=F32)
-            spread[m * CHUNK : (m + 1) * CHUNK, b * LANES : (b + 1) * LANES] = full.astype(BF16)
-    for c in copies:
-        c.wait()
-    devices = CHUNK // toks
-    for m in range(nn // step):
+    for m in range(chunks):
         out = jnp.dot(
-            spread[m * CHUNK : (m + 1) * CHUNK, :],
-            tall[...].reshape(blocks * nt * rows, width),
-            preferred_element_type=F32,
+            spread[m], tall[...].reshape(blocks * LANES, width), preferred_element_type=F32
         )
         out_ref[m * devices : (m + 1) * devices] = out.astype(BF16).reshape(devices, toks, width)
 
 
-def second_product(h, x, w, dims, toks):
-    ny, nn, nm, nx, nc = dims
-    rows, width = w.shape[2:]
-    return pl.pallas_call(
-        functools.partial(second_kernel, dims=dims, toks=toks),
-        out_shape=jax.ShapeDtypeStruct((ny * nn, toks, width), BF16),
-        in_specs=[VMEM, ANY, ANY],
+def second_product(h, places, w, toks):
+    chunks, blocks = places.shape[:2]
+    nt, _, rows, width = w.shape
+    return pl.pallas_call(
+        functools.partial(second_kernel, toks=toks),
+        out_shape=pltpu.VMEM((chunks * CHUNK // toks, toks, width), BF16),
+        in_specs=[VMEM, VMEM, HBM],
         out_specs=VMEM,
         scratch_shapes=[
-            pltpu.VMEM((ny * nm, nx * nc, rows, width), BF16),
-            pltpu.VMEM((ny * nn * toks, ny * nm * LANES), BF16),
-            pltpu.VMEM((nn, ny * toks, LANES), BF16),
-            pltpu.SemaphoreType.DMA((ny * nm,)),
-            pltpu.SemaphoreType.DMA((nn,)),
+            pltpu.VMEM((blocks, nt, rows, width), BF16),
+            pltpu.VMEM((chunks, CHUNK, blocks * LANES), BF16),
+            pltpu.SemaphoreType.DMA((blocks,)),
         ],
+        compiler_params=room(58),
         name="second_product",
-    )(h, x, w)
+    )(h, places, w)
 
 
 def combine_kernel(y_ref, out_ref, *, ny):
@@ -334,9 +359,11 @@
     x, wide, w2 = lax.optimization_barrier((x, wide, w2))
     w2 = lax.all_gather(w2[None], ("x", "c"), axis=0, tiled=True)
 
-    h = exchange(first_product(x, wide, dims, toks), "y")
-    h = exchange(activate(near(h), bias_in[None, :], dims), ("y", "zm"))
-    y = exchange(second_product(near(h), x, w2, dims, toks), ("zn", "y"))
+    h = exchange(first_product(x, near(wide), dims, toks), "y")
+    h = activate(near(h), bias_in[None, :], dims)
+    h = exchange(h, ("y", "zm"))
+    places = place(x, dims, toks)
+    y = exchange(second_product(near(h), near(places), w2, toks), ("zn", "y"))
     return combine(near(y), ny)
 
 

time: 200 us -> 197 us (0.985)
  blocking collectives: 113 us -> 93.9 us
  waiting for transfers between devices: 29.4 us -> 42 us
  starting transfers between devices: 19.4 us -> 24.2 us
  Pallas kernels: 23.3 us -> 19.5 us
  local copies, waits for them, and re-layouts: 0.76 us -> 3.09 us
    all_to_all x4 -> x3, blocking collectives: 113 us -> 93.9 us  [exchange(): return lax.all_to_all(value, axes, split_axis=0, concat_axis=0, tiled=True)]
    all_to_all x1 -> x2, waiting for transfers between devices: 14.3 us -> 27.6 us  [exchange(): return lax.all_to_all(value, axes, split_axis=0, concat_axis=0, tiled=True)]
    all_to_all x1 -> x2, starting transfers between devices: 7.25 us -> 12.1 us  [exchange(): return lax.all_to_all(value, axes, split_axis=0, concat_axis=0, tiled=True)]
    unnamed x2 -> x4, local copies, waits for them, and re-layouts: 0.01 us -> 2.31 us
    pallas_call x1, Pallas kernels: 7.59 us -> 5.45 us  [first_product(): pl.pallas_call(functools.partial(first_kernel, dims=dims, toks=toks), out...]
    pallas_call x4 -> x5, Pallas kernels: 14.8 us -> 13.2 us  [the longest x1 5.87 us: second_product(): pl.pallas_call(functools.partial(second_kernel, toks=toks), out_shape=plt...]
  transfers between devices with their start and end apart: 7 -> 8, of which waited for: 5 -> 6; matrix products, arithmetic and copies ran while one was open for 0% -> 0% of each run, Pallas kernels for 6% -> 5%
where the time goes in v5:
time: 197 us; the launch traced here: 196 us
  blocking collectives  93.9 us (48%)
  waiting for transfers between devices  42 us (21%)
  starting transfers between devices  24.2 us (12%)
  Pallas kernels  19.5 us (10%)
  between operations  13.5 us (7%)
  local copies, waits for them, and re-layouts  3.09 us (2%)
    all_to_all x3, blocking collectives, exchange(): return lax.all_to_all(value, axes, split_axis=0, concat_axis=0, tiled=True)  93.9 us
    all_to_all x2, waiting for transfers between devices, exchange(): return lax.all_to_all(value, axes, split_axis=0, concat_axis=0, tiled=True)  27.6 us
    all_to_all x2, starting transfers between devices, exchange(): return lax.all_to_all(value, axes, split_axis=0, concat_axis=0, tiled=True)  12.1 us
    ppermute x3, waiting for transfers between devices, body(): mine.append(lax.ppermute(w1, 'x', [(i, (i + s) % nx) for i in range(nx)]))  10.3 us
    ppermute x3, starting transfers between devices, body(): mine.append(lax.ppermute(w1, 'x', [(i, (i + s) % nx) for i in range(nx)]))  10.2 us
    pallas_call x1, Pallas kernels, second_product(): pl.pallas_call(functools.partial(second_kernel, toks=toks), out_shape=plt...  5.87 us
    pallas_call x1, Pallas kernels, first_product(): pl.pallas_call(functools.partial(first_kernel, dims=dims, toks=toks), out...  5.45 us
    all_gather x1, waiting for transfers between devices, body(): lax.all_gather(got[:, :, :width + LANES].reshape(ny * toks, width + LANES...  4 us
  transfers between devices with their start and end apart: 8, of which 6 were waited for; matrix products, arithmetic and copies ran while one was open for 0% of the time, Pallas kernels for 5%

profile of v5, /device:TPU:8, one launch (start us, length us, event | category | flops | bytes accessed | tf_op | source)
XLA Modules:
  0.0 196.4 jit_solution(2066694607642057275)
XLA Ops:
  6.5 0.0 all-gather.4.cloned.1.call-start
  6.5 3.0 %pack.1 = (bf16[8,16,2432]{2,1,0:T(8,128)(2,1)S(1)}, bf16[16,16,1152]{2,1,0:T(8,128)(2,1)}) custom-call(bf16[16,9216]{1,0:T(8,128)(2,1)} %tokens_ref.1, s32[8,16]{1,0:T(8,128)} %bitcast.14, bf16[9216,128]{1,0:T(8,128)(2,1)} %w_in_ref.1, bf16[128,9216]{1,0:T(8,128)(2,1)} %w_out_ref.1), custom_call_target="tpu_custom_call" | custom-call | tf_op jit(solution)/shard_map/pack/pallas_call | solution.py:101
  9.6 25.5 %all_to_all.25 = bf16[8,16,2432]{2,1,0:T(8,128)(2,1)S(1)} all-to-all(bf16[8,16,2432]{2,1,0:T(8,128)(2,1)S(1)} %get-tuple-element.12), channel_id=1, replica_groups=mesh['y'=8,'zn'=4,'zm'=2,'x'=4,'c'=2] {'y'}, dimensions={0} | all-to-all | bytes 1245184 | tf_op jit(solution)/shard_map/all_to_all | solution.py:336
  35.1 0.8 slice.8
  35.9 0.0 all-gather.4.cloned.1.call-update
  35.9 4.7 %collective-permute-start.2 = (bf16[8,16,1152]{2,1,0:T(8,128)(2,1)S(1)}, bf16[8,16,1152]{2,1,0:T(8,128)(2,1)S(1)}, u32[]{:S(2)}, u32[]{:S(2)}) collective-permute-start(bf16[8,16,1152]{2,1,0:T(8,128)(2,1)S(1)} %slice.9), channel_id=1, source_target_pairs={{0,6},{2,0},{4,2},{6,4},{1,7},{3,1},{5,3},{7,5},{8,14},{10,8},{12,... | collective-permute-start | bytes 884744 | tf_op jit(solution)/shard_map/ppermute | solution.py:355
  40.6 2.7 %collective-permute-start.1 = (bf16[8,16,1152]{2,1,0:T(8,128)(2,1)S(1)}, bf16[8,16,1152]{2,1,0:T(8,128)(2,1)S(1)}, u32[]{:S(2)}, u32[]{:S(2)}) collective-permute-start(bf16[8,16,1152]{2,1,0:T(8,128)(2,1)S(1)} %slice.9), channel_id=1, source_target_pairs={{0,4},{2,6},{4,0},{6,2},{1,5},{3,7},{5,1},{7,3},{8,12},{10,14},{12... | collective-permute-start | bytes 884744 | tf_op jit(solution)/shard_map/ppermute | solution.py:355
  43.3 2.8 %collective-permute-start = (bf16[8,16,1152]{2,1,0:T(8,128)(2,1)S(1)}, bf16[8,16,1152]{2,1,0:T(8,128)(2,1)S(1)}, u32[]{:S(2)}, u32[]{:S(2)}) collective-permute-start(bf16[8,16,1152]{2,1,0:T(8,128)(2,1)S(1)} %slice.9), channel_id=1, source_target_pairs={{0,2},{2,4},{4,6},{6,0},{1,3},{3,5},{5,7},{7,1},{8,10},{10,12},{12... | collective-permute-start | bytes 884744 | tf_op jit(solution)/shard_map/ppermute | solution.py:355
  46.1 4.7 %collective-permute-done.2 = bf16[8,16,1152]{2,1,0:T(8,128)(2,1)S(1)} collective-permute-done((bf16[8,16,1152]{2,1,0:T(8,128)(2,1)S(1)}, bf16[8,16,1152]{2,1,0:T(8,128)(2,1)S(1)}, u32[]{:S(2)}, u32[]{:S(2)}) %collective-permute-start.2) | collective-permute-done | bytes 294944 | tf_op jit(solution)/shard_map/ppermute | solution.py:355
  50.8 2.4 %collective-permute-done.1 = bf16[8,16,1152]{2,1,0:T(8,128)(2,1)S(1)} collective-permute-done((bf16[8,16,1152]{2,1,0:T(8,128)(2,1)S(1)}, bf16[8,16,1152]{2,1,0:T(8,128)(2,1)S(1)}, u32[]{:S(2)}, u32[]{:S(2)}) %collective-permute-start.1) | collective-permute-done | bytes 294944 | tf_op jit(solution)/shard_map/ppermute | solution.py:355
  53.2 3.2 %collective-permute-done = bf16[8,16,1152]{2,1,0:T(8,128)(2,1)S(1)} collective-permute-done((bf16[8,16,1152]{2,1,0:T(8,128)(2,1)S(1)}, bf16[8,16,1152]{2,1,0:T(8,128)(2,1)S(1)}, u32[]{:S(2)}, u32[]{:S(2)}) %collective-permute-start) | collective-permute-done | bytes 294944 | tf_op jit(solution)/shard_map/ppermute | solution.py:355
  56.4 0.2 pad_maximum_fusion.mine_ref
  56.6 1.9 collective-permute-start.3
  58.5 7.2 %all-to-all-start.1 = ((bf16[16,16,1152]{2,1,0:T(8,128)(2,1)}), bf16[16,16,1152]{2,1,0:T(8,128)(2,1)}, u32[]{:S(2)}, u32[]{:S(2)}) async-start(bf16[16,16,1152]{2,1,0:T(8,128)(2,1)} %get-tuple-element.15), calls=%async_computation.1 | async-start | bytes 1179648 | tf_op jit(solution)/shard_map/all_to_all | solution.py:336
  65.7 0.0 all-gather.6.cloned.1.call-start
  65.8 0.0 collective-permute-done.3.other_ref
  65.8 0.0 copy-start
  65.8 1.0 copy-done
  66.8 1.3 copy-done.1
  68.1 0.5 tile.1.wide_ref
  68.6 14.2 %all-to-all-done.1 = bf16[16,16,1152]{2,1,0:T(8,128)(2,1)} async-done(((bf16[16,16,1152]{2,1,0:T(8,128)(2,1)}), bf16[16,16,1152]{2,1,0:T(8,128)(2,1)}, u32[]{:S(2)}, u32[]{:S(2)}) %all-to-all-start.1) | async-done | bytes 589856 | tf_op jit(solution)/shard_map/all_to_all | solution.py:336
  82.8 4.0 %all-gather.4.cloned.1.call-done.x_ref = bf16[1024,1280]{1,0:T(8,128)(2,1)} async-done(((bf16[128,1280]{1,0:T(8,128)(2,1)}), bf16[1024,1280]{1,0:T(8,128)(2,1)}) %all-gather.4.cloned.1.call-update) | async-done | bytes 2621456 | tf_op jit(solution)/shard_map/all_gather | solution.py:347
  86.8 0.0 all-gather.6.cloned.1.call-update
  86.8 5.5 %first_product.1 = bf16[8,320,128]{2,1,0:T(8,128)(2,1)S(1)} custom-call(bf16[1024,1280]{1,0:T(8,128)(2,1)} %all-gather.4.cloned.1.call-done.x_ref, bf16[1152,1024]{1,0:T(8,128)(2,1)S(1)} %tile.1.wide_ref), custom_call_target="tpu_custom_call" | custom-call | tf_op jit(solution)/shard_map/first_product/pallas_call | solution.py:184
  92.3 24.3 %all_to_all.26.part_ref = bf16[8,320,128]{2,1,0:T(8,128)(2,1)S(1)} all-to-all(bf16[8,320,128]{2,1,0:T(8,128)(2,1)S(1)} %first_product.1), channel_id=1, replica_groups=mesh['y'=8,'zn'=4,'zm'=2,'x'=4,'c'=2] {'y'}, dimensions={0} | all-to-all | bytes 1310720 | tf_op jit(solution)/shard_map/all_to_all | solution.py:336
  116.6 1.6 activate.1
  118.2 4.8 %all-to-all-start.3 = ((bf16[16,160,128]{2,1,0:T(8,128)(2,1)}), bf16[16,160,128]{2,1,0:T(8,128)(2,1)S(1)}, u32[]{:S(2)}, u32[]{:S(2)}) async-start(bf16[16,160,128]{2,1,0:T(8,128)(2,1)} %activate.1), calls=%async_computation.3 | async-start | bytes 1310720 | tf_op jit(solution)/shard_map/all_to_all | solution.py:336
  123.0 2.2 %place.1.place_ref = bf16[2,16,256,80]{3,2,1,0:T(8,128)(2,1)S(1)} custom-call(bf16[1024,1280]{1,0:T(8,128)(2,1)} %all-gather.4.cloned.1.call-done.x_ref), custom_call_target="tpu_custom_call" | custom-call | tf_op jit(solution)/shard_map/place/pallas_call | solution.py:261
  125.3 13.4 %all-to-all-done.3.h_ref = bf16[16,160,128]{2,1,0:T(8,128)(2,1)S(1)} async-done(((bf16[16,160,128]{2,1,0:T(8,128)(2,1)}), bf16[16,160,128]{2,1,0:T(8,128)(2,1)S(1)}, u32[]{:S(2)}, u32[]{:S(2)}) %all-to-all-start.3) | async-done | bytes 655392 | tf_op jit(solution)/shard_map/all_to_all | solution.py:336
  138.7 5.9 %second_product.1 = bf16[32,16,1152]{2,1,0:T(8,128)(2,1)S(1)} custom-call(bf16[16,160,128]{2,1,0:T(8,128)(2,1)S(1)} %all-to-all-done.3.h_ref, bf16[2,16,256,80]{3,2,1,0:T(8,128)(2,1)S(1)} %place.1.place_ref, bf16[8,16,16,1152]{3,2,1,0:T(8,128)(2,1)} %bitcast.8), custom_call_target="tpu_custom_call" | custom-call | tf_op jit(solution)/shard_map/second_product/pallas_call | solution.py:301
  144.6 44.1 %all_to_all.27.y_ref = bf16[32,16,1152]{2,1,0:T(8,128)(2,1)S(1)} all-to-all(bf16[32,16,1152]{2,1,0:T(8,128)(2,1)S(1)} %second_product.1), channel_id=1, replica_groups=mesh['y'=8,'zn'=4,'zm'=2,'x'=4,'c'=2] {'zn','y'}, dimensions={0} | all-to-all | bytes 2359296 | tf_op jit(solution)/shard_map/all_to_all | solution.py:336
  188.7 0.9 combine.1
  (3 shorter events, 0.0 us)
Async XLA Ops:
  6.5 80.3 %all-gather.4.cloned.1.call-start = ((), (), s32[]{:S(2)}) async-start(), calls=%async_computation.5 | async-start | bytes 2949120 | tf_op jit(solution)/shard_map/all_gather | solution.py:347
  35.9 14.9 %collective-permute-start.2 = (bf16[8,16,1152]{2,1,0:T(8,128)(2,1)S(1)}, bf16[8,16,1152]{2,1,0:T(8,128)(2,1)S(1)}, u32[]{:S(2)}, u32[]{:S(2)}) collective-permute-start(bf16[8,16,1152]{2,1,0:T(8,128)(2,1)S(1)} %slice.9), channel_id=1, source_target_pairs={{0,6},{2,0},{4,2},{6,4},{1,7},{3,1},{5,3},{7,5},{8,14},{10,8},{12,... | collective-permute-start | bytes 884744 | tf_op jit(solution)/shard_map/ppermute | solution.py:355
  40.6 12.7 %collective-permute-start.1 = (bf16[8,16,1152]{2,1,0:T(8,128)(2,1)S(1)}, bf16[8,16,1152]{2,1,0:T(8,128)(2,1)S(1)}, u32[]{:S(2)}, u32[]{:S(2)}) collective-permute-start(bf16[8,16,1152]{2,1,0:T(8,128)(2,1)S(1)} %slice.9), channel_id=1, source_target_pairs={{0,4},{2,6},{4,0},{6,2},{1,5},{3,7},{5,1},{7,3},{8,12},{10,14},{12... | collective-permute-start | bytes 884744 | tf_op jit(solution)/shard_map/ppermute | solution.py:355
  43.3 13.1 %collective-permute-start = (bf16[8,16,1152]{2,1,0:T(8,128)(2,1)S(1)}, bf16[8,16,1152]{2,1,0:T(8,128)(2,1)S(1)}, u32[]{:S(2)}, u32[]{:S(2)}) collective-permute-start(bf16[8,16,1152]{2,1,0:T(8,128)(2,1)S(1)} %slice.9), channel_id=1, source_target_pairs={{0,2},{2,4},{4,6},{6,0},{1,3},{3,5},{5,7},{7,1},{8,10},{10,12},{12... | collective-permute-start | bytes 884744 | tf_op jit(solution)/shard_map/ppermute | solution.py:355
  56.6 9.2 %collective-permute-start.3 = (bf16[4,8,16,1152]{3,2,1,0:T(8,128)(2,1)S(1)}, bf16[4,8,16,1152]{3,2,1,0:T(8,128)(2,1)S(1)}, u32[]{:S(2)}, u32[]{:S(2)}) collective-permute-start(bf16[4,8,16,1152]{3,2,1,0:T(8,128)(2,1)S(1)} %pad_maximum_fusion.mine_ref), channel_id=1, source_target_pairs={{0,1},{1,0},{2,3},{3,2},{4,5},{5,4},{6,7},{7,6},{8,9},{9,8},{10,11... | collective-permute-start | bytes 3538952 | tf_op jit(solution)/shard_map/ppermute | solution.py:357
  58.5 24.3 %all-to-all-start.1 = ((bf16[16,16,1152]{2,1,0:T(8,128)(2,1)}), bf16[16,16,1152]{2,1,0:T(8,128)(2,1)}, u32[]{:S(2)}, u32[]{:S(2)}) async-start(bf16[16,16,1152]{2,1,0:T(8,128)(2,1)} %get-tuple-element.15), calls=%async_computation.1 | async-start | bytes 1179648 | tf_op jit(solution)/shard_map/all_to_all | solution.py:336
  65.7 73.0 %all-gather.6.cloned.1.call-start = ((), (), s32[]{:S(2)}) async-start(), calls=%async_computation.6 | async-start | bytes 5308416 | tf_op jit(solution)/shard_map/all_gather | solution.py:360
  65.8 1.0 copy-start
  66.8 1.3 copy-start.1
  118.2 20.5 %all-to-all-start.3 = ((bf16[16,160,128]{2,1,0:T(8,128)(2,1)}), bf16[16,160,128]{2,1,0:T(8,128)(2,1)S(1)}, u32[]{:S(2)}, u32[]{:S(2)}) async-start(bf16[16,160,128]{2,1,0:T(8,128)(2,1)} %activate.1), calls=%async_computation.3 | async-start | bytes 1310720 | tf_op jit(solution)/shard_map/all_to_all | solution.py:336
Sparse Core Ops, SparseCore 0:
  36.0 50.7 all-gather.3
  88.9 38.2 all-gather.5

commit v6 on v5

--- a/solution.py
+++ b/solution.py
@@ -32,14 +32,13 @@
     return pltpu.with_memory_space_constraint(value, pltpu.VMEM)
 
 
-def pack_kernel(tokens_ref, ids_ref, w_in_ref, w_out_ref, out_ref, w2_ref, in_rows, sems, *, dims):
+def pack_kernel(tokens_ref, ids_ref, w_in_ref, out_ref, in_rows, sems, *, dims):
     ny, nn, nm, nx, nc = dims
     nz, nt = nn * nm, nx * nc
     share = lax.axis_index("x") * nc + lax.axis_index("c")
     width = tokens_ref.shape[1] // ny
     part = width // nt
     toks = tokens_ref.shape[0]
-    rows = w_out_ref.shape[0] // nt
     copies = []
     for k in range(ny):
         top = pl.multiple_of(k * width + share * part, 16)
@@ -53,13 +52,6 @@
                 tokens_ref.at[:, cut], out_ref.at[k, :, pl.ds(0, width)], sems.at[1, k]
             )
         )
-        for m in range(nm):
-            top = pl.multiple_of(share * rows, 16)
-            copies.append(
-                pltpu.make_async_copy(
-                    w_out_ref.at[pl.ds(top, rows), cut], w2_ref.at[k * nm + m], sems.at[2 + m, k]
-                )
-            )
     for c in copies:
         c.start()
     same = lax.broadcasted_iota(jnp.int32, (ids_ref.shape[0],) * 2, 0)
@@ -93,25 +85,62 @@
         c.wait()
 
 
-def pack(tokens, ids, w_in, w_out, dims):
-    ny, _, nm, nx, nc = dims
+def pack(tokens, ids, w_in, dims):
+    ny, _, _, nx, nc = dims
     toks, model = tokens.shape
     width = model // ny
-    rows = w_out.shape[0] // (nx * nc)
     return pl.pallas_call(
         functools.partial(pack_kernel, dims=dims),
-        out_shape=(
-            pltpu.VMEM((ny, toks, 2 * width + LANES), BF16),
-            jax.ShapeDtypeStruct((ny * nm, rows, width), BF16),
-        ),
-        in_specs=[HBM, VMEM, HBM, HBM],
-        out_specs=(VMEM, VMEM),
+        out_shape=pltpu.VMEM((ny, toks, 2 * width + LANES), BF16),
+        in_specs=[HBM, VMEM, HBM],
+        out_specs=VMEM,
         scratch_shapes=[
             pltpu.VMEM((ny, width // (nx * nc), LANES), BF16),
-            pltpu.SemaphoreType.DMA((2 + nm, ny)),
+            pltpu.SemaphoreType.DMA((2, ny)),
         ],
         name="pack",
-    )(tokens, ids, w_in, w_out)
+    )(tokens, ids, w_in)
+
+
+def share_kernel(w_ref, out_ref, rows, sem, *, dims):
+    ny, _, _, _, nc = dims
+    width = out_ref.shape[2]
+    part = lax.axis_index("x") * nc + lax.axis_index("c")
+    top = pl.ds(pl.multiple_of(part * rows.shape[0], 16), rows.shape[0])
+    load = pltpu.make_async_copy(w_ref.at[top, :], rows, sem)
+    load.start()
+    load.wait()
+    for k in range(ny):
+        out_ref[k] = rows[:, k * width : (k + 1) * width]
+
+
+def share(w, dims):
+    ny, _, _, nx, nc = dims
+    rows = w.shape[0] // (nx * nc)
+    return pl.pallas_call(
+        functools.partial(share_kernel, dims=dims),
+        out_shape=jax.ShapeDtypeStruct((ny, rows, w.shape[1] // ny), BF16),
+        in_specs=[HBM],
+        out_specs=VMEM,
+        scratch_shapes=[pltpu.VMEM((rows, w.shape[1]), BF16), pltpu.SemaphoreType.DMA],
+        name="share",
+    )(w)
+
+
+def join_kernel(mine_ref, other_ref, out_ref):
+    for k in range(mine_ref.shape[0]):
+        out_ref[k, 0] = mine_ref[k]
+        out_ref[k, 1] = other_ref[k]
+
+
+def join(mine, other):
+    return pl.pallas_call(
+        join_kernel,
+        out_shape=jax.ShapeDtypeStruct((mine.shape[0], 2) + mine.shape[1:], BF16),
+        in_specs=[VMEM, VMEM],
+        out_specs=VMEM,
+        name="join",
+    )(mine, other)
 
 
 def tile_kernel(mine_ref, other_ref, wide_ref, *, dims):
@@ -271,13 +300,15 @@
     )(x)
 
 
-def second_kernel(h_ref, place_ref, w_ref, out_ref, tall, spread, sems, *, toks):
+def second_kernel(h_ref, place_ref, w_ref, out_ref, tall, spread, sems, *, dims, toks):
     chunks, blocks, _, per = place_ref.shape
     width = w_ref.shape[3]
     devices = CHUNK // toks
-    copies = [
-        pltpu.make_async_copy(w_ref.at[:, b], tall.at[b], sems.at[b]) for b in range(blocks)
-    ]
+    nm, zm = dims[2], lax.axis_index("zm")
+    copies = []
+    for b in range(blocks):
+        source = b // nm * nm + (b + nm - zm) % nm
+        copies.append(pltpu.make_async_copy(w_ref.at[:, source], tall.at[b], sems.at[b]))
     for c in copies:
         c.start()
     for m in range(chunks):
@@ -295,11 +326,11 @@
         out_ref[m * devices : (m + 1) * devices] = out.astype(BF16).reshape(devices, toks, width)
 
 
-def second_product(h, places, w, toks):
+def second_product(h, places, w, dims, toks):
     chunks, blocks = places.shape[:2]
     nt, _, rows, width = w.shape
     return pl.pallas_call(
-        functools.partial(second_kernel, toks=toks),
+        functools.partial(second_kernel, dims=dims, toks=toks),
         out_shape=pltpu.VMEM((chunks * CHUNK // toks, toks, width), BF16),
         in_specs=[VMEM, VMEM, HBM],
         out_specs=VMEM,
@@ -338,18 +369,20 @@
 
 def body(tokens, block_ids, w_in, bias_in, w_out):
     dims = sizes()
-    ny, _, _, nx, nc = dims
+    ny, _, nm, nx, nc = dims
     toks = tokens.shape[0]
     width = tokens.shape[1] // ny
 
-    payload, w2 = pack(tokens, block_ids.T, w_in, w_out, dims)
+    payload = pack(tokens, block_ids.T, w_in, dims)
     got = exchange(payload, "y")
+    w2 = share(w_out, dims)
+    pair = lax.ppermute(w2, "zm", [(i, nm - 1 - i) for i in range(nm)])
+    w2 = join(near(w2), near(pair))
     x = lax.all_gather(
         got[:, :, : width + LANES].reshape(ny * toks, width + LANES), ("zn", "zm"), axis=0, tiled=True
     )
     w1 = got[:, :, width + LANES :]
-    w2, w1 = lax.optimization_barrier((w2, w1))
-    w2 = exchange(w2, ("y", "zm"))
+    w2 = exchange(w2, "y")
     mine = [w1]
     for s in range(1, nx):
         mine.append(lax.ppermute(w1, "x", [(i, (i + s) % nx) for i in range(nx)]))
@@ -357,13 +390,14 @@
     other = lax.ppermute(mine, "c", [(i, nc - 1 - i) for i in range(nc)])
     wide = tile(near(mine), near(other), dims)
     x, wide, w2 = lax.optimization_barrier((x, wide, w2))
-    w2 = lax.all_gather(w2[None], ("x", "c"), axis=0, tiled=True)
+    w2 = w2.reshape((1, ny * nm) + w2.shape[2:])
+    w2 = lax.all_gather(w2, ("x", "c"), axis=0, tiled=True)
 
     h = exchange(first_product(x, near(wide), dims, toks), "y")
     h = activate(near(h), bias_in[None, :], dims)
     h = exchange(h, ("y", "zm"))
     places = place(x, dims, toks)
-    y = exchange(second_product(near(h), near(places), w2, toks), ("zn", "y"))
+    y = exchange(second_product(near(h), near(places), w2, dims, toks), ("zn", "y"))
     return combine(near(y), ny)
 
 

time: 197 us -> 192 us (0.975)
  waiting for transfers between devices: 42 us -> 35.4 us
  starting transfers between devices: 24.2 us -> 29.4 us
  blocking collectives: 93.9 us -> 89 us
    ppermute x0 -> x1, waiting for transfers between devices: none -> 10.4 us  [body(): pair = lax.ppermute(w2, 'zm', [(i, nm - 1 - i) for i in range(nm)])]
    ppermute x3, waiting for transfers between devices: 10.3 us -> 0.01 us  [body(): mine.append(lax.ppermute(w1, 'x', [(i, (i + s) % nx) for i in range(nx)]))]
    all_to_all x3, blocking collectives: 93.9 us -> 89 us  [exchange(): return lax.all_to_all(value, axes, split_axis=0, concat_axis=0, tiled=True)]
    ppermute x0 -> x1, starting transfers between devices: none -> 4.28 us  [body(): pair = lax.ppermute(w2, 'zm', [(i, nm - 1 - i) for i in range(nm)])]
    all_gather x1, waiting for transfers between devices: 4 us -> 0.01 us  [body(): lax.all_gather(got[:, :, :width + LANES].reshape(ny * toks, width + LANES...]
    all_to_all x2, waiting for transfers between devices: 27.6 us -> 24.9 us  [exchange(): return lax.all_to_all(value, axes, split_axis=0, concat_axis=0, tiled=True)]
    pallas_call x2 -> x4, Pallas kernels: 8.91 us -> 10.4 us  [the longest x1 5.9 us: second_product(): pl.pallas_call(functools.partial(second_kernel, dims=dims, toks=toks), ou...]
  transfers between devices with their start and end apart: 8 -> 9, of which waited for: 6 -> 3; matrix products, arithmetic and copies ran while one was open for 0% -> 0% of each run, Pallas kernels for 5% -> 6%
where the time goes in v6:
time: 192 us
  blocking collectives  89 us (46%)
  waiting for transfers between devices  35.4 us (18%)
  starting transfers between devices  29.4 us (15%)
  Pallas kernels  21 us (11%)
  between operations  13.5 us (7%)
  local copies, waits for them, and re-layouts  3.15 us (2%)
    all_to_all x3, blocking collectives, exchange(): return lax.all_to_all(value, axes, split_axis=0, concat_axis=0, tiled=True)  89 us
    all_to_all x2, waiting for transfers between devices, exchange(): return lax.all_to_all(value, axes, split_axis=0, concat_axis=0, tiled=True)  24.9 us
    ppermute x3, starting transfers between devices, body(): mine.append(lax.ppermute(w1, 'x', [(i, (i + s) % nx) for i in range(nx)]))  12 us
    all_to_all x2, starting transfers between devices, exchange(): return lax.all_to_all(value, axes, split_axis=0, concat_axis=0, tiled=True)  11.3 us
    ppermute x1, waiting for transfers between devices, body(): pair = lax.ppermute(w2, 'zm', [(i, nm - 1 - i) for i in range(nm)])  10.4 us
    pallas_call x1, Pallas kernels, second_product(): pl.pallas_call(functools.partial(second_kernel, dims=dims, toks=toks), ou...  5.9 us
    pallas_call x1, Pallas kernels, first_product(): pl.pallas_call(functools.partial(first_kernel, dims=dims, toks=toks), out...  5.45 us
    ppermute x1, starting transfers between devices, body(): pair = lax.ppermute(w2, 'zm', [(i, nm - 1 - i) for i in range(nm)])  4.28 us
  transfers between devices with their start and end apart: 9, of which 3 were waited for; matrix products, arithmetic and copies ran while one was open for 0% of the time, Pallas kernels for 6%

profile of v6, /device:TPU:8, one launch (start us, length us, event | category | flops | bytes accessed | tf_op | source)
XLA Modules:
  0.0 191.7 jit_solution(8723745051522861152)
XLA Ops:
  6.5 1.9 pack.1
  8.4 25.5 %all_to_all.25 = bf16[8,16,2432]{2,1,0:T(8,128)(2,1)S(1)} all-to-all(bf16[8,16,2432]{2,1,0:T(8,128)(2,1)S(1)} %pack.1), channel_id=1, replica_groups=mesh['y'=8,'zn'=4,'zm'=2,'x'=4,'c'=2] {'y'}, dimensions={0} | all-to-all | bytes 1245184 | tf_op jit(solution)/shard_map/all_to_all | solution.py:367
  33.9 0.8 slice.8
  34.7 0.0 all-gather.3.cloned.1.call-update
  34.8 4.9 %collective-permute-start.1 = (bf16[8,16,1152]{2,1,0:T(8,128)(2,1)S(1)}, bf16[8,16,1152]{2,1,0:T(8,128)(2,1)S(1)}, u32[]{:S(2)}, u32[]{:S(2)}) collective-permute-start(bf16[8,16,1152]{2,1,0:T(8,128)(2,1)S(1)} %get-tuple-element.12), channel_id=1, source_target_pairs={{0,4},{2,6},{4,0},{6,2},{1,5},{3,7},{5,1},{7,3},{8,12},{10,14},{12... | collective-permute-start | bytes 884744 | tf_op jit(solution)/shard_map/ppermute | solution.py:388
  39.7 2.5 %collective-permute-start = (bf16[8,16,1152]{2,1,0:T(8,128)(2,1)S(1)}, bf16[8,16,1152]{2,1,0:T(8,128)(2,1)S(1)}, u32[]{:S(2)}, u32[]{:S(2)}) collective-permute-start(bf16[8,16,1152]{2,1,0:T(8,128)(2,1)S(1)} %get-tuple-element.12), channel_id=1, source_target_pairs={{0,2},{2,4},{4,6},{6,0},{1,3},{3,5},{5,7},{7,1},{8,10},{10,12},{12... | collective-permute-start | bytes 884744 | tf_op jit(solution)/shard_map/ppermute | solution.py:388
  42.2 4.6 %collective-permute-start.2 = (bf16[8,16,1152]{2,1,0:T(8,128)(2,1)S(1)}, bf16[8,16,1152]{2,1,0:T(8,128)(2,1)S(1)}, u32[]{:S(2)}, u32[]{:S(2)}) collective-permute-start(bf16[8,16,1152]{2,1,0:T(8,128)(2,1)S(1)} %get-tuple-element.12), channel_id=1, source_target_pairs={{0,6},{2,0},{4,2},{6,4},{1,7},{3,1},{5,3},{7,5},{8,14},{10,8},{12,... | collective-permute-start | bytes 884744 | tf_op jit(solution)/shard_map/ppermute | solution.py:388
  46.8 1.7 share.1.mine_ref
  48.5 4.3 %collective-permute-start.4 = (bf16[8,16,1152]{2,1,0:T(8,128)(2,1)}, bf16[8,16,1152]{2,1,0:T(8,128)(2,1)S(1)}, u32[]{:S(2)}, u32[]{:S(2)}) collective-permute-start(bf16[8,16,1152]{2,1,0:T(8,128)(2,1)} %share.1.mine_ref), channel_id=1, source_target_pairs={{0,8},{8,0},{1,9},{9,1},{2,10},{10,2},{3,11},{11,3},{4,12},{12,4},... | collective-permute-start | bytes 884744 | tf_op jit(solution)/shard_map/ppermute | solution.py:379
  52.8 0.0 collective-permute-done.1
  52.8 0.0 collective-permute-done
  52.8 0.0 collective-permute-done.2
  52.8 0.0 copy-start.2
  52.8 0.2 pad_maximum_fusion.mine_ref
  53.0 1.9 %collective-permute-start.3 = (bf16[4,8,16,1152]{3,2,1,0:T(8,128)(2,1)S(1)}, bf16[4,8,16,1152]{3,2,1,0:T(8,128)(2,1)S(1)}, u32[]{:S(2)}, u32[]{:S(2)}) collective-permute-start(bf16[4,8,16,1152]{3,2,1,0:T(8,128)(2,1)S(1)} %pad_maximum_fusion.mine_ref), channel_id=1, source_target_pairs={{0,1},{1,0},{2,3},{3,2},{4,5},{5,4},{6,7},{7,6},{8,9},{9,8},{10,11... | collective-permute-start | bytes 3538952 | tf_op jit(solution)/shard_map/ppermute | solution.py:390
  54.9 10.4 %collective-permute-done.4.other_ref = bf16[8,16,1152]{2,1,0:T(8,128)(2,1)S(1)} collective-permute-done((bf16[8,16,1152]{2,1,0:T(8,128)(2,1)}, bf16[8,16,1152]{2,1,0:T(8,128)(2,1)S(1)}, u32[]{:S(2)}, u32[]{:S(2)}) %collective-permute-start.4) | collective-permute-done | bytes 294944 | tf_op jit(solution)/shard_map/ppermute | solution.py:379
  65.3 0.9 join.1
  66.2 6.4 %all-to-all-start.1 = ((bf16[8,2,16,1152]{3,2,1,0:T(8,128)(2,1)}), bf16[8,2,16,1152]{3,2,1,0:T(8,128)(2,1)}, u32[]{:S(2)}, u32[]{:S(2)}) async-start(bf16[8,2,16,1152]{3,2,1,0:T(8,128)(2,1)} %join.1), calls=%async_computation.1 | async-start | bytes 1179648 | tf_op jit(solution)/shard_map/all_to_all | solution.py:367
  72.6 1.0 copy-done
  73.6 1.3 copy-done.1
  74.9 0.5 tile.1.wide_ref
  75.4 12.4 %all-to-all-done.1 = bf16[8,2,16,1152]{3,2,1,0:T(8,128)(2,1)} async-done(((bf16[8,2,16,1152]{3,2,1,0:T(8,128)(2,1)}), bf16[8,2,16,1152]{3,2,1,0:T(8,128)(2,1)}, u32[]{:S(2)}, u32[]{:S(2)}) %all-to-all-start.1) | async-done | bytes 589856 | tf_op jit(solution)/shard_map/all_to_all | solution.py:367
  87.8 0.0 all-gather.5.cloned.1.call-update
  87.9 5.4 %first_product.1 = bf16[8,320,128]{2,1,0:T(8,128)(2,1)S(1)} custom-call(bf16[1024,1280]{1,0:T(8,128)(2,1)} %all-gather.3.cloned.1.call-done.x_ref, bf16[1152,1024]{1,0:T(8,128)(2,1)S(1)} %tile.1.wide_ref), custom_call_target="tpu_custom_call" | custom-call | tf_op jit(solution)/shard_map/first_product/pallas_call | solution.py:213
  93.3 22.0 %all_to_all.26.part_ref = bf16[8,320,128]{2,1,0:T(8,128)(2,1)S(1)} all-to-all(bf16[8,320,128]{2,1,0:T(8,128)(2,1)S(1)} %first_product.1), channel_id=1, replica_groups=mesh['y'=8,'zn'=4,'zm'=2,'x'=4,'c'=2] {'y'}, dimensions={0} | all-to-all | bytes 1310720 | tf_op jit(solution)/shard_map/all_to_all | solution.py:367
  115.3 1.6 activate.1
  116.9 4.8 %all-to-all-start.3 = ((bf16[16,160,128]{2,1,0:T(8,128)(2,1)}), bf16[16,160,128]{2,1,0:T(8,128)(2,1)S(1)}, u32[]{:S(2)}, u32[]{:S(2)}) async-start(bf16[16,160,128]{2,1,0:T(8,128)(2,1)} %activate.1), calls=%async_computation.3 | async-start | bytes 1310720 | tf_op jit(solution)/shard_map/all_to_all | solution.py:367
  121.7 2.2 %place.1.place_ref = bf16[2,16,256,80]{3,2,1,0:T(8,128)(2,1)S(1)} custom-call(bf16[1024,1280]{1,0:T(8,128)(2,1)} %all-gather.3.cloned.1.call-done.x_ref), custom_call_target="tpu_custom_call" | custom-call | tf_op jit(solution)/shard_map/place/pallas_call | solution.py:290
  124.0 12.5 %all-to-all-done.3.h_ref = bf16[16,160,128]{2,1,0:T(8,128)(2,1)S(1)} async-done(((bf16[16,160,128]{2,1,0:T(8,128)(2,1)}), bf16[16,160,128]{2,1,0:T(8,128)(2,1)S(1)}, u32[]{:S(2)}, u32[]{:S(2)}) %all-to-all-start.3) | async-done | bytes 655392 | tf_op jit(solution)/shard_map/all_to_all | solution.py:367
  136.5 5.9 %second_product.1 = bf16[32,16,1152]{2,1,0:T(8,128)(2,1)S(1)} custom-call(bf16[16,160,128]{2,1,0:T(8,128)(2,1)S(1)} %all-to-all-done.3.h_ref, bf16[2,16,256,80]{3,2,1,0:T(8,128)(2,1)S(1)} %place.1.place_ref, bf16[8,16,16,1152]{3,2,1,0:T(8,128)(2,1)} %all-gather.5.cloned.1.call-done.w_ref), custom_call_target="tpu_custom_call" | custom-call | tf_op jit(solution)/shard_map/second_product/pallas_call | solution.py:332
  142.4 41.6 %all_to_all.27.y_ref = bf16[32,16,1152]{2,1,0:T(8,128)(2,1)S(1)} all-to-all(bf16[32,16,1152]{2,1,0:T(8,128)(2,1)S(1)} %second_product.1), channel_id=1, replica_groups=mesh['y'=8,'zn'=4,'zm'=2,'x'=4,'c'=2] {'zn','y'}, dimensions={0} | all-to-all | bytes 2359296 | tf_op jit(solution)/shard_map/all_to_all | solution.py:367
  184.0 0.9 combine.1
  (9 shorter events, 0.1 us)
Async XLA Ops:
  6.5 81.3 %all-gather.3.cloned.1.call-start = ((), (), s32[]{:S(2)}) async-start(), calls=%async_computation.5 | async-start | bytes 2949120 | tf_op jit(solution)/shard_map/all_gather | solution.py:381
  34.8 18.0 %collective-permute-start.1 = (bf16[8,16,1152]{2,1,0:T(8,128)(2,1)S(1)}, bf16[8,16,1152]{2,1,0:T(8,128)(2,1)S(1)}, u32[]{:S(2)}, u32[]{:S(2)}) collective-permute-start(bf16[8,16,1152]{2,1,0:T(8,128)(2,1)S(1)} %get-tuple-element.12), channel_id=1, source_target_pairs={{0,4},{2,6},{4,0},{6,2},{1,5},{3,7},{5,1},{7,3},{8,12},{10,14},{12... | collective-permute-start | bytes 884744 | tf_op jit(solution)/shard_map/ppermute | solution.py:388
  39.7 13.1 %collective-permute-start = (bf16[8,16,1152]{2,1,0:T(8,128)(2,1)S(1)}, bf16[8,16,1152]{2,1,0:T(8,128)(2,1)S(1)}, u32[]{:S(2)}, u32[]{:S(2)}) collective-permute-start(bf16[8,16,1152]{2,1,0:T(8,128)(2,1)S(1)} %get-tuple-element.12), channel_id=1, source_target_pairs={{0,2},{2,4},{4,6},{6,0},{1,3},{3,5},{5,7},{7,1},{8,10},{10,12},{12... | collective-permute-start | bytes 884744 | tf_op jit(solution)/shard_map/ppermute | solution.py:388
  42.2 10.6 %collective-permute-start.2 = (bf16[8,16,1152]{2,1,0:T(8,128)(2,1)S(1)}, bf16[8,16,1152]{2,1,0:T(8,128)(2,1)S(1)}, u32[]{:S(2)}, u32[]{:S(2)}) collective-permute-start(bf16[8,16,1152]{2,1,0:T(8,128)(2,1)S(1)} %get-tuple-element.12), channel_id=1, source_target_pairs={{0,6},{2,0},{4,2},{6,4},{1,7},{3,1},{5,3},{7,5},{8,14},{10,8},{12,... | collective-permute-start | bytes 884744 | tf_op jit(solution)/shard_map/ppermute | solution.py:388
  48.5 16.8 %collective-permute-start.4 = (bf16[8,16,1152]{2,1,0:T(8,128)(2,1)}, bf16[8,16,1152]{2,1,0:T(8,128)(2,1)S(1)}, u32[]{:S(2)}, u32[]{:S(2)}) collective-permute-start(bf16[8,16,1152]{2,1,0:T(8,128)(2,1)} %share.1.mine_ref), channel_id=1, source_target_pairs={{0,8},{8,0},{1,9},{9,1},{2,10},{10,2},{3,11},{11,3},{4,12},{12,4},... | collective-permute-start | bytes 884744 | tf_op jit(solution)/shard_map/ppermute | solution.py:379
  52.8 12.5 %copy-start.2 = (bf16[8,16,1152]{2,1,0:T(8,128)(2,1)S(1)}, bf16[8,16,1152]{2,1,0:T(8,128)(2,1)}, u32[]{:S(2)}) copy-start(bf16[8,16,1152]{2,1,0:T(8,128)(2,1)} %share.1.mine_ref) | copy-start | bytes 884740
  53.0 19.6 %collective-permute-start.3 = (bf16[4,8,16,1152]{3,2,1,0:T(8,128)(2,1)S(1)}, bf16[4,8,16,1152]{3,2,1,0:T(8,128)(2,1)S(1)}, u32[]{:S(2)}, u32[]{:S(2)}) collective-permute-start(bf16[4,8,16,1152]{3,2,1,0:T(8,128)(2,1)S(1)} %pad_maximum_fusion.mine_ref), channel_id=1, source_target_pairs={{0,1},{1,0},{2,3},{3,2},{4,5},{5,4},{6,7},{7,6},{8,9},{9,8},{10,11... | collective-permute-start | bytes 3538952 | tf_op jit(solution)/shard_map/ppermute | solution.py:390
  66.2 21.7 %all-to-all-start.1 = ((bf16[8,2,16,1152]{3,2,1,0:T(8,128)(2,1)}), bf16[8,2,16,1152]{3,2,1,0:T(8,128)(2,1)}, u32[]{:S(2)}, u32[]{:S(2)}) async-start(bf16[8,2,16,1152]{3,2,1,0:T(8,128)(2,1)} %join.1), calls=%async_computation.1 | async-start | bytes 1179648 | tf_op jit(solution)/shard_map/all_to_all | solution.py:367
  72.6 63.9 %all-gather.5.cloned.1.call-start = ((), (), s32[]{:S(2)}) async-start(), calls=%async_computation.6 | async-start | bytes 5308416 | tf_op jit(solution)/shard_map/all_gather | solution.py:394
  72.6 1.1 copy-start
  73.6 1.3 copy-start.1
  116.9 19.6 %all-to-all-start.3 = ((bf16[16,160,128]{2,1,0:T(8,128)(2,1)}), bf16[16,160,128]{2,1,0:T(8,128)(2,1)S(1)}, u32[]{:S(2)}, u32[]{:S(2)}) async-start(bf16[16,160,128]{2,1,0:T(8,128)(2,1)} %activate.1), calls=%async_computation.3 | async-start | bytes 1310720 | tf_op jit(solution)/shard_map/all_to_all | solution.py:367
Sparse Core Ops, SparseCore 0:
  34.8 51.2 all-gather.2
  88.3 36.8 all-gather.4

commit v7 on v6

--- a/solution.py
+++ b/solution.py
@@ -32,7 +32,7 @@
     return pltpu.with_memory_space_constraint(value, pltpu.VMEM)
 
 
-def pack_kernel(tokens_ref, ids_ref, w_in_ref, out_ref, in_rows, sems, *, dims):
+def pack_kernel(tokens_ref, ids_ref, w_in_ref, out_ref, id_rows, in_rows, id_sem, sems, *, dims):
     ny, nn, nm, nx, nc = dims
     nz, nt = nn * nm, nx * nc
     share = lax.axis_index("x") * nc + lax.axis_index("c")
@@ -52,12 +52,15 @@
                 tokens_ref.at[:, cut], out_ref.at[k, :, pl.ds(0, width)], sems.at[1, k]
             )
         )
+    names = pltpu.make_async_copy(ids_ref, id_rows, id_sem)
+    names.start()
     for c in copies:
         c.start()
+    names.wait()
     same = lax.broadcasted_iota(jnp.int32, (ids_ref.shape[0],) * 2, 0)
     same = same == lax.broadcasted_iota(jnp.int32, same.shape, 1)
     ids = lax.dot_general(
-        ids_ref[...].astype(F32).astype(BF16),
+        id_rows[...].astype(F32).astype(BF16),
         jnp.where(same, 1.0, 0.0).astype(BF16),
         (((0,), (0,)), ((), ())),
         preferred_element_type=F32,
@@ -92,10 +95,12 @@
     return pl.pallas_call(
         functools.partial(pack_kernel, dims=dims),
         out_shape=pltpu.VMEM((ny, toks, 2 * width + LANES), BF16),
-        in_specs=[HBM, VMEM, HBM],
+        in_specs=[HBM, HBM, HBM],
         out_specs=VMEM,
         scratch_shapes=[
+            pltpu.VMEM(ids.shape, ids.dtype),
             pltpu.VMEM((ny, width // (nx * nc), LANES), BF16),
+            pltpu.SemaphoreType.DMA,
             pltpu.SemaphoreType.DMA((2, ny)),
         ],
         name="pack",
@@ -317,9 +322,9 @@
                 place_ref[m, b], h_ref[b, m * per : (m + 1) * per, :], preferred_element_type=F32
             )
             spread[m, :, b * LANES : (b + 1) * LANES] = full.astype(BF16)
-    for c in copies:
-        c.wait()
-    for m in range(chunks):
+        if m == 0:
+            for c in copies:
+                c.wait()
         out = jnp.dot(
             spread[m], tall[...].reshape(blocks * LANES, width), preferred_element_type=F32
         )
@@ -394,7 +399,7 @@
     w2 = lax.all_gather(w2, ("x", "c"), axis=0, tiled=True)
 
     h = exchange(first_product(x, near(wide), dims, toks), "y")
-    h = activate(near(h), bias_in[None, :], dims)
+    h = activate(near(h), near(bias_in[None, :]), dims)
     h = exchange(h, ("y", "zm"))
     places = place(x, dims, toks)
     y = exchange(second_product(near(h), near(places), w2, dims, toks), ("zn", "y"))

time: 192 us -> 191 us (level)
  no operation moved by 1% of the time
where the time goes in v7:
time: 191 us; the launch traced here: 190 us
  blocking collectives  89 us (47%)
  waiting for transfers between devices  35.3 us (18%)
  starting transfers between devices  29.4 us (15%)
  Pallas kernels  19.7 us (10%)
  between operations  13.6 us (7%)
  local copies, waits for them, and re-layouts  3.13 us (2%)
    all_to_all x3, blocking collectives, exchange(): return lax.all_to_all(value, axes, split_axis=0, concat_axis=0, tiled=True)  89 us
    all_to_all x2, waiting for transfers between devices, exchange(): return lax.all_to_all(value, axes, split_axis=0, concat_axis=0, tiled=True)  24.9 us
    ppermute x3, starting transfers between devices, body(): mine.append(lax.ppermute(w1, 'x', [(i, (i + s) % nx) for i in range(nx)]))  12 us
    all_to_all x2, starting transfers between devices, exchange(): return lax.all_to_all(value, axes, split_axis=0, concat_axis=0, tiled=True)  11.2 us
    ppermute x1, waiting for transfers between devices, body(): pair = lax.ppermute(w2, 'zm', [(i, nm - 1 - i) for i in range(nm)])  10.4 us
    pallas_call x1, Pallas kernels, second_product(): pl.pallas_call(functools.partial(second_kernel, dims=dims, toks=toks), ou...  5.62 us
    pallas_call x1, Pallas kernels, first_product(): pl.pallas_call(functools.partial(first_kernel, dims=dims, toks=toks), out...  5.45 us
    ppermute x1, starting transfers between devices, body(): pair = lax.ppermute(w2, 'zm', [(i, nm - 1 - i) for i in range(nm)])  4.28 us
  transfers between devices with their start and end apart: 9, of which 3 were waited for; matrix products, arithmetic and copies ran while one was open for 0% of the time, Pallas kernels for 6%

profile of v7, /device:TPU:8, one launch (start us, length us, event | category | flops | bytes accessed | tf_op | source)
XLA Modules:
  0.0 190.4 jit_solution(4622734869147006976)
XLA Ops:
  6.5 1.6 pack.1
  8.1 25.5 %all_to_all.25 = bf16[8,16,2432]{2,1,0:T(8,128)(2,1)S(1)} all-to-all(bf16[8,16,2432]{2,1,0:T(8,128)(2,1)S(1)} %pack.1), channel_id=1, replica_groups=mesh['y'=8,'zn'=4,'zm'=2,'x'=4,'c'=2] {'y'}, dimensions={0} | all-to-all | bytes 1245184 | tf_op jit(solution)/shard_map/all_to_all | solution.py:372
  33.6 0.8 slice.8
  34.3 0.0 all-gather.3.cloned.1.call-update
  34.4 4.9 %collective-permute-start.1 = (bf16[8,16,1152]{2,1,0:T(8,128)(2,1)S(1)}, bf16[8,16,1152]{2,1,0:T(8,128)(2,1)S(1)}, u32[]{:S(2)}, u32[]{:S(2)}) collective-permute-start(bf16[8,16,1152]{2,1,0:T(8,128)(2,1)S(1)} %get-tuple-element.12), channel_id=1, source_target_pairs={{0,4},{2,6},{4,0},{6,2},{1,5},{3,7},{5,1},{7,3},{8,12},{10,14},{12... | collective-permute-start | bytes 884744 | tf_op jit(solution)/shard_map/ppermute | solution.py:393
  39.4 2.5 %collective-permute-start = (bf16[8,16,1152]{2,1,0:T(8,128)(2,1)S(1)}, bf16[8,16,1152]{2,1,0:T(8,128)(2,1)S(1)}, u32[]{:S(2)}, u32[]{:S(2)}) collective-permute-start(bf16[8,16,1152]{2,1,0:T(8,128)(2,1)S(1)} %get-tuple-element.12), channel_id=1, source_target_pairs={{0,2},{2,4},{4,6},{6,0},{1,3},{3,5},{5,7},{7,1},{8,10},{10,12},{12... | collective-permute-start | bytes 884744 | tf_op jit(solution)/shard_map/ppermute | solution.py:393
  41.9 4.6 %collective-permute-start.2 = (bf16[8,16,1152]{2,1,0:T(8,128)(2,1)S(1)}, bf16[8,16,1152]{2,1,0:T(8,128)(2,1)S(1)}, u32[]{:S(2)}, u32[]{:S(2)}) collective-permute-start(bf16[8,16,1152]{2,1,0:T(8,128)(2,1)S(1)} %get-tuple-element.12), channel_id=1, source_target_pairs={{0,6},{2,0},{4,2},{6,4},{1,7},{3,1},{5,3},{7,5},{8,14},{10,8},{12,... | collective-permute-start | bytes 884744 | tf_op jit(solution)/shard_map/ppermute | solution.py:393
  46.4 1.7 share.1.mine_ref
  48.2 4.3 %collective-permute-start.4 = (bf16[8,16,1152]{2,1,0:T(8,128)(2,1)}, bf16[8,16,1152]{2,1,0:T(8,128)(2,1)S(1)}, u32[]{:S(2)}, u32[]{:S(2)}) collective-permute-start(bf16[8,16,1152]{2,1,0:T(8,128)(2,1)} %share.1.mine_ref), channel_id=1, source_target_pairs={{0,8},{8,0},{1,9},{9,1},{2,10},{10,2},{3,11},{11,3},{4,12},{12,4},... | collective-permute-start | bytes 884744 | tf_op jit(solution)/shard_map/ppermute | solution.py:384
  52.4 0.0 collective-permute-done.1
  52.5 0.0 collective-permute-done.2
  52.5 0.0 copy-start.2
  52.5 0.2 pad_maximum_fusion.mine_ref
  52.7 1.9 %collective-permute-start.3 = (bf16[4,8,16,1152]{3,2,1,0:T(8,128)(2,1)S(1)}, bf16[4,8,16,1152]{3,2,1,0:T(8,128)(2,1)S(1)}, u32[]{:S(2)}, u32[]{:S(2)}) collective-permute-start(bf16[4,8,16,1152]{3,2,1,0:T(8,128)(2,1)S(1)} %pad_maximum_fusion.mine_ref), channel_id=1, source_target_pairs={{0,1},{1,0},{2,3},{3,2},{4,5},{5,4},{6,7},{7,6},{8,9},{9,8},{10,11... | collective-permute-start | bytes 3538952 | tf_op jit(solution)/shard_map/ppermute | solution.py:395
  54.6 10.4 %collective-permute-done.4.other_ref = bf16[8,16,1152]{2,1,0:T(8,128)(2,1)S(1)} collective-permute-done((bf16[8,16,1152]{2,1,0:T(8,128)(2,1)}, bf16[8,16,1152]{2,1,0:T(8,128)(2,1)S(1)}, u32[]{:S(2)}, u32[]{:S(2)}) %collective-permute-start.4) | collective-permute-done | bytes 294944 | tf_op jit(solution)/shard_map/ppermute | solution.py:384
  65.0 0.9 join.1
  65.8 6.4 %all-to-all-start.1 = ((bf16[8,2,16,1152]{3,2,1,0:T(8,128)(2,1)}), bf16[8,2,16,1152]{3,2,1,0:T(8,128)(2,1)}, u32[]{:S(2)}, u32[]{:S(2)}) async-start(bf16[8,2,16,1152]{3,2,1,0:T(8,128)(2,1)} %join.1), calls=%async_computation.1 | async-start | bytes 1179648 | tf_op jit(solution)/shard_map/all_to_all | solution.py:372
  72.2 1.0 copy-done
  73.3 1.3 copy-done.1
  74.6 0.5 tile.1.wide_ref
  75.1 12.4 %all-to-all-done.1 = bf16[8,2,16,1152]{3,2,1,0:T(8,128)(2,1)} async-done(((bf16[8,2,16,1152]{3,2,1,0:T(8,128)(2,1)}), bf16[8,2,16,1152]{3,2,1,0:T(8,128)(2,1)}, u32[]{:S(2)}, u32[]{:S(2)}) %all-to-all-start.1) | async-done | bytes 589856 | tf_op jit(solution)/shard_map/all_to_all | solution.py:372
  87.5 0.0 all-gather.5.cloned.1.call-update
  87.5 5.5 %first_product.1 = bf16[8,320,128]{2,1,0:T(8,128)(2,1)S(1)} custom-call(bf16[1024,1280]{1,0:T(8,128)(2,1)} %all-gather.3.cloned.1.call-done.x_ref, bf16[1152,1024]{1,0:T(8,128)(2,1)S(1)} %tile.1.wide_ref), custom_call_target="tpu_custom_call" | custom-call | tf_op jit(solution)/shard_map/first_product/pallas_call | solution.py:218
  93.0 0.0 copy-start.3
  93.0 22.0 %all_to_all.26.part_ref = bf16[8,320,128]{2,1,0:T(8,128)(2,1)S(1)} all-to-all(bf16[8,320,128]{2,1,0:T(8,128)(2,1)S(1)} %first_product.1), channel_id=1, replica_groups=mesh['y'=8,'zn'=4,'zm'=2,'x'=4,'c'=2] {'y'}, dimensions={0} | all-to-all | bytes 1310720 | tf_op jit(solution)/shard_map/all_to_all | solution.py:372
  115.0 0.9 activate.1
  115.9 4.8 %all-to-all-start.3 = ((bf16[16,160,128]{2,1,0:T(8,128)(2,1)}), bf16[16,160,128]{2,1,0:T(8,128)(2,1)S(1)}, u32[]{:S(2)}, u32[]{:S(2)}) async-start(bf16[16,160,128]{2,1,0:T(8,128)(2,1)} %activate.1), calls=%async_computation.3 | async-start | bytes 1310720 | tf_op jit(solution)/shard_map/all_to_all | solution.py:372
  120.8 2.2 %place.1.place_ref = bf16[2,16,256,80]{3,2,1,0:T(8,128)(2,1)S(1)} custom-call(bf16[1024,1280]{1,0:T(8,128)(2,1)} %all-gather.3.cloned.1.call-done.x_ref), custom_call_target="tpu_custom_call" | custom-call | tf_op jit(solution)/shard_map/place/pallas_call | solution.py:295
  123.0 12.5 %all-to-all-done.3.h_ref = bf16[16,160,128]{2,1,0:T(8,128)(2,1)S(1)} async-done(((bf16[16,160,128]{2,1,0:T(8,128)(2,1)}), bf16[16,160,128]{2,1,0:T(8,128)(2,1)S(1)}, u32[]{:S(2)}, u32[]{:S(2)}) %all-to-all-start.3) | async-done | bytes 655392 | tf_op jit(solution)/shard_map/all_to_all | solution.py:372
  135.5 5.6 %second_product.1 = bf16[32,16,1152]{2,1,0:T(8,128)(2,1)S(1)} custom-call(bf16[16,160,128]{2,1,0:T(8,128)(2,1)S(1)} %all-to-all-done.3.h_ref, bf16[2,16,256,80]{3,2,1,0:T(8,128)(2,1)S(1)} %place.1.place_ref, bf16[8,16,16,1152]{3,2,1,0:T(8,128)(2,1)} %all-gather.5.cloned.1.call-done.w_ref), custom_call_target="tpu_custom_call" | custom-call | tf_op jit(solution)/shard_map/second_product/pallas_call | solution.py:337
  141.1 41.5 %all_to_all.27.y_ref = bf16[32,16,1152]{2,1,0:T(8,128)(2,1)S(1)} all-to-all(bf16[32,16,1152]{2,1,0:T(8,128)(2,1)S(1)} %second_product.1), channel_id=1, replica_groups=mesh['y'=8,'zn'=4,'zm'=2,'x'=4,'c'=2] {'zn','y'}, dimensions={0} | all-to-all | bytes 2359296 | tf_op jit(solution)/shard_map/all_to_all | solution.py:372
  182.7 0.9 combine.1
  (11 shorter events, 0.1 us)
Async XLA Ops:
  6.5 81.0 %all-gather.3.cloned.1.call-start = ((), (), s32[]{:S(2)}) async-start(), calls=%async_computation.5 | async-start | bytes 2949120 | tf_op jit(solution)/shard_map/all_gather | solution.py:386
  34.4 18.0 %collective-permute-start.1 = (bf16[8,16,1152]{2,1,0:T(8,128)(2,1)S(1)}, bf16[8,16,1152]{2,1,0:T(8,128)(2,1)S(1)}, u32[]{:S(2)}, u32[]{:S(2)}) collective-permute-start(bf16[8,16,1152]{2,1,0:T(8,128)(2,1)S(1)} %get-tuple-element.12), channel_id=1, source_target_pairs={{0,4},{2,6},{4,0},{6,2},{1,5},{3,7},{5,1},{7,3},{8,12},{10,14},{12... | collective-permute-start | bytes 884744 | tf_op jit(solution)/shard_map/ppermute | solution.py:393
  39.4 13.1 %collective-permute-start = (bf16[8,16,1152]{2,1,0:T(8,128)(2,1)S(1)}, bf16[8,16,1152]{2,1,0:T(8,128)(2,1)S(1)}, u32[]{:S(2)}, u32[]{:S(2)}) collective-permute-start(bf16[8,16,1152]{2,1,0:T(8,128)(2,1)S(1)} %get-tuple-element.12), channel_id=1, source_target_pairs={{0,2},{2,4},{4,6},{6,0},{1,3},{3,5},{5,7},{7,1},{8,10},{10,12},{12... | collective-permute-start | bytes 884744 | tf_op jit(solution)/shard_map/ppermute | solution.py:393
  41.9 10.6 %collective-permute-start.2 = (bf16[8,16,1152]{2,1,0:T(8,128)(2,1)S(1)}, bf16[8,16,1152]{2,1,0:T(8,128)(2,1)S(1)}, u32[]{:S(2)}, u32[]{:S(2)}) collective-permute-start(bf16[8,16,1152]{2,1,0:T(8,128)(2,1)S(1)} %get-tuple-element.12), channel_id=1, source_target_pairs={{0,6},{2,0},{4,2},{6,4},{1,7},{3,1},{5,3},{7,5},{8,14},{10,8},{12,... | collective-permute-start | bytes 884744 | tf_op jit(solution)/shard_map/ppermute | solution.py:393
  48.2 16.8 %collective-permute-start.4 = (bf16[8,16,1152]{2,1,0:T(8,128)(2,1)}, bf16[8,16,1152]{2,1,0:T(8,128)(2,1)S(1)}, u32[]{:S(2)}, u32[]{:S(2)}) collective-permute-start(bf16[8,16,1152]{2,1,0:T(8,128)(2,1)} %share.1.mine_ref), channel_id=1, source_target_pairs={{0,8},{8,0},{1,9},{9,1},{2,10},{10,2},{3,11},{11,3},{4,12},{12,4},... | collective-permute-start | bytes 884744 | tf_op jit(solution)/shard_map/ppermute | solution.py:384
  52.5 12.5 %copy-start.2 = (bf16[8,16,1152]{2,1,0:T(8,128)(2,1)S(1)}, bf16[8,16,1152]{2,1,0:T(8,128)(2,1)}, u32[]{:S(2)}) copy-start(bf16[8,16,1152]{2,1,0:T(8,128)(2,1)} %share.1.mine_ref) | copy-start | bytes 884740
  52.7 19.6 %collective-permute-start.3 = (bf16[4,8,16,1152]{3,2,1,0:T(8,128)(2,1)S(1)}, bf16[4,8,16,1152]{3,2,1,0:T(8,128)(2,1)S(1)}, u32[]{:S(2)}, u32[]{:S(2)}) collective-permute-start(bf16[4,8,16,1152]{3,2,1,0:T(8,128)(2,1)S(1)} %pad_maximum_fusion.mine_ref), channel_id=1, source_target_pairs={{0,1},{1,0},{2,3},{3,2},{4,5},{5,4},{6,7},{7,6},{8,9},{9,8},{10,11... | collective-permute-start | bytes 3538952 | tf_op jit(solution)/shard_map/ppermute | solution.py:395
  65.8 21.7 %all-to-all-start.1 = ((bf16[8,2,16,1152]{3,2,1,0:T(8,128)(2,1)}), bf16[8,2,16,1152]{3,2,1,0:T(8,128)(2,1)}, u32[]{:S(2)}, u32[]{:S(2)}) async-start(bf16[8,2,16,1152]{3,2,1,0:T(8,128)(2,1)} %join.1), calls=%async_computation.1 | async-start | bytes 1179648 | tf_op jit(solution)/shard_map/all_to_all | solution.py:372
  72.2 63.3 %all-gather.5.cloned.1.call-start = ((), (), s32[]{:S(2)}) async-start(), calls=%async_computation.6 | async-start | bytes 5308416 | tf_op jit(solution)/shard_map/all_gather | solution.py:399
  72.2 1.1 copy-start
  73.3 1.3 copy-start.1
  93.0 22.0 %copy-start.3 = (f32[128]{0:T(128)S(1)}, f32[128]{0:T(128)}, u32[]{:S(2)}) copy-start(f32[128]{0:T(128)} %param.8) | copy-start | bytes 1540
  115.9 19.6 %all-to-all-start.3 = ((bf16[16,160,128]{2,1,0:T(8,128)(2,1)}), bf16[16,160,128]{2,1,0:T(8,128)(2,1)S(1)}, u32[]{:S(2)}, u32[]{:S(2)}) async-start(bf16[16,160,128]{2,1,0:T(8,128)(2,1)} %activate.1), calls=%async_computation.3 | async-start | bytes 1310720 | tf_op jit(solution)/shard_map/all_to_all | solution.py:372
Sparse Core Ops, SparseCore 0:
  34.5 51.2 all-gather.2
  88.0 36.8 all-gather.4
